TPU v7x, 32 devices: a whole 2x2x4 slice. The times are simulated.
32 devices in a mesh: rows: 2 (over x), cols: 8 (over z, y), frames: 2 (over core).
Axes of the slice: x: 2, y: 2, z: 4, core: 2. Of those that a mesh axis runs over, the one named last changes fastest.
Arguments:
- lidar_map: bfloat16 [8, 96, 192, 256], P('frames', ('rows', 'cols')), parts along dimension 0, may hold values from -6 to 6
- camera_map: bfloat16 [8, 96, 192, 80], P('frames', None, ('rows', 'cols')), parts along dimension 0, may hold values from -6 to 6
- joined_weight: bfloat16 [3, 3, 336, 256], replicated, may hold values from -0.15625 to 0.15625
- joined_bias: float32 [256], replicated, may hold values from -0.5 to 0.5
- block_weight: bfloat16 [3, 3, 256, 128], replicated, may hold values from -0.1875 to 0.1875
- block_bias: float32 [128], replicated, may hold values from -0.5 to 0.5
- down_weight: bfloat16 [3, 3, 128, 256], replicated, may hold values from -0.25 to 0.25
- down_bias: float32 [256], replicated, may hold values from -0.5 to 0.5
- proj_weight: bfloat16 [256, 128], replicated, may hold values from -0.5 to 0.5
- proj_bias: float32 [128], replicated, may hold values from -0.5 to 0.5
Outputs:
- encoded: bfloat16 [8, 96, 192, 256], P('frames', 'rows', 'cols'), parts along dimension 0
There are 2 independent parts, one for each index of `frames`. A program takes and returns all parts, laid end to end along the dimension named above; an argument that names none is the same for every part. Nothing has to cross between parts.
All inputs are finite; a program needn't handle non-finite values.
Results may differ from a plain program's by a relative error of at most 0.0058.
Values may be sent and summed in bfloat16 or wider, within the bound.
No kernel may reach another device: no remote copies, remote signals or barrier semaphores. Data moves between devices by JAX's collectives and lax.ppermute only.
A program may use at most 64 MiB of HBM per device.

v0:
```python
import jax
import jax.numpy as jnp
from jax import lax
from jax.experimental import pallas as pl
from jax.experimental.pallas import tpu as pltpu
from jax.sharding import PartitionSpec as P


AXES = ("rows", "cols")
CHUNKS = 2
RUN = 1
HALVES = 2
SIDE = 4
UP, DOWN = 3, 2
BF = jnp.bfloat16


def rounded(n, to):
    return -(-n // to) * to


def limit(mib):
    return pltpu.CompilerParams(vmem_limit_bytes=mib * 2**20)


def whole(a):
    return pl.BlockSpec(a.shape, lambda *_: (0,) * a.ndim)


def weights_kernel(joint, square, w1, w2, *, lidar, camera):
    joined, block = joint.shape[1], square.shape[1]
    ch = lidar + camera
    deep = w1.shape[0] // 3
    for dy in range(3):
        base = dy * deep
        for dx in range(3):
            at = (dy * 3 + dx) * ch
            w1[base + dx * lidar : base + (dx + 1) * lidar, :] = joint[at : at + lidar, :]
            to = base + 3 * lidar + dx * camera
            w1[to : to + camera, :] = joint[at + lidar : at + ch, :]
        w1[base + 3 * ch : base + deep, :] = jnp.zeros((deep - 3 * ch, joined), BF)
    tall = square.shape[0]
    gap = w2.shape[0] - tall
    w2[0:tall, 0:block] = square[...]
    w2[tall:, 0:block] = jnp.zeros((gap, block), BF)
    w2[gap:, block:] = square[...]
    w2[0:gap, block:] = jnp.zeros((gap, block), BF)


def camera_pack_kernel(pos, x, *outs, tr, span):
    frames, sc, ch, rows = x.shape
    groups = len(outs)
    width = frames * span
    place = pos[0]
    row = lax.broadcasted_iota(jnp.int32, (rows, width), 0)
    lane = lax.broadcasted_iota(jnp.int32, (rows, width), 1)
    picks = []
    for f in range(frames):
        parts = []
        for p in range(groups):
            start = lax.rem(place + p, groups) * tr - UP
            parts.append(jnp.where(row + f * span == lane + start, jnp.where(lane // span == f, 1.0, 0.0), 0.0).astype(BF))
        picks.append(jnp.concatenate(parts, axis=1))
    y = None
    for f in range(frames):
        part = jnp.dot(x[f].reshape(sc * ch, rows), picks[f], preferred_element_type=jnp.float32)
        y = part if y is None else y + part
    for p in range(groups):
        outs[p][...] = y[:, p * width : (p + 1) * width].astype(BF).reshape(sc, ch, width)


def camera_unpack_kernel(pos, *refs, groups, sc, cam_ch):
    strips = refs[:groups]
    left, right, out, stage, cells = refs[groups:]
    group = pos[0]
    lanes = left.shape[2]
    pitch = cells.shape[1]
    for p in range(groups):
        q = lax.rem(group - p + groups, groups)
        stage[pl.ds(UP + q * sc, sc)] = strips[p][...]
    stage[0:UP] = left[...]
    n = UP + groups * sc + DOWN
    stage[n - DOWN : n] = right[...]
    lead = SIDE - UP
    cells[:, 0:8, :] = jnp.zeros((lanes, 8, 128), jnp.float32)
    low = (lead + n) // 8 * 8
    cells[:, low:, :] = jnp.zeros((lanes, pitch - low, 128), jnp.float32)
    for c in range(n):
        x = stage[c].astype(jnp.float32)
        x = jnp.concatenate([x, jnp.zeros((128 - cam_ch, lanes), jnp.float32)], axis=0)
        cells[:, lead + c, :] = x.T
    step = 8
    flat = step * pitch
    lane = lax.broadcasted_iota(jnp.int32, (flat, 128), 1)

    def widen(i, _):
        x = cells[pl.ds(i * step, step)].reshape(flat, 128)
        taps = [pltpu.roll(x, 1, 0), x, pltpu.roll(x, flat - 1, 0)]
        for v in range(out.shape[2] // 128):
            y = jnp.zeros((flat, 128), jnp.float32)
            for t in range(3):
                lo, hi = t * cam_ch - v * 128, (t + 1) * cam_ch - v * 128
                if hi > 0 and lo < 128:
                    turned = pltpu.roll(taps[t], lo % 128, 1) if lo % 128 else taps[t]
                    y = jnp.where((lane >= lo) & (lane < hi), turned, y)
            out[pl.ds(i * step, step), :, v * 128 : (v + 1) * 128] = y.astype(BF).reshape(step, pitch, 128)
        return 0

    lax.fori_loop(0, lanes // step, widen, 0)


def pick_kernel(pos, *refs):
    parts = (len(refs) - 2) // 2
    tail, head = refs[-2:]
    for d in range(parts):

        @pl.when(pos[0] == d)
        def _():
            tail[...] = refs[d][...]

        @pl.when(pos[1] == d)
        def _():
            head[...] = refs[parts + d][...]


def pick(arrays, tail_of, head_of, dim):
    size = arrays[0].shape[dim]
    specs, shapes, outs = [], [], []
    for n, at in ((UP, size // UP - 1), (DOWN, 0)):
        shape = arrays[0].shape[:dim] + (n,) + arrays[0].shape[dim + 1 :]
        where = tuple(at if i == dim else 0 for i in range(len(shape)))
        specs += [pl.BlockSpec(shape, lambda i, p, where=where: where)] * len(arrays)
        shapes.append(jax.ShapeDtypeStruct(shape, BF))
        outs.append(pl.BlockSpec(shape, lambda i, p, n=len(shape): (0,) * n))
    return pl.pallas_call(
        pick_kernel,
        grid_spec=pltpu.PrefetchScalarGridSpec(num_scalar_prefetch=1, grid=(1,), in_specs=specs, out_specs=outs),
        out_shape=shapes,
        compiler_params=limit(3),
    )(jnp.stack([tail_of, head_of]).astype(jnp.int32), *arrays, *arrays)


def conv_kernel(pos, *refs, parts, sh, tr, pitch, rows, cols):
    windows = refs[:parts]
    above, below, camera, w1, b1, w2, b2 = refs[parts : parts + 7]
    outs = refs[parts + 7 : parts + 7 + HALVES]
    tile, taps, mid, cells = refs[parts + 7 + HALVES :]
    group, member, half_id = pos[0], pos[1], pos[2]
    wide = windows[0].shape[2]
    lidar = windows[0].shape[3]
    joined = w1.shape[1]
    block = w2.shape[1] // 2

    @pl.when(pl.program_id(0) == 0)
    def _():
        tile[...] = jnp.zeros(tile.shape, BF)

    tile[0:UP, 0:wide, :] = above[0]
    for d in range(parts):
        source = lax.rem(member - d + parts, parts)
        tile[pl.ds(UP + source * sh, sh), 0:wide, :] = windows[d][0]
    tile[UP + tr : UP + tr + DOWN, 0:wide, :] = below[0]

    step = 6
    flat = step * pitch

    def shift(i, _):
        r = i * step
        x = tile[pl.ds(r, step)].reshape(flat, lidar)
        x32 = x.astype(jnp.float32)
        taps[pl.ds(r, step), :, 0:lidar] = pltpu.roll(x32, 1, 0).astype(BF).reshape(step, pitch, lidar)
        taps[pl.ds(r, step), :, lidar : 2 * lidar] = x.reshape(step, pitch, lidar)
        taps[pl.ds(r, step), :, 2 * lidar :] = pltpu.roll(x32, flat - 1, 0).astype(BF).reshape(step, pitch, lidar)
        return 0

    lax.fori_loop(0, (tr + 6) // step, shift, 0)

    n1 = 4
    m1 = n1 * pitch
    col0 = member * (wide - 2 * SIDE) - SIDE

    def first(i, _):
        r = i * n1
        lhs = []
        for dy in range(3):
            lhs.append(taps[pl.ds(r + dy, n1)].reshape(m1, 3 * lidar))
            lhs.append(camera[0, pl.ds(r + dy, n1)].reshape(m1, camera.shape[3]))
        acc = jnp.dot(jnp.concatenate(lhs, axis=1), w1[...], preferred_element_type=jnp.float32)
        v = jnp.maximum(acc + b1[...], 0.0)
        at = lax.broadcasted_iota(jnp.int32, (m1, joined), 0)
        row = group * tr - 2 + r + at // pitch
        col = col0 + at % pitch
        keep = (row >= 0) & (row < rows) & (col >= 0) & (col < cols)
        v = jnp.where(keep, v, 0.0)
        shape = (n1 // 2, 2, pitch, joined)
        p = pl.ds(i * (n1 // 2), n1 // 2)
        mid[p, :, :, 0:joined] = pltpu.roll(v, 1, 0).astype(BF).reshape(shape)
        mid[p, :, :, joined : 2 * joined] = v.astype(BF).reshape(shape)
        mid[p, :, :, 2 * joined :] = pltpu.roll(v, m1 - 1, 0).astype(BF).reshape(shape)
        return 0

    lax.fori_loop(0, (tr + 4) // n1, first, 0)

    n2 = (tr + 2) // 2
    m2 = n2 * pitch
    lhs = [mid[i // 2 : i // 2 + n2, i % 2].reshape(m2, 3 * joined) for i in range(4)]
    acc = jnp.dot(jnp.concatenate(lhs, axis=1), w2[...], preferred_element_type=jnp.float32)
    v = jnp.maximum(acc + b2[...], 0.0)
    at = lax.broadcasted_iota(jnp.int32, (m2, 2 * block), 0)
    half = lax.broadcasted_iota(jnp.int32, (m2, 2 * block), 1) // block
    row = group * tr - 1 + (at // pitch) * 2 + half
    col = col0 + at % pitch
    keep = (row >= 0) & (row < rows) & (col >= 0) & (col < cols)
    v = jnp.where(keep, v, 0.0)
    cells[:, 0] = v[:, :block].reshape(n2, pitch, block)
    cells[:, 1] = v[:, block:].reshape(n2, pitch, block)
    pairs = tr // 2
    w = (wide - 2 * SIDE) // HALVES
    for sub in range(HALVES):
        c = SIDE + sub * w
        even = cells[0:pairs, 1, c : c + w, :].astype(BF)
        odd = cells[1 : pairs + 1, 0, c : c + w, :].astype(BF)
        top = cells[0, 0, c : c + w, :]
        corner = jnp.broadcast_to(cells[pairs, 0, c - 1 : c, :], (w, block))
        edge = jnp.where(half_id == 0, top, corner).astype(BF)
        beside = cells[0:pairs, :, c - 1, :].reshape(tr, block).astype(BF)
        for h in range(HALVES):

            @pl.when(lax.rem(half_id + h, HALVES) == sub)
            def _():
                outs[h][0, 0:pairs, 0] = even
                outs[h][0, 0:pairs, 1] = odd
                outs[h][0, pairs, 0] = edge
                outs[h][0, pairs, 1] = beside


def encode_kernel(pos, *refs, parts, half_rows, w):
    pieces = refs[:parts]
    w3, b3, wp, bp = refs[parts : parts + 4]
    out, grid, grown = refs[-3:]
    me = pos[0]
    block = pieces[0].shape[4]
    for h in range(parts):
        part = lax.rem(me - h + parts, parts)
        base = part * half_rows
        x = pieces[h]
        grid[pl.ds(base, half_rows), 1, 1 : w + 1, :] = x[0, 0:half_rows, 0].astype(jnp.float32)
        grid[pl.ds(base + 1, half_rows), 0, 1 : w + 1, :] = x[0, 0:half_rows, 1].astype(jnp.float32)
        beside = x[0, half_rows, 1].astype(jnp.float32)
        for r in range(2 * half_rows):
            grid[base + r // 2, r % 2, 0:1, :] = beside[r : r + 1]
        edge = x[0, half_rows, 0].astype(jnp.float32)

        @pl.when(part == 0)
        def _():
            grid[0, 0, 1 : w + 1, :] = edge

        @pl.when(part == parts - 1)
        def _():
            grid[parts * half_rows, 0, 0:1, :] = edge[0:1]

    n = parts * half_rows
    jd = rounded(w // 2, 8)
    m = n * jd
    lhs = []
    for a in range(3):
        for b in range(3):
            x = grid[pl.ds(a // 2, n), a % 2, pl.ds(b, jd, stride=2), :]
            lhs.append(x.reshape(m, block).astype(BF))
    deep = jnp.dot(jnp.concatenate(lhs, axis=1), w3[...], preferred_element_type=jnp.float32)
    deep = jnp.maximum(deep + b3[...], 0.0).astype(BF)
    branch = jnp.dot(deep, wp[...], preferred_element_type=jnp.float32)
    branch = jnp.maximum(branch + bp[...], 0.0).astype(BF).astype(jnp.float32).reshape(n, jd, wp.shape[1])
    grown[:, pl.ds(0, jd, stride=2), :] = branch
    grown[:, pl.ds(1, jd, stride=2), :] = branch
    up = grown[:, 0:w, :].astype(BF)
    out[0, :, 0, :, 0:block] = grid[0:n, 1, 1 : w + 1, :].astype(BF)
    out[0, :, 1, :, 0:block] = grid[1 : n + 1, 0, 1 : w + 1, :].astype(BF)
    out[0, :, 0, :, block:] = up
    out[0, :, 1, :, block:] = up


def solution(mesh):
    n_rows, n_cols = mesh.shape["rows"], mesh.shape["cols"]
    members = n_cols // HALVES
    groups = n_rows * HALVES
    total = n_rows * n_cols

    def local(lidar, camera, joined_weight, joined_bias, block_weight, block_bias, down_weight, down_bias, proj_weight, proj_bias):
        frames, sh, cols, lidar_ch = lidar.shape
        rows, sc, cam_ch = camera.shape[1:]
        tr = sh * members
        tw = cols // members
        wide = tw + 2 * SIDE
        pitch = rounded(wide, 16)
        w = cols // n_cols
        joined = joined_weight.shape[3]
        block = block_weight.shape[3]
        place = lax.axis_index(AXES)
        group = place // members
        member = place % members
        cindex = lax.axis_index("cols")
        kgroup = cindex // members

        def send(x, pairs):
            return lax.ppermute(x, AXES, pairs)

        def across(x, by_group, by_member):
            pairs = []
            for g in range(groups):
                for j in range(members):
                    if 0 <= g + by_group < groups and 0 <= j + by_member < members:
                        pairs.append((g * members + j, (g + by_group) * members + j + by_member))
            return send(x, pairs)

        joint = joined_weight.reshape(-1, joined)
        square = block_weight.reshape(-1, block)
        deep1 = 3 * (3 * lidar_ch + rounded(3 * cam_ch, 256))
        w1, w2 = pl.pallas_call(
            lambda *refs: weights_kernel(*refs, lidar=lidar_ch, camera=cam_ch),
            out_shape=[
                jax.ShapeDtypeStruct((deep1, joined), BF),
                jax.ShapeDtypeStruct((4 * 3 * joined, 2 * block), BF),
            ],
            compiler_params=limit(14),
            name="weights",
        )(joint, square)
        w3 = down_weight.reshape(-1, down_weight.shape[3])
        b1 = joined_bias.reshape(1, -1)
        b2 = jnp.concatenate([block_bias, block_bias]).reshape(1, -1)
        b3 = down_bias.reshape(1, -1)
        bp = proj_bias.reshape(1, -1)

        span = rounded(tr + UP + DOWN, 8)
        lanes = frames * span
        turned = jnp.transpose(camera, (0, 2, 3, 1))
        strip = jax.ShapeDtypeStruct((sc, cam_ch, lanes), BF)
        packed = pl.pallas_call(
            lambda *refs: camera_pack_kernel(*refs, tr=tr, span=span),
            grid_spec=pltpu.PrefetchScalarGridSpec(
                num_scalar_prefetch=1,
                grid=(1,),
                in_specs=[whole(turned)],
                out_specs=[whole(strip)] * groups,
            ),
            out_shape=[strip] * groups,
            compiler_params=limit(14),
            name="camera_pack",
        )(place.reshape(1).astype(jnp.int32), turned)
        lidar, packed = lax.optimization_barrier((lidar, packed))
        arrived = [
            send(packed[p], [(s, ((s + p) % groups) * members + s // groups) for s in range(total)])
            for p in range(groups)
        ]
        tail, head = pick(arrived, (group + 1) % groups, group, 0)
        left = across(tail, 0, 1)
        right = across(head, 0, -1)
        cam = pl.pallas_call(
            lambda *refs: camera_unpack_kernel(*refs, groups=groups, sc=sc, cam_ch=cam_ch),
            grid_spec=pltpu.PrefetchScalarGridSpec(
                num_scalar_prefetch=1,
                grid=(1,),
                in_specs=[whole(x) for x in arrived] + [whole(left), whole(right)],
                out_specs=pl.BlockSpec((lanes, pitch, rounded(3 * cam_ch, 256)), lambda i, p: (0, 0, 0)),
                scratch_shapes=[
                    pltpu.VMEM((tw + UP + DOWN, cam_ch, lanes), BF),
                    pltpu.VMEM((lanes, pitch, 128), jnp.float32),
                ],
            ),
            out_shape=jax.ShapeDtypeStruct((lanes, pitch, rounded(3 * cam_ch, 256)), BF),
            compiler_params=limit(16),
            name="camera_unpack",
        )(group.reshape(1).astype(jnp.int32), *arrived, left, right)
        cam = cam.reshape(frames, span, pitch, -1)

        padded = jnp.pad(lidar, ((0, 0), (0, 0), (SIDE, SIDE), (0, 0)))
        pos = jnp.stack([group, member, kgroup]).astype(jnp.int32)
        pairs2 = (tr + 2) // 2
        half_rows = tr // 2
        n = HALVES * half_rows
        jd = rounded(w // 2, 8)
        blocks = jax.ShapeDtypeStruct((RUN, pairs2, 2, w, block), BF)
        flops = 2 * RUN * pitch * ((tr + 4) * w1.shape[0] * joined + pairs2 * w2.shape[0] * 2 * block)
        encoded = None
        step = frames // CHUNKS
        for f0 in range(0, frames, step):
            windows = []
            for d in range(members):
                x = lax.dynamic_slice(padded, (f0, 0, ((member + d) % members) * tw, 0), (step, sh, wide, lidar_ch))
                if d:
                    x = send(x, [(g * members + j, g * members + (j + d) % members) for g in range(groups) for j in range(members)])
                windows.append(x)
            last, head = pick(windows, (member + 1) % members, member, 1)
            above = across(last, 1, 0)
            below = across(head, -1, 0)
            for f1 in range(f0, f0 + step, RUN):
                framed = lambda a, lo: pl.BlockSpec((1,) + a.shape[1:], lambda f, p: (f + lo,) + (0,) * (a.ndim - 1))
                lo = f1 - f0
                tiles = pl.pallas_call(
                    lambda *refs: conv_kernel(*refs, parts=members, sh=sh, tr=tr, pitch=pitch, rows=rows, cols=cols),
                    grid_spec=pltpu.PrefetchScalarGridSpec(
                        num_scalar_prefetch=1,
                        grid=(RUN,),
                        in_specs=[framed(x, lo) for x in [*windows, above, below]] + [framed(cam, f1), whole(w1), whole(b1), whole(w2), whole(b2)],
                        out_specs=[framed(blocks, 0)] * HALVES,
                        scratch_shapes=[
                            pltpu.VMEM((tr + 6, pitch, lidar_ch), BF),
                            pltpu.VMEM((tr + 6, pitch, 3 * lidar_ch), BF),
                            pltpu.VMEM(((tr + 4) // 2, 2, pitch, 3 * joined), BF),
                            pltpu.VMEM((pairs2, 2, pitch, block), jnp.float32),
                        ],
                    ),
                    out_shape=[blocks] * HALVES,
                    compiler_params=limit(28),
                    cost_estimate=pl.CostEstimate(flops=flops, bytes_accessed=2 * 10**6 * RUN, transcendentals=0),
                    name="convs",
                )(pos, *windows, above, below, cam, w1, b1, w2, b2)
                pieces = []
                for h in range(HALVES):
                    pairs = []
                    for s in range(total):
                        r, c = divmod(s, n_cols)
                        k, j = divmod(c, members)
                        pairs.append((s, r * n_cols + HALVES * j + (k + h) % HALVES))
                    pieces.append(send(tiles[h], pairs))
                old = [] if encoded is None else [encoded]
                encoded = pl.pallas_call(
                    lambda *refs: encode_kernel(*refs, parts=HALVES, half_rows=half_rows, w=w),
                    grid_spec=pltpu.PrefetchScalarGridSpec(
                        num_scalar_prefetch=1,
                        grid=(RUN,),
                        in_specs=[framed(x, 0) for x in pieces] + [whole(x) for x in (w3, b3, proj_weight, bp)] + [pl.BlockSpec(memory_space=pl.ANY)] * len(old),
                        out_specs=pl.BlockSpec((1, n, 2, w, 2 * block), lambda f, p, f1=f1: (f + f1, 0, 0, 0, 0)),
                        scratch_shapes=[
                            pltpu.VMEM((n + 1, 2, rounded(w + 1, 8) + 16, block), jnp.float32),
                            pltpu.VMEM((n, 2 * jd, block), jnp.float32),
                        ],
                    ),
                    out_shape=jax.ShapeDtypeStruct((frames, n, 2, w, 2 * block), BF),
                    input_output_aliases={5 + HALVES: 0} if old else {},
                    compiler_params=limit(12),
                    cost_estimate=pl.CostEstimate(flops=2 * RUN * n * jd * w3.shape[0] * 256, bytes_accessed=10**6 * RUN, transcendentals=0),
                    name="encode",
                )(cindex.reshape(1).astype(jnp.int32), *pieces, w3, b3, proj_weight, bp, *old)
        return encoded.reshape(frames, 2 * n, w, 2 * block)

    return jax.shard_map(
        local,
        mesh=mesh,
        in_specs=(
            P("frames", AXES, None, None),
            P("frames", None, AXES, None),
            P(), P(), P(), P(), P(), P(), P(), P(),
        ),
        out_specs=P("frames", "rows", "cols", None),
        check_vma=False,
    )
```

profile of v0, /device:TPU:2, one launch (start us, length us, event | category | flops | bytes accessed | tf_op | source)
XLA Modules:
  0.0 152.8 jit_solution(5810957170199836259)
XLA Ops:
  1.2 2.0 %camera_pack.1 = (bf16[12,80,128]{2,1,0:T(8,128)(2,1)}, bf16[12,80,128]{2,1,0:T(8,128)(2,1)}, bf16[12,80,128]{2,1,0:T(8,128)(2,1)}, bf16[12,80,128]{2,1,0:T(8,128)(2,1)S(1)}) custom-call(s32[1]{0:T(128)} %bitcast.4.refs_0_, bf16[4,12,80,96]{3,2,1,0:T(8,128)(2,1)S(1)} %bitcast.26), custom_call_target="tpu_custom_call" | custom-call | tf_op jit(solution)/shard_map/camera_pack/pallas_call | solution.py:338
  3.2 3.4 %collective-permute-start.5 = (bf16[12,80,128]{2,1,0:T(8,128)(2,1)}, bf16[12,80,128]{2,1,0:T(8,128)(2,1)S(1)}, u32[]{:S(2)}, u32[]{:S(2)}) collective-permute-start(bf16[12,80,128]{2,1,0:T(8,128)(2,1)} %get-tuple-element.37), channel_id=1, source_target_pairs={{0,0},{2,8},{4,16},{6,24},{8,2},{10,10},{12,18},{14,26},{16,4},{18... | collective-permute-start | bytes 737288 | tf_op jit(solution)/shard_map/ppermute | solution.py:306
  6.7 4.2 %collective-permute-start.6 = (bf16[12,80,128]{2,1,0:T(8,128)(2,1)}, bf16[12,80,128]{2,1,0:T(8,128)(2,1)S(1)}, u32[]{:S(2)}, u32[]{:S(2)}) collective-permute-start(bf16[12,80,128]{2,1,0:T(8,128)(2,1)} %get-tuple-element.38), channel_id=1, source_target_pairs={{0,8},{2,16},{4,24},{6,0},{8,10},{10,18},{12,26},{14,2},{16,12},{1... | collective-permute-start | bytes 737288 | tf_op jit(solution)/shard_map/ppermute | solution.py:306
  10.9 4.5 %pad_dynamic-slice_fusion = (bf16[2,6,56,256]{3,2,1,0:T(8,128)(2,1)}, bf16[2,6,56,256]{3,2,1,0:T(8,128)(2,1)}, bf16[2,6,56,256]{3,2,1,0:T(8,128)(2,1)}, bf16[2,6...) fusion(s32[]{:T(128)S(6)} %select_n.72, ...), kind=kLoop, calls=%fused_computation | loop fusion | bytes 5111824 | tf_op jit(solution)/shard_map/dynamic_slice | solution.py:389
  15.4 3.4 %collective-permute-start.8 = (bf16[12,80,128]{2,1,0:T(8,128)(2,1)S(1)}, bf16[12,80,128]{2,1,0:T(8,128)(2,1)S(1)}, u32[]{:S(2)}, u32[]{:S(2)}) collective-permute-start(bf16[12,80,128]{2,1,0:T(8,128)(2,1)S(1)} %get-tuple-element.40), channel_id=1, source_target_pairs={{0,24},{2,0},{4,8},{6,16},{8,26},{10,2},{12,10},{14,18},{16,28},{1... | collective-permute-start | bytes 737288 | tf_op jit(solution)/shard_map/ppermute | solution.py:306
  18.8 17.3 %collective-permute-done.5.refs_0_.refs_4_.refs_1_ = bf16[12,80,128]{2,1,0:T(8,128)(2,1)S(1)} collective-permute-done((bf16[12,80,128]{2,1,0:T(8,128)(2,1)}, bf16[12,80,128]{2,1,0:T(8,128)(2,1)S(1)}, u32[]{:S(2)}, u32[]{:S(2)}) %collective-permute-start.5) | collective-permute-done | bytes 245792 | tf_op jit(solution)/shard_map/ppermute | solution.py:306
  36.1 2.0 %collective-permute-start.15 = (bf16[2,6,56,256]{3,2,1,0:T(8,128)(2,1)}, bf16[2,6,56,256]{3,2,1,0:T(8,128)(2,1)}, u32[]{:S(2)}, u32[]{:S(2)}) collective-permute-start(bf16[2,6,56,256]{3,2,1,0:T(8,128)(2,1)} %get-tuple-element.59), channel_id=1, source_target_pairs={{0,2},{2,4},{4,6},{6,0},{8,10},{10,12},{12,14},{14,8},{16,18},{18,... | collective-permute-start | bytes 1032200 | tf_op jit(solution)/shard_map/ppermute | solution.py:306
  38.1 13.8 %collective-permute-done.8.refs_3_.refs_7_.refs_4_ = bf16[12,80,128]{2,1,0:T(8,128)(2,1)S(1)} collective-permute-done((bf16[12,80,128]{2,1,0:T(8,128)(2,1)S(1)}, bf16[12,80,128]{2,1,0:T(8,128)(2,1)S(1)}, u32[]{:S(2)}, u32[]{:S(2)}) %collective-permute-start.8) | collective-permute-done | bytes 245792 | tf_op jit(solution)/shard_map/ppermute | solution.py:306
  52.6 3.9 %collective-permute-start.9 = (bf16[3,80,128]{2,1,0:T(8,128)(2,1)S(1)}, bf16[3,80,128]{2,1,0:T(8,128)(2,1)S(1)}, u32[]{:S(2)}, u32[]{:S(2)}) collective-permute-start(bf16[3,80,128]{2,1,0:T(8,128)(2,1)S(1)} %get-tuple-element.41), channel_id=1, source_target_pairs={{0,2},{2,4},{4,6},{8,10},{10,12},{12,14},{16,18},{18,20},{20,22},{... | collective-permute-start | bytes 184328 | tf_op jit(solution)/shard_map/ppermute | solution.py:306
  61.6 3.6 %collective-permute-done.10.refs_6_ = bf16[2,80,128]{2,1,0:T(8,128)(2,1)S(1)} collective-permute-done((bf16[2,80,128]{2,1,0:T(8,128)(2,1)S(1)}, bf16[2,80,128]{2,1,0:T(8,128)(2,1)S(1)}, u32[]{:S(2)}, u32[]{:S(2)}) %collective-permute-start.10) | collective-permute-done | bytes 40992 | tf_op jit(solution)/shard_map/ppermute | solution.py:306
  65.2 6.6 %collective-permute-start.3 = (bf16[2,3,56,256]{3,2,1,0:T(8,128)(2,1)S(1)}, bf16[2,3,56,256]{3,2,1,0:T(8,128)(2,1)S(1)}, u32[]{:S(2)}, u32[]{:S(2)}) collective-permute-start(bf16[2,3,56,256]{3,2,1,0:T(8,128)(2,1)S(1)} %get-tuple-element.35), channel_id=1, source_target_pairs={{0,8},{2,10},{4,12},{6,14},{8,16},{10,18},{12,20},{14,22},{16,24},... | collective-permute-start | bytes 516104 | tf_op jit(solution)/shard_map/ppermute | solution.py:306
  71.9 1.9 %collective-permute-start.4 = (bf16[2,2,56,256]{3,2,1,0:T(8,128)(2,1)S(1)}, bf16[2,2,56,256]{3,2,1,0:T(8,128)(2,1)S(1)}, u32[]{:S(2)}, u32[]{:S(2)}) collective-permute-start(bf16[2,2,56,256]{3,2,1,0:T(8,128)(2,1)S(1)} %get-tuple-element.36), channel_id=1, source_target_pairs={{8,0},{10,2},{12,4},{14,6},{16,8},{18,10},{20,12},{22,14},{24,16},... | collective-permute-start | bytes 344072 | tf_op jit(solution)/shard_map/ppermute | solution.py:306
  74.2 4.8 %camera_unpack.1 = bf16[128,64,256]{2,1,0:T(8,128)(2,1)S(1)} custom-call(s32[1]{0:T(128)} %bitcast.1.refs_0_, bf16[12,80,128]{2,1,0:T(8,128)(2,1)S(1)} %collective-permute-done.5.refs_0_.refs_4_.refs_1_, bf16[12,80,128]{2,1,0:T(8,128)(2,1)S(1)} %collective-permute-done.6.refs_1_.refs_5_.refs_2_, ...), custom_call_target="tpu_custom_call" | custom-call | tf_op jit(solution)/shard_map/camera_unpack/pallas_call | solution.py:358
  81.0 4.8 %collective-permute-start.18 = (bf16[2,3,56,256]{3,2,1,0:T(8,128)(2,1)S(1)}, bf16[2,3,56,256]{3,2,1,0:T(8,128)(2,1)S(1)}, u32[]{:S(2)}, u32[]{:S(2)}) collective-permute-start(bf16[2,3,56,256]{3,2,1,0:T(8,128)(2,1)S(1)} %get-tuple-element.49), channel_id=1, source_target_pairs={{0,8},{2,10},{4,12},{6,14},{8,16},{10,18},{12,20},{14,22},{16,24},... | collective-permute-start | bytes 516104 | tf_op jit(solution)/shard_map/ppermute | solution.py:306
  85.8 2.8 %collective-permute-start.19 = (bf16[2,2,56,256]{3,2,1,0:T(8,128)(2,1)S(1)}, bf16[2,2,56,256]{3,2,1,0:T(8,128)(2,1)S(1)}, u32[]{:S(2)}, u32[]{:S(2)}) collective-permute-start(bf16[2,2,56,256]{3,2,1,0:T(8,128)(2,1)S(1)} %get-tuple-element.50), channel_id=1, source_target_pairs={{8,0},{10,2},{12,4},{14,6},{16,8},{18,10},{20,12},{22,14},{24,16},... | collective-permute-start | bytes 344072 | tf_op jit(solution)/shard_map/ppermute | solution.py:306
  88.7 8.2 %convs.5 = (bf16[1,13,2,24,128]{4,3,2,1,0:T(8,128)(2,1)S(1)}, bf16[1,13,2,24,128]{4,3,2,1,0:T(8,128)(2,1)S(1)}) custom-call(s32[3]{0:T(128)S(1)} %pad_add_fusion.refs_0_, bf16[2,6,56,256]{3,2,1,0:T(8,128)(2,1)S(1)} %get-tuple-element.61.refs_0_.refs_4_.refs_1_, bf16[2,6,56,256]{3,2,1,0:T(8,128)(2,1)} %collective-permute-done.refs_1_.refs_5_.refs_2_, ...), custom_call_target="tpu_custom_call" | custom-call | flops 4127195136 | bytes 2000000 | tf_op jit(solution)/shard_map/convs/pallas_call | solution.py:399
  97.6 6.9 %collective-permute-start.14 = (bf16[1,13,2,24,128]{4,3,2,1,0:T(8,128)(2,1)S(1)}, bf16[1,13,2,24,128]{4,3,2,1,0:T(8,128)(2,1)S(1)}, u32[]{:S(2)}, u32[]{:S(2)}) collective-permute-start(bf16[1,13,2,24,128]{4,3,2,1,0:T(8,128)(2,1)S(1)} %get-tuple-element.48), channel_id=1, source_target_pairs={{0,2},{2,6},{4,10},{6,14},{8,0},{10,4},{12,8},{14,12},{16,18},{18,... | collective-permute-start | bytes 479240 | tf_op jit(solution)/shard_map/ppermute | solution.py:306
  104.4 8.2 %convs.6 = (bf16[1,13,2,24,128]{4,3,2,1,0:T(8,128)(2,1)S(1)}, bf16[1,13,2,24,128]{4,3,2,1,0:T(8,128)(2,1)S(1)}) custom-call(s32[3]{0:T(128)S(1)} %pad_add_fusion.refs_0_, bf16[2,6,56,256]{3,2,1,0:T(8,128)(2,1)S(1)} %get-tuple-element.58.refs_0_.refs_4_.refs_1_, bf16[2,6,56,256]{3,2,1,0:T(8,128)(2,1)} %collective-permute-done.15.refs_1_.refs_5_.refs_2_, ...), custom_call_target="tpu_custom_call" | custom-call | flops 4127195136 | bytes 2000000 | tf_op jit(solution)/shard_map/convs/pallas_call | solution.py:399
  113.3 4.4 %collective-permute-start.21 = (bf16[1,13,2,24,128]{4,3,2,1,0:T(8,128)(2,1)S(1)}, bf16[1,13,2,24,128]{4,3,2,1,0:T(8,128)(2,1)S(1)}, u32[]{:S(2)}, u32[]{:S(2)}) collective-permute-start(bf16[1,13,2,24,128]{4,3,2,1,0:T(8,128)(2,1)S(1)} %get-tuple-element.52), channel_id=1, source_target_pairs={{0,2},{2,6},{4,10},{6,14},{8,0},{10,4},{12,8},{14,12},{16,18},{18,... | collective-permute-start | bytes 479240 | tf_op jit(solution)/shard_map/ppermute | solution.py:306
  117.7 8.2 %convs.7 = (bf16[1,13,2,24,128]{4,3,2,1,0:T(8,128)(2,1)S(1)}, bf16[1,13,2,24,128]{4,3,2,1,0:T(8,128)(2,1)S(1)}) custom-call(s32[3]{0:T(128)S(1)} %pad_add_fusion.refs_0_, bf16[2,6,56,256]{3,2,1,0:T(8,128)(2,1)S(1)} %get-tuple-element.58.refs_0_.refs_4_.refs_1_, bf16[2,6,56,256]{3,2,1,0:T(8,128)(2,1)} %collective-permute-done.15.refs_1_.refs_5_.refs_2_, ...), custom_call_target="tpu_custom_call" | custom-call | flops 4127195136 | bytes 2000000 | tf_op jit(solution)/shard_map/convs/pallas_call | solution.py:399
  126.7 4.2 %collective-permute-start.23 = (bf16[1,13,2,24,128]{4,3,2,1,0:T(8,128)(2,1)S(1)}, bf16[1,13,2,24,128]{4,3,2,1,0:T(8,128)(2,1)S(1)}, u32[]{:S(2)}, u32[]{:S(2)}) collective-permute-start(bf16[1,13,2,24,128]{4,3,2,1,0:T(8,128)(2,1)S(1)} %get-tuple-element.54), channel_id=1, source_target_pairs={{0,2},{2,6},{4,10},{6,14},{8,0},{10,4},{12,8},{14,12},{16,18},{18,... | collective-permute-start | bytes 479240 | tf_op jit(solution)/shard_map/ppermute | solution.py:306
  130.9 8.2 %convs.4 = (bf16[1,13,2,24,128]{4,3,2,1,0:T(8,128)(2,1)S(1)}, bf16[1,13,2,24,128]{4,3,2,1,0:T(8,128)(2,1)S(1)}) custom-call(s32[3]{0:T(128)S(1)} %pad_add_fusion.refs_0_, bf16[2,6,56,256]{3,2,1,0:T(8,128)(2,1)S(1)} %get-tuple-element.61.refs_0_.refs_4_.refs_1_, bf16[2,6,56,256]{3,2,1,0:T(8,128)(2,1)} %collective-permute-done.refs_1_.refs_5_.refs_2_, ...), custom_call_target="tpu_custom_call" | custom-call | flops 4127195136 | bytes 2000000 | tf_op jit(solution)/shard_map/convs/pallas_call | solution.py:399
  139.8 4.2 %collective-permute-start.12 = (bf16[1,13,2,24,128]{4,3,2,1,0:T(8,128)(2,1)S(1)}, bf16[1,13,2,24,128]{4,3,2,1,0:T(8,128)(2,1)S(1)}, u32[]{:S(2)}, u32[]{:S(2)}) collective-permute-start(bf16[1,13,2,24,128]{4,3,2,1,0:T(8,128)(2,1)S(1)} %get-tuple-element.46), channel_id=1, source_target_pairs={{0,2},{2,6},{4,10},{6,14},{8,0},{10,4},{12,8},{14,12},{16,18},{18,... | collective-permute-start | bytes 479240 | tf_op jit(solution)/shard_map/ppermute | solution.py:306
  148.7 2.6 %collective-permute-done.12.refs_2_ = bf16[1,13,2,24,128]{4,3,2,1,0:T(8,128)(2,1)S(1)} collective-permute-done((bf16[1,13,2,24,128]{4,3,2,1,0:T(8,128)(2,1)S(1)}, bf16[1,13,2,24,128]{4,3,2,1,0:T(8,128)(2,1)S(1)}, u32[]{:S(2)}, u32[]{:S(2)}) %collective-permute-start.12) | collective-permute-done | bytes 159776 | tf_op jit(solution)/shard_map/ppermute | solution.py:306
  (61 shorter events, 18.2 us)
Async XLA Ops:
  3.2 32.8 %collective-permute-start.5 = (bf16[12,80,128]{2,1,0:T(8,128)(2,1)}, bf16[12,80,128]{2,1,0:T(8,128)(2,1)S(1)}, u32[]{:S(2)}, u32[]{:S(2)}) collective-permute-start(bf16[12,80,128]{2,1,0:T(8,128)(2,1)} %get-tuple-element.37), channel_id=1, source_target_pairs={{0,0},{2,8},{4,16},{6,24},{8,2},{10,10},{12,18},{14,26},{16,4},{18... | collective-permute-start | bytes 737288 | tf_op jit(solution)/shard_map/ppermute | solution.py:306
  6.7 29.4 %collective-permute-start.6 = (bf16[12,80,128]{2,1,0:T(8,128)(2,1)}, bf16[12,80,128]{2,1,0:T(8,128)(2,1)S(1)}, u32[]{:S(2)}, u32[]{:S(2)}) collective-permute-start(bf16[12,80,128]{2,1,0:T(8,128)(2,1)} %get-tuple-element.38), channel_id=1, source_target_pairs={{0,8},{2,16},{4,24},{6,0},{8,10},{10,18},{12,26},{14,2},{16,12},{1... | collective-permute-start | bytes 737288 | tf_op jit(solution)/shard_map/ppermute | solution.py:306
  15.3 36.6 %collective-permute-start = (bf16[2,6,56,256]{3,2,1,0:T(8,128)(2,1)}, bf16[2,6,56,256]{3,2,1,0:T(8,128)(2,1)}, u32[]{:S(2)}, u32[]{:S(2)}) collective-permute-start(bf16[2,6,56,256]{3,2,1,0:T(8,128)(2,1)} %get-tuple-element.56), channel_id=1, source_target_pairs={{0,2},{2,4},{4,6},{6,0},{8,10},{10,12},{12,14},{14,8},{16,18},{18,... | collective-permute-start | bytes 1032200 | tf_op jit(solution)/shard_map/ppermute | solution.py:306
  15.3 20.8 %collective-permute-start.7 = (bf16[12,80,128]{2,1,0:T(8,128)(2,1)}, bf16[12,80,128]{2,1,0:T(8,128)(2,1)S(1)}, u32[]{:S(2)}, u32[]{:S(2)}) collective-permute-start(bf16[12,80,128]{2,1,0:T(8,128)(2,1)} %get-tuple-element.39), channel_id=1, source_target_pairs={{0,16},{2,24},{4,0},{6,8},{8,18},{10,26},{12,2},{14,10},{16,20},{1... | collective-permute-start | bytes 737288 | tf_op jit(solution)/shard_map/ppermute | solution.py:306
  15.4 36.5 %collective-permute-start.8 = (bf16[12,80,128]{2,1,0:T(8,128)(2,1)S(1)}, bf16[12,80,128]{2,1,0:T(8,128)(2,1)S(1)}, u32[]{:S(2)}, u32[]{:S(2)}) collective-permute-start(bf16[12,80,128]{2,1,0:T(8,128)(2,1)S(1)} %get-tuple-element.40), channel_id=1, source_target_pairs={{0,24},{2,0},{4,8},{6,16},{8,26},{10,2},{12,10},{14,18},{16,28},{1... | collective-permute-start | bytes 737288 | tf_op jit(solution)/shard_map/ppermute | solution.py:306
  36.1 16.5 %collective-permute-start.1 = (bf16[2,6,56,256]{3,2,1,0:T(8,128)(2,1)}, bf16[2,6,56,256]{3,2,1,0:T(8,128)(2,1)}, u32[]{:S(2)}, u32[]{:S(2)}) collective-permute-start(bf16[2,6,56,256]{3,2,1,0:T(8,128)(2,1)} %get-tuple-element.57), channel_id=1, source_target_pairs={{0,4},{2,6},{4,0},{6,2},{8,12},{10,14},{12,8},{14,10},{16,20},{18,... | collective-permute-start | bytes 1032200 | tf_op jit(solution)/shard_map/ppermute | solution.py:306
  36.1 22.3 %collective-permute-start.2 = (bf16[2,6,56,256]{3,2,1,0:T(8,128)(2,1)}, bf16[2,6,56,256]{3,2,1,0:T(8,128)(2,1)}, u32[]{:S(2)}, u32[]{:S(2)}) collective-permute-start(bf16[2,6,56,256]{3,2,1,0:T(8,128)(2,1)} %get-tuple-element.62), channel_id=1, source_target_pairs={{0,6},{2,0},{4,2},{6,4},{8,14},{10,8},{12,10},{14,12},{16,22},{18,... | collective-permute-start | bytes 1032200 | tf_op jit(solution)/shard_map/ppermute | solution.py:306
  36.1 43.0 %collective-permute-start.15 = (bf16[2,6,56,256]{3,2,1,0:T(8,128)(2,1)}, bf16[2,6,56,256]{3,2,1,0:T(8,128)(2,1)}, u32[]{:S(2)}, u32[]{:S(2)}) collective-permute-start(bf16[2,6,56,256]{3,2,1,0:T(8,128)(2,1)} %get-tuple-element.59), channel_id=1, source_target_pairs={{0,2},{2,4},{4,6},{6,0},{8,10},{10,12},{12,14},{14,8},{16,18},{18,... | collective-permute-start | bytes 1032200 | tf_op jit(solution)/shard_map/ppermute | solution.py:306
  51.9 27.2 %collective-permute-start.16 = (bf16[2,6,56,256]{3,2,1,0:T(8,128)(2,1)}, bf16[2,6,56,256]{3,2,1,0:T(8,128)(2,1)}, u32[]{:S(2)}, u32[]{:S(2)}) collective-permute-start(bf16[2,6,56,256]{3,2,1,0:T(8,128)(2,1)} %get-tuple-element.60), channel_id=1, source_target_pairs={{0,4},{2,6},{4,0},{6,2},{8,12},{10,14},{12,8},{14,10},{16,20},{18,... | collective-permute-start | bytes 1032200 | tf_op jit(solution)/shard_map/ppermute | solution.py:306
  51.9 27.2 %collective-permute-start.17 = (bf16[2,6,56,256]{3,2,1,0:T(8,128)(2,1)}, bf16[2,6,56,256]{3,2,1,0:T(8,128)(2,1)}, u32[]{:S(2)}, u32[]{:S(2)}) collective-permute-start(bf16[2,6,56,256]{3,2,1,0:T(8,128)(2,1)} %get-tuple-element.55), channel_id=1, source_target_pairs={{0,6},{2,0},{4,2},{6,4},{8,14},{10,8},{12,10},{14,12},{16,22},{18,... | collective-permute-start | bytes 1032200 | tf_op jit(solution)/shard_map/ppermute | solution.py:306
  52.6 19.3 %collective-permute-start.9 = (bf16[3,80,128]{2,1,0:T(8,128)(2,1)S(1)}, bf16[3,80,128]{2,1,0:T(8,128)(2,1)S(1)}, u32[]{:S(2)}, u32[]{:S(2)}) collective-permute-start(bf16[3,80,128]{2,1,0:T(8,128)(2,1)S(1)} %get-tuple-element.41), channel_id=1, source_target_pairs={{0,2},{2,4},{4,6},{8,10},{10,12},{12,14},{16,18},{18,20},{20,22},{... | collective-permute-start | bytes 184328 | tf_op jit(solution)/shard_map/ppermute | solution.py:306
  58.3 6.9 %collective-permute-start.10 = (bf16[2,80,128]{2,1,0:T(8,128)(2,1)S(1)}, bf16[2,80,128]{2,1,0:T(8,128)(2,1)S(1)}, u32[]{:S(2)}, u32[]{:S(2)}) collective-permute-start(bf16[2,80,128]{2,1,0:T(8,128)(2,1)S(1)} %get-tuple-element.42), channel_id=1, source_target_pairs={{2,0},{4,2},{6,4},{10,8},{12,10},{14,12},{18,16},{20,18},{22,20},{... | collective-permute-start | bytes 122888 | tf_op jit(solution)/shard_map/ppermute | solution.py:306
  65.2 23.5 %collective-permute-start.3 = (bf16[2,3,56,256]{3,2,1,0:T(8,128)(2,1)S(1)}, bf16[2,3,56,256]{3,2,1,0:T(8,128)(2,1)S(1)}, u32[]{:S(2)}, u32[]{:S(2)}) collective-permute-start(bf16[2,3,56,256]{3,2,1,0:T(8,128)(2,1)S(1)} %get-tuple-element.35), channel_id=1, source_target_pairs={{0,8},{2,10},{4,12},{6,14},{8,16},{10,18},{12,20},{14,22},{16,24},... | collective-permute-start | bytes 516104 | tf_op jit(solution)/shard_map/ppermute | solution.py:306
  71.9 16.8 %collective-permute-start.4 = (bf16[2,2,56,256]{3,2,1,0:T(8,128)(2,1)S(1)}, bf16[2,2,56,256]{3,2,1,0:T(8,128)(2,1)S(1)}, u32[]{:S(2)}, u32[]{:S(2)}) collective-permute-start(bf16[2,2,56,256]{3,2,1,0:T(8,128)(2,1)S(1)} %get-tuple-element.36), channel_id=1, source_target_pairs={{8,0},{10,2},{12,4},{14,6},{16,8},{18,10},{20,12},{22,14},{24,16},... | collective-permute-start | bytes 344072 | tf_op jit(solution)/shard_map/ppermute | solution.py:306
  81.0 23.4 %collective-permute-start.18 = (bf16[2,3,56,256]{3,2,1,0:T(8,128)(2,1)S(1)}, bf16[2,3,56,256]{3,2,1,0:T(8,128)(2,1)S(1)}, u32[]{:S(2)}, u32[]{:S(2)}) collective-permute-start(bf16[2,3,56,256]{3,2,1,0:T(8,128)(2,1)S(1)} %get-tuple-element.49), channel_id=1, source_target_pairs={{0,8},{2,10},{4,12},{6,14},{8,16},{10,18},{12,20},{14,22},{16,24},... | collective-permute-start | bytes 516104 | tf_op jit(solution)/shard_map/ppermute | solution.py:306
  85.8 18.6 %collective-permute-start.19 = (bf16[2,2,56,256]{3,2,1,0:T(8,128)(2,1)S(1)}, bf16[2,2,56,256]{3,2,1,0:T(8,128)(2,1)S(1)}, u32[]{:S(2)}, u32[]{:S(2)}) collective-permute-start(bf16[2,2,56,256]{3,2,1,0:T(8,128)(2,1)S(1)} %get-tuple-element.50), channel_id=1, source_target_pairs={{8,0},{10,2},{12,4},{14,6},{16,8},{18,10},{20,12},{22,14},{24,16},... | collective-permute-start | bytes 344072 | tf_op jit(solution)/shard_map/ppermute | solution.py:306
  96.9 50.2 %collective-permute-start.13 = (bf16[1,13,2,24,128]{4,3,2,1,0:T(8,128)(2,1)S(1)}, bf16[1,13,2,24,128]{4,3,2,1,0:T(8,128)(2,1)S(1)}, u32[]{:S(2)}, u32[]{:S(2)}) collective-permute-start(bf16[1,13,2,24,128]{4,3,2,1,0:T(8,128)(2,1)S(1)} %get-tuple-element.47), channel_id=1, source_target_pairs={{0,0},{2,4},{4,8},{6,12},{8,2},{10,6},{12,10},{14,14},{16,16},{18,... | collective-permute-start | bytes 479240 | tf_op jit(solution)/shard_map/ppermute | solution.py:306
  97.6 49.5 %collective-permute-start.14 = (bf16[1,13,2,24,128]{4,3,2,1,0:T(8,128)(2,1)S(1)}, bf16[1,13,2,24,128]{4,3,2,1,0:T(8,128)(2,1)S(1)}, u32[]{:S(2)}, u32[]{:S(2)}) collective-permute-start(bf16[1,13,2,24,128]{4,3,2,1,0:T(8,128)(2,1)S(1)} %get-tuple-element.48), channel_id=1, source_target_pairs={{0,2},{2,6},{4,10},{6,14},{8,0},{10,4},{12,8},{14,12},{16,18},{18,... | collective-permute-start | bytes 479240 | tf_op jit(solution)/shard_map/ppermute | solution.py:306
  112.7 14.0 %collective-permute-start.20 = (bf16[1,13,2,24,128]{4,3,2,1,0:T(8,128)(2,1)S(1)}, bf16[1,13,2,24,128]{4,3,2,1,0:T(8,128)(2,1)S(1)}, u32[]{:S(2)}, u32[]{:S(2)}) collective-permute-start(bf16[1,13,2,24,128]{4,3,2,1,0:T(8,128)(2,1)S(1)} %get-tuple-element.51), channel_id=1, source_target_pairs={{0,0},{2,4},{4,8},{6,12},{8,2},{10,6},{12,10},{14,14},{16,16},{18,... | collective-permute-start | bytes 479240 | tf_op jit(solution)/shard_map/ppermute | solution.py:306
  113.3 32.2 %collective-permute-start.21 = (bf16[1,13,2,24,128]{4,3,2,1,0:T(8,128)(2,1)S(1)}, bf16[1,13,2,24,128]{4,3,2,1,0:T(8,128)(2,1)S(1)}, u32[]{:S(2)}, u32[]{:S(2)}) collective-permute-start(bf16[1,13,2,24,128]{4,3,2,1,0:T(8,128)(2,1)S(1)} %get-tuple-element.52), channel_id=1, source_target_pairs={{0,2},{2,6},{4,10},{6,14},{8,0},{10,4},{12,8},{14,12},{16,18},{18,... | collective-permute-start | bytes 479240 | tf_op jit(solution)/shard_map/ppermute | solution.py:306
  125.9 13.2 %collective-permute-start.22 = (bf16[1,13,2,24,128]{4,3,2,1,0:T(8,128)(2,1)S(1)}, bf16[1,13,2,24,128]{4,3,2,1,0:T(8,128)(2,1)S(1)}, u32[]{:S(2)}, u32[]{:S(2)}) collective-permute-start(bf16[1,13,2,24,128]{4,3,2,1,0:T(8,128)(2,1)S(1)} %get-tuple-element.53), channel_id=1, source_target_pairs={{0,0},{2,4},{4,8},{6,12},{8,2},{10,6},{12,10},{14,14},{16,16},{18,... | collective-permute-start | bytes 479240 | tf_op jit(solution)/shard_map/ppermute | solution.py:306
  126.7 13.1 %collective-permute-start.23 = (bf16[1,13,2,24,128]{4,3,2,1,0:T(8,128)(2,1)S(1)}, bf16[1,13,2,24,128]{4,3,2,1,0:T(8,128)(2,1)S(1)}, u32[]{:S(2)}, u32[]{:S(2)}) collective-permute-start(bf16[1,13,2,24,128]{4,3,2,1,0:T(8,128)(2,1)S(1)} %get-tuple-element.54), channel_id=1, source_target_pairs={{0,2},{2,6},{4,10},{6,14},{8,0},{10,4},{12,8},{14,12},{16,18},{18,... | collective-permute-start | bytes 479240 | tf_op jit(solution)/shard_map/ppermute | solution.py:306
  139.1 9.5 %collective-permute-start.11 = (bf16[1,13,2,24,128]{4,3,2,1,0:T(8,128)(2,1)S(1)}, bf16[1,13,2,24,128]{4,3,2,1,0:T(8,128)(2,1)S(1)}, u32[]{:S(2)}, u32[]{:S(2)}) collective-permute-start(bf16[1,13,2,24,128]{4,3,2,1,0:T(8,128)(2,1)S(1)} %get-tuple-element.45), channel_id=1, source_target_pairs={{0,0},{2,4},{4,8},{6,12},{8,2},{10,6},{12,10},{14,14},{16,16},{18,... | collective-permute-start | bytes 479240 | tf_op jit(solution)/shard_map/ppermute | solution.py:306
  139.8 11.4 %collective-permute-start.12 = (bf16[1,13,2,24,128]{4,3,2,1,0:T(8,128)(2,1)S(1)}, bf16[1,13,2,24,128]{4,3,2,1,0:T(8,128)(2,1)S(1)}, u32[]{:S(2)}, u32[]{:S(2)}) collective-permute-start(bf16[1,13,2,24,128]{4,3,2,1,0:T(8,128)(2,1)S(1)} %get-tuple-element.46), channel_id=1, source_target_pairs={{0,2},{2,6},{4,10},{6,14},{8,0},{10,4},{12,8},{14,12},{16,18},{18,... | collective-permute-start | bytes 479240 | tf_op jit(solution)/shard_map/ppermute | solution.py:306
  (9 other events, 167.5 us)
where the time goes:
time: 153 us
  starting transfers between devices  56.9 us (37%)
  Pallas kernels  50.5 us (33%)
  waiting for transfers between devices  39.1 us (26%)
  local copies, waits for them, and re-layouts  5.71 us (4%)
    ppermute x24, starting transfers between devices, send(): return lax.ppermute(x, AXES, pairs)  56.9 us
    ppermute x24, waiting for transfers between devices, send(): return lax.ppermute(x, AXES, pairs)  39.1 us
    pallas_call x4, Pallas kernels, local(): pl.pallas_call(lambda *refs: conv_kernel(*refs, parts=members, sh=sh, tr=...  32.8 us
    pallas_call x4, Pallas kernels, local(): pl.pallas_call(lambda *refs: encode_kernel(*refs, parts=HALVES, half_rows...  6.15 us
    pallas_call x1, Pallas kernels, local(): pl.pallas_call(lambda *refs: camera_unpack_kernel(*refs, groups=groups, s...  4.82 us
    dynamic_slice x1, local copies, waits for them, and re-layouts, local(): lax.dynamic_slice(padded, (f0, 0, (member + d) % members * tw, 0), (step,...  4.46 us
    pallas_call x3, Pallas kernels, pick(): pl.pallas_call(pick_kernel, grid_spec=pltpu.PrefetchScalarGridSpec(num_sc...  4.34 us
  transfers between devices with their start and end apart: 24, of which 5 were waited for; matrix products, arithmetic and copies ran while one was open for 3% of the time, Pallas kernels for 31%

commit v1 on v0

--- a/solution.py
+++ b/solution.py
@@ -145,7 +145,7 @@
     above, below, camera, w1, b1, w2, b2 = refs[parts : parts + 7]
     outs = refs[parts + 7 : parts + 7 + HALVES]
     tile, taps, mid, cells = refs[parts + 7 + HALVES :]
-    group, member, half_id = pos[0], pos[1], pos[2]
+    group, member, half_id, column = pos[0], pos[1], pos[2], pos[3]
     wide = windows[0].shape[2]
     lidar = windows[0].shape[3]
     joined = w1.shape[1]
@@ -177,7 +177,7 @@
 
     n1 = 4
     m1 = n1 * pitch
-    col0 = member * (wide - 2 * SIDE) - SIDE
+    col0 = column * (wide - 2 * SIDE) - SIDE
 
     def first(i, _):
         r = i * n1
@@ -285,6 +285,9 @@
     members = n_cols // HALVES
     groups = n_rows * HALVES
     total = n_rows * n_cols
+    half = members // 2
+    tile_of = [2 * m if m < half else 2 * (members - 1 - m) + 1 for m in range(members)]
+    holder = [tile_of.index(j) for j in range(members)]
 
     def local(lidar, camera, joined_weight, joined_bias, block_weight, block_bias, down_weight, down_bias, proj_weight, proj_bias):
         frames, sh, cols, lidar_ch = lidar.shape
@@ -305,13 +308,16 @@
         def send(x, pairs):
             return lax.ppermute(x, AXES, pairs)
 
-        def across(x, by_group, by_member):
+        def across(x, by_group, by_column):
             pairs = []
             for g in range(groups):
                 for j in range(members):
-                    if 0 <= g + by_group < groups and 0 <= j + by_member < members:
-                        pairs.append((g * members + j, (g + by_group) * members + j + by_member))
+                    if 0 <= g + by_group < groups and 0 <= j + by_column < members:
+                        pairs.append((g * members + holder[j], (g + by_group) * members + holder[j + by_column]))
             return send(x, pairs)
+
+        def column_of(m):
+            return jnp.where(m < half, 2 * m, 2 * (members - 1 - m) + 1)
 
         joint = joined_weight.reshape(-1, joined)
         square = block_weight.reshape(-1, block)
@@ -349,7 +355,7 @@
         )(place.reshape(1).astype(jnp.int32), turned)
         lidar, packed = lax.optimization_barrier((lidar, packed))
         arrived = [
-            send(packed[p], [(s, ((s + p) % groups) * members + s // groups) for s in range(total)])
+            send(packed[p], [(s, ((s + p) % groups) * members + holder[s // groups]) for s in range(total)])
             for p in range(groups)
         ]
         tail, head = pick(arrived, (group + 1) % groups, group, 0)
@@ -374,7 +380,7 @@
         cam = cam.reshape(frames, span, pitch, -1)
 
         padded = jnp.pad(lidar, ((0, 0), (0, 0), (SIDE, SIDE), (0, 0)))
-        pos = jnp.stack([group, member, kgroup]).astype(jnp.int32)
+        pos = jnp.stack([group, member, kgroup, column_of(member)]).astype(jnp.int32)
         pairs2 = (tr + 2) // 2
         half_rows = tr // 2
         n = HALVES * half_rows
@@ -386,7 +392,7 @@
         for f0 in range(0, frames, step):
             windows = []
             for d in range(members):
-                x = lax.dynamic_slice(padded, (f0, 0, ((member + d) % members) * tw, 0), (step, sh, wide, lidar_ch))
+                x = lax.dynamic_slice(padded, (f0, 0, column_of((member + d) % members) * tw, 0), (step, sh, wide, lidar_ch))
                 if d:
                     x = send(x, [(g * members + j, g * members + (j + d) % members) for g in range(groups) for j in range(members)])
                 windows.append(x)
@@ -413,15 +419,14 @@
                     out_shape=[blocks] * HALVES,
                     compiler_params=limit(28),
                     cost_estimate=pl.CostEstimate(flops=flops, bytes_accessed=2 * 10**6 * RUN, transcendentals=0),
-                    name="convs",
                 )(pos, *windows, above, below, cam, w1, b1, w2, b2)
                 pieces = []
                 for h in range(HALVES):
                     pairs = []
                     for s in range(total):
                         r, c = divmod(s, n_cols)
-                        k, j = divmod(c, members)
-                        pairs.append((s, r * n_cols + HALVES * j + (k + h) % HALVES))
+                        k, m = divmod(c, members)
+                        pairs.append((s, r * n_cols + HALVES * tile_of[m] + (k + h) % HALVES))
                     pieces.append(send(tiles[h], pairs))
                 old = [] if encoded is None else [encoded]
                 encoded = pl.pallas_call(
@@ -440,7 +445,6 @@
                     input_output_aliases={5 + HALVES: 0} if old else {},
                     compiler_params=limit(12),
                     cost_estimate=pl.CostEstimate(flops=2 * RUN * n * jd * w3.shape[0] * 256, bytes_accessed=10**6 * RUN, transcendentals=0),
-                    name="encode",
                 )(cindex.reshape(1).astype(jnp.int32), *pieces, w3, b3, proj_weight, bp, *old)
         return encoded.reshape(frames, 2 * n, w, 2 * block)
 

time: 153 us -> 147 us (0.961)
  the two profiles are of different devices: /device:TPU:2 before, /device:TPU:0 now
where the time goes in v1:
time: 147 us; the launch traced here: 144 us
  starting transfers between devices  75.6 us (51%)
  Pallas kernels  50.5 us (34%)
  waiting for transfers between devices  11.6 us (8%)
  local copies, waits for them, and re-layouts  5.74 us (4%)
    ppermute x24, starting transfers between devices, send(): return lax.ppermute(x, AXES, pairs)  75.6 us
    pallas_call x4, Pallas kernels, local(): pl.pallas_call(lambda *refs: conv_kernel(*refs, parts=members, sh=sh, tr=...  32.8 us
    ppermute x24, waiting for transfers between devices, send(): return lax.ppermute(x, AXES, pairs)  11.6 us
    pallas_call x4, Pallas kernels, local(): pl.pallas_call(lambda *refs: encode_kernel(*refs, parts=HALVES, half_rows...  6.15 us
    pallas_call x1, Pallas kernels, local(): pl.pallas_call(lambda *refs: camera_unpack_kernel(*refs, groups=groups, s...  4.82 us
    dynamic_slice x1, local copies, waits for them, and re-layouts, local(): lax.dynamic_slice(padded, (f0, 0, column_of((member + d) % members) * tw,...  4.5 us
    pallas_call x3, Pallas kernels, pick(): pl.pallas_call(pick_kernel, grid_spec=pltpu.PrefetchScalarGridSpec(num_sc...  4.34 us
  transfers between devices with their start and end apart: 24, of which 3 were waited for; matrix products, arithmetic and copies ran while one was open for 3% of the time, Pallas kernels for 33%

profile of v1, /device:TPU:0, one launch (start us, length us, event | category | flops | bytes accessed | tf_op | source)
XLA Modules:
  0.0 144.1 jit_solution(8434262986332393277)
XLA Ops:
  1.2 2.0 %camera_pack.1 = (bf16[12,80,128]{2,1,0:T(8,128)(2,1)}, bf16[12,80,128]{2,1,0:T(8,128)(2,1)}, bf16[12,80,128]{2,1,0:T(8,128)(2,1)}, bf16[12,80,128]{2,1,0:T(8,128)(2,1)S(1)}) custom-call(s32[1]{0:T(128)} %bitcast.5.refs_0_, bf16[4,12,80,96]{3,2,1,0:T(8,128)(2,1)S(1)} %bitcast.27), custom_call_target="tpu_custom_call" | custom-call | tf_op jit(solution)/shard_map/camera_pack/pallas_call | solution.py:344
  4.8 7.7 %collective-permute-start.6 = (bf16[12,80,128]{2,1,0:T(8,128)(2,1)}, bf16[12,80,128]{2,1,0:T(8,128)(2,1)S(1)}, u32[]{:S(2)}, u32[]{:S(2)}) collective-permute-start(bf16[12,80,128]{2,1,0:T(8,128)(2,1)} %get-tuple-element.38), channel_id=1, source_target_pairs={{0,8},{2,16},{4,24},{6,0},{8,14},{10,22},{12,30},{14,6},{16,10},{1... | collective-permute-start | bytes 737288 | tf_op jit(solution)/shard_map/ppermute | solution.py:309
  12.6 4.5 %pad_dynamic-slice_fusion = (bf16[2,6,56,256]{3,2,1,0:T(8,128)(2,1)}, bf16[2,6,56,256]{3,2,1,0:T(8,128)(2,1)}, bf16[2,6,56,256]{3,2,1,0:T(8,128)(2,1)}, bf16[2,6...) fusion(s32[]{:T(128)S(6)} %select_n.96, ...), kind=kLoop, calls=%fused_computation | loop fusion | bytes 5111824 | tf_op jit(solution)/shard_map/dynamic_slice | solution.py:395
  17.6 4.2 %collective-permute-start.7 = (bf16[12,80,128]{2,1,0:T(8,128)(2,1)}, bf16[12,80,128]{2,1,0:T(8,128)(2,1)S(1)}, u32[]{:S(2)}, u32[]{:S(2)}) collective-permute-start(bf16[12,80,128]{2,1,0:T(8,128)(2,1)} %get-tuple-element.39), channel_id=1, source_target_pairs={{0,16},{2,24},{4,0},{6,8},{8,22},{10,30},{12,6},{14,14},{16,18},{1... | collective-permute-start | bytes 737288 | tf_op jit(solution)/shard_map/ppermute | solution.py:309
  21.8 1.9 %collective-permute-start.8 = (bf16[12,80,128]{2,1,0:T(8,128)(2,1)S(1)}, bf16[12,80,128]{2,1,0:T(8,128)(2,1)S(1)}, u32[]{:S(2)}, u32[]{:S(2)}) collective-permute-start(bf16[12,80,128]{2,1,0:T(8,128)(2,1)S(1)} %get-tuple-element.40), channel_id=1, source_target_pairs={{0,24},{2,0},{4,8},{6,16},{8,30},{10,6},{12,14},{14,22},{16,26},{1... | collective-permute-start | bytes 737288 | tf_op jit(solution)/shard_map/ppermute | solution.py:309
  23.7 2.4 %collective-permute-start.1 = (bf16[2,6,56,256]{3,2,1,0:T(8,128)(2,1)}, bf16[2,6,56,256]{3,2,1,0:T(8,128)(2,1)}, u32[]{:S(2)}, u32[]{:S(2)}) collective-permute-start(bf16[2,6,56,256]{3,2,1,0:T(8,128)(2,1)} %get-tuple-element.57), channel_id=1, source_target_pairs={{0,4},{2,6},{4,0},{6,2},{8,12},{10,14},{12,8},{14,10},{16,20},{18,... | collective-permute-start | bytes 1032200 | tf_op jit(solution)/shard_map/ppermute | solution.py:309
  26.1 1.7 %collective-permute-done.7.refs_2_.refs_6_.refs_3_ = bf16[12,80,128]{2,1,0:T(8,128)(2,1)S(1)} collective-permute-done((bf16[12,80,128]{2,1,0:T(8,128)(2,1)}, bf16[12,80,128]{2,1,0:T(8,128)(2,1)S(1)}, u32[]{:S(2)}, u32[]{:S(2)}) %collective-permute-start.7) | collective-permute-done | bytes 245792 | tf_op jit(solution)/shard_map/ppermute | solution.py:309
  27.8 6.5 %collective-permute-start.15 = (bf16[2,6,56,256]{3,2,1,0:T(8,128)(2,1)}, bf16[2,6,56,256]{3,2,1,0:T(8,128)(2,1)}, u32[]{:S(2)}, u32[]{:S(2)}) collective-permute-start(bf16[2,6,56,256]{3,2,1,0:T(8,128)(2,1)} %get-tuple-element.59), channel_id=1, source_target_pairs={{0,2},{2,4},{4,6},{6,0},{8,10},{10,12},{12,14},{14,8},{16,18},{18,... | collective-permute-start | bytes 1032200 | tf_op jit(solution)/shard_map/ppermute | solution.py:309
  34.3 3.5 %collective-permute-start.16 = (bf16[2,6,56,256]{3,2,1,0:T(8,128)(2,1)}, bf16[2,6,56,256]{3,2,1,0:T(8,128)(2,1)}, u32[]{:S(2)}, u32[]{:S(2)}) collective-permute-start(bf16[2,6,56,256]{3,2,1,0:T(8,128)(2,1)} %get-tuple-element.60), channel_id=1, source_target_pairs={{0,4},{2,6},{4,0},{6,2},{8,12},{10,14},{12,8},{14,10},{16,20},{18,... | collective-permute-start | bytes 1032200 | tf_op jit(solution)/shard_map/ppermute | solution.py:309
  38.5 7.0 %collective-permute-start.9 = (bf16[3,80,128]{2,1,0:T(8,128)(2,1)S(1)}, bf16[3,80,128]{2,1,0:T(8,128)(2,1)S(1)}, u32[]{:S(2)}, u32[]{:S(2)}) collective-permute-start(bf16[3,80,128]{2,1,0:T(8,128)(2,1)S(1)} %get-tuple-element.41), channel_id=1, source_target_pairs={{0,6},{6,2},{2,4},{8,14},{14,10},{10,12},{16,22},{22,18},{18,20},{... | collective-permute-start | bytes 184328 | tf_op jit(solution)/shard_map/ppermute | solution.py:309
  46.8 1.9 %shard_map.100 = (bf16[2,3,56,256]{3,2,1,0:T(8,128)(2,1)S(1)}, bf16[2,2,56,256]{3,2,1,0:T(8,128)(2,1)S(1)}) custom-call(s32[2]{0:T(128)S(1)} %pad_add_fusion.1.pos, bf16[2,6,56,256]{3,2,1,0:T(8,128)(2,1)S(1)} %get-tuple-element.61.refs_0_.refs_4_.refs_1_, bf16[2,6,56,256]{3,2,1,0:T(8,128)(2,1)} %collective-permute-done.refs_1_.refs_5_.refs_2_, ...), custom_call_target="tpu_custom_call" | custom-call | tf_op jit(solution)/shard_map/pallas_call | solution.py:135
  48.7 8.9 %collective-permute-done.10.refs_6_ = bf16[2,80,128]{2,1,0:T(8,128)(2,1)S(1)} collective-permute-done((bf16[2,80,128]{2,1,0:T(8,128)(2,1)S(1)}, bf16[2,80,128]{2,1,0:T(8,128)(2,1)S(1)}, u32[]{:S(2)}, u32[]{:S(2)}) %collective-permute-start.10) | collective-permute-done | bytes 40992 | tf_op jit(solution)/shard_map/ppermute | solution.py:309
  57.6 6.6 %collective-permute-start.3 = (bf16[2,3,56,256]{3,2,1,0:T(8,128)(2,1)S(1)}, bf16[2,3,56,256]{3,2,1,0:T(8,128)(2,1)S(1)}, u32[]{:S(2)}, u32[]{:S(2)}) collective-permute-start(bf16[2,3,56,256]{3,2,1,0:T(8,128)(2,1)S(1)} %get-tuple-element.35), channel_id=1, source_target_pairs={{0,8},{6,14},{2,10},{4,12},{8,16},{14,22},{10,18},{12,20},{16,24},... | collective-permute-start | bytes 516104 | tf_op jit(solution)/shard_map/ppermute | solution.py:309
  66.0 4.8 %camera_unpack.1 = bf16[128,64,256]{2,1,0:T(8,128)(2,1)S(1)} custom-call(s32[1]{0:T(128)} %bitcast.1.refs_0_, bf16[12,80,128]{2,1,0:T(8,128)(2,1)S(1)} %collective-permute-done.5.refs_0_.refs_4_.refs_1_, bf16[12,80,128]{2,1,0:T(8,128)(2,1)S(1)} %collective-permute-done.6.refs_1_.refs_5_.refs_2_, ...), custom_call_target="tpu_custom_call" | custom-call | tf_op jit(solution)/shard_map/camera_unpack/pallas_call | solution.py:364
  70.9 1.9 %shard_map.104 = (bf16[2,3,56,256]{3,2,1,0:T(8,128)(2,1)S(1)}, bf16[2,2,56,256]{3,2,1,0:T(8,128)(2,1)S(1)}) custom-call(s32[2]{0:T(128)S(1)} %pad_add_fusion.1.pos, bf16[2,6,56,256]{3,2,1,0:T(8,128)(2,1)S(1)} %get-tuple-element.58.refs_0_.refs_4_.refs_1_, bf16[2,6,56,256]{3,2,1,0:T(8,128)(2,1)} %collective-permute-done.15.refs_1_.refs_5_.refs_2_, ...), custom_call_target="tpu_custom_call" | custom-call | tf_op jit(solution)/shard_map/pallas_call | solution.py:135
  72.7 5.5 %collective-permute-start.18 = (bf16[2,3,56,256]{3,2,1,0:T(8,128)(2,1)S(1)}, bf16[2,3,56,256]{3,2,1,0:T(8,128)(2,1)S(1)}, u32[]{:S(2)}, u32[]{:S(2)}) collective-permute-start(bf16[2,3,56,256]{3,2,1,0:T(8,128)(2,1)S(1)} %get-tuple-element.49), channel_id=1, source_target_pairs={{0,8},{6,14},{2,10},{4,12},{8,16},{14,22},{10,18},{12,20},{16,24},... | collective-permute-start | bytes 516104 | tf_op jit(solution)/shard_map/ppermute | solution.py:309
  79.5 8.2 %shard_map.103 = (bf16[1,13,2,24,128]{4,3,2,1,0:T(8,128)(2,1)S(1)}, bf16[1,13,2,24,128]{4,3,2,1,0:T(8,128)(2,1)S(1)}) custom-call(s32[4]{0:T(128)S(1)} %pad_add_fusion.refs_0_, bf16[2,6,56,256]{3,2,1,0:T(8,128)(2,1)S(1)} %get-tuple-element.61.refs_0_.refs_4_.refs_1_, bf16[2,6,56,256]{3,2,1,0:T(8,128)(2,1)} %collective-permute-done.refs_1_.refs_5_.refs_2_, ...), custom_call_target="tpu_custom_call" | custom-call | flops 4127195136 | bytes 2000000 | tf_op jit(solution)/shard_map/pallas_call | solution.py:405
  88.4 8.2 %collective-permute-start.14 = (bf16[1,13,2,24,128]{4,3,2,1,0:T(8,128)(2,1)S(1)}, bf16[1,13,2,24,128]{4,3,2,1,0:T(8,128)(2,1)S(1)}, u32[]{:S(2)}, u32[]{:S(2)}) collective-permute-start(bf16[1,13,2,24,128]{4,3,2,1,0:T(8,128)(2,1)S(1)} %get-tuple-element.48), channel_id=1, source_target_pairs={{0,2},{2,10},{4,14},{6,6},{8,0},{10,8},{12,12},{14,4},{16,18},{18,... | collective-permute-start | bytes 479240 | tf_op jit(solution)/shard_map/ppermute | solution.py:309
  96.6 8.2 %shard_map.105 = (bf16[1,13,2,24,128]{4,3,2,1,0:T(8,128)(2,1)S(1)}, bf16[1,13,2,24,128]{4,3,2,1,0:T(8,128)(2,1)S(1)}) custom-call(s32[4]{0:T(128)S(1)} %pad_add_fusion.refs_0_, bf16[2,6,56,256]{3,2,1,0:T(8,128)(2,1)S(1)} %get-tuple-element.58.refs_0_.refs_4_.refs_1_, bf16[2,6,56,256]{3,2,1,0:T(8,128)(2,1)} %collective-permute-done.15.refs_1_.refs_5_.refs_2_, ...), custom_call_target="tpu_custom_call" | custom-call | flops 4127195136 | bytes 2000000 | tf_op jit(solution)/shard_map/pallas_call | solution.py:405
  105.5 3.4 %collective-permute-start.21 = (bf16[1,13,2,24,128]{4,3,2,1,0:T(8,128)(2,1)S(1)}, bf16[1,13,2,24,128]{4,3,2,1,0:T(8,128)(2,1)S(1)}, u32[]{:S(2)}, u32[]{:S(2)}) collective-permute-start(bf16[1,13,2,24,128]{4,3,2,1,0:T(8,128)(2,1)S(1)} %get-tuple-element.52), channel_id=1, source_target_pairs={{0,2},{2,10},{4,14},{6,6},{8,0},{10,8},{12,12},{14,4},{16,18},{18,... | collective-permute-start | bytes 479240 | tf_op jit(solution)/shard_map/ppermute | solution.py:309
  108.9 8.2 %shard_map.106 = (bf16[1,13,2,24,128]{4,3,2,1,0:T(8,128)(2,1)S(1)}, bf16[1,13,2,24,128]{4,3,2,1,0:T(8,128)(2,1)S(1)}) custom-call(s32[4]{0:T(128)S(1)} %pad_add_fusion.refs_0_, bf16[2,6,56,256]{3,2,1,0:T(8,128)(2,1)S(1)} %get-tuple-element.58.refs_0_.refs_4_.refs_1_, bf16[2,6,56,256]{3,2,1,0:T(8,128)(2,1)} %collective-permute-done.15.refs_1_.refs_5_.refs_2_, ...), custom_call_target="tpu_custom_call" | custom-call | flops 4127195136 | bytes 2000000 | tf_op jit(solution)/shard_map/pallas_call | solution.py:405
  117.8 7.1 %collective-permute-start.23 = (bf16[1,13,2,24,128]{4,3,2,1,0:T(8,128)(2,1)S(1)}, bf16[1,13,2,24,128]{4,3,2,1,0:T(8,128)(2,1)S(1)}, u32[]{:S(2)}, u32[]{:S(2)}) collective-permute-start(bf16[1,13,2,24,128]{4,3,2,1,0:T(8,128)(2,1)S(1)} %get-tuple-element.54), channel_id=1, source_target_pairs={{0,2},{2,10},{4,14},{6,6},{8,0},{10,8},{12,12},{14,4},{16,18},{18,... | collective-permute-start | bytes 479240 | tf_op jit(solution)/shard_map/ppermute | solution.py:309
  124.9 8.2 %shard_map.102 = (bf16[1,13,2,24,128]{4,3,2,1,0:T(8,128)(2,1)S(1)}, bf16[1,13,2,24,128]{4,3,2,1,0:T(8,128)(2,1)S(1)}) custom-call(s32[4]{0:T(128)S(1)} %pad_add_fusion.refs_0_, bf16[2,6,56,256]{3,2,1,0:T(8,128)(2,1)S(1)} %get-tuple-element.61.refs_0_.refs_4_.refs_1_, bf16[2,6,56,256]{3,2,1,0:T(8,128)(2,1)} %collective-permute-done.refs_1_.refs_5_.refs_2_, ...), custom_call_target="tpu_custom_call" | custom-call | flops 4127195136 | bytes 2000000 | tf_op jit(solution)/shard_map/pallas_call | solution.py:405
  133.8 3.2 %collective-permute-start.12 = (bf16[1,13,2,24,128]{4,3,2,1,0:T(8,128)(2,1)S(1)}, bf16[1,13,2,24,128]{4,3,2,1,0:T(8,128)(2,1)S(1)}, u32[]{:S(2)}, u32[]{:S(2)}) collective-permute-start(bf16[1,13,2,24,128]{4,3,2,1,0:T(8,128)(2,1)S(1)} %get-tuple-element.46), channel_id=1, source_target_pairs={{0,2},{2,10},{4,14},{6,6},{8,0},{10,8},{12,12},{14,4},{16,18},{18,... | collective-permute-start | bytes 479240 | tf_op jit(solution)/shard_map/ppermute | solution.py:309
  (61 shorter events, 18.2 us)
Async XLA Ops:
  3.2 20.4 %collective-permute-start.5 = (bf16[12,80,128]{2,1,0:T(8,128)(2,1)}, bf16[12,80,128]{2,1,0:T(8,128)(2,1)S(1)}, u32[]{:S(2)}, u32[]{:S(2)}) collective-permute-start(bf16[12,80,128]{2,1,0:T(8,128)(2,1)} %get-tuple-element.37), channel_id=1, source_target_pairs={{0,0},{2,8},{4,16},{6,24},{8,6},{10,14},{12,22},{14,30},{16,2},{18... | collective-permute-start | bytes 737288 | tf_op jit(solution)/shard_map/ppermute | solution.py:309
  4.8 21.3 %collective-permute-start.6 = (bf16[12,80,128]{2,1,0:T(8,128)(2,1)}, bf16[12,80,128]{2,1,0:T(8,128)(2,1)S(1)}, u32[]{:S(2)}, u32[]{:S(2)}) collective-permute-start(bf16[12,80,128]{2,1,0:T(8,128)(2,1)} %get-tuple-element.38), channel_id=1, source_target_pairs={{0,8},{2,16},{4,24},{6,0},{8,14},{10,22},{12,30},{14,6},{16,10},{1... | collective-permute-start | bytes 737288 | tf_op jit(solution)/shard_map/ppermute | solution.py:309
  17.1 20.6 %collective-permute-start = (bf16[2,6,56,256]{3,2,1,0:T(8,128)(2,1)}, bf16[2,6,56,256]{3,2,1,0:T(8,128)(2,1)}, u32[]{:S(2)}, u32[]{:S(2)}) collective-permute-start(bf16[2,6,56,256]{3,2,1,0:T(8,128)(2,1)} %get-tuple-element.56), channel_id=1, source_target_pairs={{0,2},{2,4},{4,6},{6,0},{8,10},{10,12},{12,14},{14,8},{16,18},{18,... | collective-permute-start | bytes 1032200 | tf_op jit(solution)/shard_map/ppermute | solution.py:309
  17.6 10.2 %collective-permute-start.7 = (bf16[12,80,128]{2,1,0:T(8,128)(2,1)}, bf16[12,80,128]{2,1,0:T(8,128)(2,1)S(1)}, u32[]{:S(2)}, u32[]{:S(2)}) collective-permute-start(bf16[12,80,128]{2,1,0:T(8,128)(2,1)} %get-tuple-element.39), channel_id=1, source_target_pairs={{0,16},{2,24},{4,0},{6,8},{8,22},{10,30},{12,6},{14,14},{16,18},{1... | collective-permute-start | bytes 737288 | tf_op jit(solution)/shard_map/ppermute | solution.py:309
  21.8 12.5 %collective-permute-start.8 = (bf16[12,80,128]{2,1,0:T(8,128)(2,1)S(1)}, bf16[12,80,128]{2,1,0:T(8,128)(2,1)S(1)}, u32[]{:S(2)}, u32[]{:S(2)}) collective-permute-start(bf16[12,80,128]{2,1,0:T(8,128)(2,1)S(1)} %get-tuple-element.40), channel_id=1, source_target_pairs={{0,24},{2,0},{4,8},{6,16},{8,30},{10,6},{12,14},{14,22},{16,26},{1... | collective-permute-start | bytes 737288 | tf_op jit(solution)/shard_map/ppermute | solution.py:309
  23.7 14.8 %collective-permute-start.1 = (bf16[2,6,56,256]{3,2,1,0:T(8,128)(2,1)}, bf16[2,6,56,256]{3,2,1,0:T(8,128)(2,1)}, u32[]{:S(2)}, u32[]{:S(2)}) collective-permute-start(bf16[2,6,56,256]{3,2,1,0:T(8,128)(2,1)} %get-tuple-element.57), channel_id=1, source_target_pairs={{0,4},{2,6},{4,0},{6,2},{8,12},{10,14},{12,8},{14,10},{16,20},{18,... | collective-permute-start | bytes 1032200 | tf_op jit(solution)/shard_map/ppermute | solution.py:309
  26.1 19.4 %collective-permute-start.2 = (bf16[2,6,56,256]{3,2,1,0:T(8,128)(2,1)}, bf16[2,6,56,256]{3,2,1,0:T(8,128)(2,1)}, u32[]{:S(2)}, u32[]{:S(2)}) collective-permute-start(bf16[2,6,56,256]{3,2,1,0:T(8,128)(2,1)} %get-tuple-element.62), channel_id=1, source_target_pairs={{0,6},{2,0},{4,2},{6,4},{8,14},{10,8},{12,10},{14,12},{16,22},{18,... | collective-permute-start | bytes 1032200 | tf_op jit(solution)/shard_map/ppermute | solution.py:309
  27.8 43.1 %collective-permute-start.15 = (bf16[2,6,56,256]{3,2,1,0:T(8,128)(2,1)}, bf16[2,6,56,256]{3,2,1,0:T(8,128)(2,1)}, u32[]{:S(2)}, u32[]{:S(2)}) collective-permute-start(bf16[2,6,56,256]{3,2,1,0:T(8,128)(2,1)} %get-tuple-element.59), channel_id=1, source_target_pairs={{0,2},{2,4},{4,6},{6,0},{8,10},{10,12},{12,14},{14,8},{16,18},{18,... | collective-permute-start | bytes 1032200 | tf_op jit(solution)/shard_map/ppermute | solution.py:309
  34.3 36.6 %collective-permute-start.16 = (bf16[2,6,56,256]{3,2,1,0:T(8,128)(2,1)}, bf16[2,6,56,256]{3,2,1,0:T(8,128)(2,1)}, u32[]{:S(2)}, u32[]{:S(2)}) collective-permute-start(bf16[2,6,56,256]{3,2,1,0:T(8,128)(2,1)} %get-tuple-element.60), channel_id=1, source_target_pairs={{0,4},{2,6},{4,0},{6,2},{8,12},{10,14},{12,8},{14,10},{16,20},{18,... | collective-permute-start | bytes 1032200 | tf_op jit(solution)/shard_map/ppermute | solution.py:309
  37.8 33.1 %collective-permute-start.17 = (bf16[2,6,56,256]{3,2,1,0:T(8,128)(2,1)}, bf16[2,6,56,256]{3,2,1,0:T(8,128)(2,1)}, u32[]{:S(2)}, u32[]{:S(2)}) collective-permute-start(bf16[2,6,56,256]{3,2,1,0:T(8,128)(2,1)} %get-tuple-element.55), channel_id=1, source_target_pairs={{0,6},{2,0},{4,2},{6,4},{8,14},{10,8},{12,10},{14,12},{16,22},{18,... | collective-permute-start | bytes 1032200 | tf_op jit(solution)/shard_map/ppermute | solution.py:309
  38.5 25.8 %collective-permute-start.9 = (bf16[3,80,128]{2,1,0:T(8,128)(2,1)S(1)}, bf16[3,80,128]{2,1,0:T(8,128)(2,1)S(1)}, u32[]{:S(2)}, u32[]{:S(2)}) collective-permute-start(bf16[3,80,128]{2,1,0:T(8,128)(2,1)S(1)} %get-tuple-element.41), channel_id=1, source_target_pairs={{0,6},{6,2},{2,4},{8,14},{14,10},{10,12},{16,22},{22,18},{18,20},{... | collective-permute-start | bytes 184328 | tf_op jit(solution)/shard_map/ppermute | solution.py:309
  45.5 12.2 %collective-permute-start.10 = (bf16[2,80,128]{2,1,0:T(8,128)(2,1)S(1)}, bf16[2,80,128]{2,1,0:T(8,128)(2,1)S(1)}, u32[]{:S(2)}, u32[]{:S(2)}) collective-permute-start(bf16[2,80,128]{2,1,0:T(8,128)(2,1)S(1)} %get-tuple-element.42), channel_id=1, source_target_pairs={{6,0},{2,6},{4,2},{14,8},{10,14},{12,10},{22,16},{18,22},{20,18},{... | collective-permute-start | bytes 122888 | tf_op jit(solution)/shard_map/ppermute | solution.py:309
  57.6 21.9 %collective-permute-start.3 = (bf16[2,3,56,256]{3,2,1,0:T(8,128)(2,1)S(1)}, bf16[2,3,56,256]{3,2,1,0:T(8,128)(2,1)S(1)}, u32[]{:S(2)}, u32[]{:S(2)}) collective-permute-start(bf16[2,3,56,256]{3,2,1,0:T(8,128)(2,1)S(1)} %get-tuple-element.35), channel_id=1, source_target_pairs={{0,8},{6,14},{2,10},{4,12},{8,16},{14,22},{10,18},{12,20},{16,24},... | collective-permute-start | bytes 516104 | tf_op jit(solution)/shard_map/ppermute | solution.py:309
  64.2 15.3 %collective-permute-start.4 = (bf16[2,2,56,256]{3,2,1,0:T(8,128)(2,1)S(1)}, bf16[2,2,56,256]{3,2,1,0:T(8,128)(2,1)S(1)}, u32[]{:S(2)}, u32[]{:S(2)}) collective-permute-start(bf16[2,2,56,256]{3,2,1,0:T(8,128)(2,1)S(1)} %get-tuple-element.36), channel_id=1, source_target_pairs={{8,0},{14,6},{10,2},{12,4},{16,8},{22,14},{18,10},{20,12},{24,16},... | collective-permute-start | bytes 344072 | tf_op jit(solution)/shard_map/ppermute | solution.py:309
  72.7 23.9 %collective-permute-start.18 = (bf16[2,3,56,256]{3,2,1,0:T(8,128)(2,1)S(1)}, bf16[2,3,56,256]{3,2,1,0:T(8,128)(2,1)S(1)}, u32[]{:S(2)}, u32[]{:S(2)}) collective-permute-start(bf16[2,3,56,256]{3,2,1,0:T(8,128)(2,1)S(1)} %get-tuple-element.49), channel_id=1, source_target_pairs={{0,8},{6,14},{2,10},{4,12},{8,16},{14,22},{10,18},{12,20},{16,24},... | collective-permute-start | bytes 516104 | tf_op jit(solution)/shard_map/ppermute | solution.py:309
  78.2 18.4 %collective-permute-start.19 = (bf16[2,2,56,256]{3,2,1,0:T(8,128)(2,1)S(1)}, bf16[2,2,56,256]{3,2,1,0:T(8,128)(2,1)S(1)}, u32[]{:S(2)}, u32[]{:S(2)}) collective-permute-start(bf16[2,2,56,256]{3,2,1,0:T(8,128)(2,1)S(1)} %get-tuple-element.50), channel_id=1, source_target_pairs={{8,0},{14,6},{10,2},{12,4},{16,8},{22,14},{18,10},{20,12},{24,16},... | collective-permute-start | bytes 344072 | tf_op jit(solution)/shard_map/ppermute | solution.py:309
  87.8 52.4 %collective-permute-start.13 = (bf16[1,13,2,24,128]{4,3,2,1,0:T(8,128)(2,1)S(1)}, bf16[1,13,2,24,128]{4,3,2,1,0:T(8,128)(2,1)S(1)}, u32[]{:S(2)}, u32[]{:S(2)}) collective-permute-start(bf16[1,13,2,24,128]{4,3,2,1,0:T(8,128)(2,1)S(1)} %get-tuple-element.47), channel_id=1, source_target_pairs={{0,0},{2,8},{4,12},{6,4},{8,2},{10,10},{12,14},{14,6},{16,16},{18,... | collective-permute-start | bytes 479240 | tf_op jit(solution)/shard_map/ppermute | solution.py:309
  88.4 51.7 %collective-permute-start.14 = (bf16[1,13,2,24,128]{4,3,2,1,0:T(8,128)(2,1)S(1)}, bf16[1,13,2,24,128]{4,3,2,1,0:T(8,128)(2,1)S(1)}, u32[]{:S(2)}, u32[]{:S(2)}) collective-permute-start(bf16[1,13,2,24,128]{4,3,2,1,0:T(8,128)(2,1)S(1)} %get-tuple-element.48), channel_id=1, source_target_pairs={{0,2},{2,10},{4,14},{6,6},{8,0},{10,8},{12,12},{14,4},{16,18},{18,... | collective-permute-start | bytes 479240 | tf_op jit(solution)/shard_map/ppermute | solution.py:309
  104.8 12.9 %collective-permute-start.20 = (bf16[1,13,2,24,128]{4,3,2,1,0:T(8,128)(2,1)S(1)}, bf16[1,13,2,24,128]{4,3,2,1,0:T(8,128)(2,1)S(1)}, u32[]{:S(2)}, u32[]{:S(2)}) collective-permute-start(bf16[1,13,2,24,128]{4,3,2,1,0:T(8,128)(2,1)S(1)} %get-tuple-element.51), channel_id=1, source_target_pairs={{0,0},{2,8},{4,12},{6,4},{8,2},{10,10},{12,14},{14,6},{16,16},{18,... | collective-permute-start | bytes 479240 | tf_op jit(solution)/shard_map/ppermute | solution.py:309
  105.5 33.1 %collective-permute-start.21 = (bf16[1,13,2,24,128]{4,3,2,1,0:T(8,128)(2,1)S(1)}, bf16[1,13,2,24,128]{4,3,2,1,0:T(8,128)(2,1)S(1)}, u32[]{:S(2)}, u32[]{:S(2)}) collective-permute-start(bf16[1,13,2,24,128]{4,3,2,1,0:T(8,128)(2,1)S(1)} %get-tuple-element.52), channel_id=1, source_target_pairs={{0,2},{2,10},{4,14},{6,6},{8,0},{10,8},{12,12},{14,4},{16,18},{18,... | collective-permute-start | bytes 479240 | tf_op jit(solution)/shard_map/ppermute | solution.py:309
  117.1 16.1 %collective-permute-start.22 = (bf16[1,13,2,24,128]{4,3,2,1,0:T(8,128)(2,1)S(1)}, bf16[1,13,2,24,128]{4,3,2,1,0:T(8,128)(2,1)S(1)}, u32[]{:S(2)}, u32[]{:S(2)}) collective-permute-start(bf16[1,13,2,24,128]{4,3,2,1,0:T(8,128)(2,1)S(1)} %get-tuple-element.53), channel_id=1, source_target_pairs={{0,0},{2,8},{4,12},{6,4},{8,2},{10,10},{12,14},{14,6},{16,16},{18,... | collective-permute-start | bytes 479240 | tf_op jit(solution)/shard_map/ppermute | solution.py:309
  117.8 16.0 %collective-permute-start.23 = (bf16[1,13,2,24,128]{4,3,2,1,0:T(8,128)(2,1)S(1)}, bf16[1,13,2,24,128]{4,3,2,1,0:T(8,128)(2,1)S(1)}, u32[]{:S(2)}, u32[]{:S(2)}) collective-permute-start(bf16[1,13,2,24,128]{4,3,2,1,0:T(8,128)(2,1)S(1)} %get-tuple-element.54), channel_id=1, source_target_pairs={{0,2},{2,10},{4,14},{6,6},{8,0},{10,8},{12,12},{14,4},{16,18},{18,... | collective-permute-start | bytes 479240 | tf_op jit(solution)/shard_map/ppermute | solution.py:309
  133.2 8.5 %collective-permute-start.11 = (bf16[1,13,2,24,128]{4,3,2,1,0:T(8,128)(2,1)S(1)}, bf16[1,13,2,24,128]{4,3,2,1,0:T(8,128)(2,1)S(1)}, u32[]{:S(2)}, u32[]{:S(2)}) collective-permute-start(bf16[1,13,2,24,128]{4,3,2,1,0:T(8,128)(2,1)S(1)} %get-tuple-element.45), channel_id=1, source_target_pairs={{0,0},{2,8},{4,12},{6,4},{8,2},{10,10},{12,14},{14,6},{16,16},{18,... | collective-permute-start | bytes 479240 | tf_op jit(solution)/shard_map/ppermute | solution.py:309
  133.8 8.8 %collective-permute-start.12 = (bf16[1,13,2,24,128]{4,3,2,1,0:T(8,128)(2,1)S(1)}, bf16[1,13,2,24,128]{4,3,2,1,0:T(8,128)(2,1)S(1)}, u32[]{:S(2)}, u32[]{:S(2)}) collective-permute-start(bf16[1,13,2,24,128]{4,3,2,1,0:T(8,128)(2,1)S(1)} %get-tuple-element.46), channel_id=1, source_target_pairs={{0,2},{2,10},{4,14},{6,6},{8,0},{10,8},{12,12},{14,4},{16,18},{18,... | collective-permute-start | bytes 479240 | tf_op jit(solution)/shard_map/ppermute | solution.py:309
  (9 other events, 173.3 us)

commit v2 on v1

--- a/solution.py
+++ b/solution.py
@@ -1,3 +1,5 @@
+import functools
+
 import jax
 import jax.numpy as jnp
 from jax import lax
@@ -8,7 +10,6 @@
 
 AXES = ("rows", "cols")
 CHUNKS = 2
-RUN = 1
 HALVES = 2
 SIDE = 4
 UP, DOWN = 3, 2
@@ -35,7 +36,8 @@
         base = dy * deep
         for dx in range(3):
             at = (dy * 3 + dx) * ch
-            w1[base + dx * lidar : base + (dx + 1) * lidar, :] = joint[at : at + lidar, :]
+            to = base + (1, 0, 2)[dx] * lidar
+            w1[to : to + lidar, :] = joint[at : at + lidar, :]
             to = base + 3 * lidar + dx * camera
             w1[to : to + camera, :] = joint[at + lidar : at + ch, :]
         w1[base + 3 * ch : base + deep, :] = jnp.zeros((deep - 3 * ch, joined), BF)
@@ -140,58 +142,69 @@
     )(jnp.stack([tail_of, head_of]).astype(jnp.int32), *arrays, *arrays)
 
 
-def conv_kernel(pos, *refs, parts, sh, tr, pitch, rows, cols):
+def conv_scratch(tr, pitch, lidar, joined, block, pairs):
+    return [
+        pltpu.VMEM((tr + 6, pitch, lidar), BF),
+        pltpu.VMEM((tr + 6, pitch, 2 * lidar), BF),
+        pltpu.VMEM(((tr + 4) // 2, 2, pitch, 3 * joined), BF),
+        pltpu.VMEM((pairs, 2, pitch, block), jnp.float32),
+        pltpu.VMEM((pitch, joined), jnp.float32),
+    ]
+
+
+def conv_kernel(pos, *refs, parts, sh, tr, pitch, rows, cols, at, cam_at):
     windows = refs[:parts]
     above, below, camera, w1, b1, w2, b2 = refs[parts : parts + 7]
     outs = refs[parts + 7 : parts + 7 + HALVES]
-    tile, taps, mid, cells = refs[parts + 7 + HALVES :]
+    tile, taps, mid, cells, inside = refs[parts + 7 + HALVES :]
     group, member, half_id, column = pos[0], pos[1], pos[2], pos[3]
     wide = windows[0].shape[2]
     lidar = windows[0].shape[3]
     joined = w1.shape[1]
     block = w2.shape[1] // 2
-
-    @pl.when(pl.program_id(0) == 0)
-    def _():
-        tile[...] = jnp.zeros(tile.shape, BF)
-
-    tile[0:UP, 0:wide, :] = above[0]
+    col0 = column * (wide - 2 * SIDE) - SIDE
+
+    edge_cols = pitch - wide
+    tile[:, wide:, :] = jnp.zeros((tr + 6, edge_cols, lidar), BF)
+    tile[tr + UP + DOWN :, 0:wide, :] = jnp.zeros((tr + 6 - tr - UP - DOWN, wide, lidar), BF)
+    col = lax.broadcasted_iota(jnp.int32, inside.shape, 0) + col0
+    inside[...] = jnp.where((col >= 0) & (col < cols), 1.0, 0.0)
+
+    tile[0:UP, 0:wide, :] = above[at]
     for d in range(parts):
         source = lax.rem(member - d + parts, parts)
-        tile[pl.ds(UP + source * sh, sh), 0:wide, :] = windows[d][0]
-    tile[UP + tr : UP + tr + DOWN, 0:wide, :] = below[0]
+        tile[pl.ds(UP + source * sh, sh), 0:wide, :] = windows[d][at]
+    tile[UP + tr : UP + tr + DOWN, 0:wide, :] = below[at]
 
     step = 6
     flat = step * pitch
 
     def shift(i, _):
         r = i * step
-        x = tile[pl.ds(r, step)].reshape(flat, lidar)
-        x32 = x.astype(jnp.float32)
-        taps[pl.ds(r, step), :, 0:lidar] = pltpu.roll(x32, 1, 0).astype(BF).reshape(step, pitch, lidar)
-        taps[pl.ds(r, step), :, lidar : 2 * lidar] = x.reshape(step, pitch, lidar)
-        taps[pl.ds(r, step), :, 2 * lidar :] = pltpu.roll(x32, flat - 1, 0).astype(BF).reshape(step, pitch, lidar)
+        x = tile[pl.ds(r, step)].reshape(flat, lidar).astype(jnp.float32)
+        taps[pl.ds(r, step), :, 0:lidar] = pltpu.roll(x, 1, 0).astype(BF).reshape(step, pitch, lidar)
+        taps[pl.ds(r, step), :, lidar:] = pltpu.roll(x, flat - 1, 0).astype(BF).reshape(step, pitch, lidar)
         return 0
 
     lax.fori_loop(0, (tr + 6) // step, shift, 0)
 
-    n1 = 4
+    n1 = (tr + 4) // 2
     m1 = n1 * pitch
-    col0 = column * (wide - 2 * SIDE) - SIDE
 
     def first(i, _):
         r = i * n1
         lhs = []
         for dy in range(3):
-            lhs.append(taps[pl.ds(r + dy, n1)].reshape(m1, 3 * lidar))
-            lhs.append(camera[0, pl.ds(r + dy, n1)].reshape(m1, camera.shape[3]))
+            lhs.append(tile[pl.ds(r + dy, n1)].reshape(m1, lidar))
+            lhs.append(taps[pl.ds(r + dy, n1)].reshape(m1, 2 * lidar))
+            lhs.append(camera[cam_at, pl.ds(r + dy, n1)].reshape(m1, camera.shape[3]))
         acc = jnp.dot(jnp.concatenate(lhs, axis=1), w1[...], preferred_element_type=jnp.float32)
-        v = jnp.maximum(acc + b1[...], 0.0)
-        at = lax.broadcasted_iota(jnp.int32, (m1, joined), 0)
-        row = group * tr - 2 + r + at // pitch
-        col = col0 + at % pitch
-        keep = (row >= 0) & (row < rows) & (col >= 0) & (col < cols)
-        v = jnp.where(keep, v, 0.0)
+        v = jnp.maximum(acc + b1[...], 0.0).reshape(n1, pitch, joined)
+        kept = []
+        for y in range(n1):
+            row = group * tr - 2 + r + y
+            kept.append(v[y] * (inside[...] * jnp.where((row >= 0) & (row < rows), 1.0, 0.0)))
+        v = jnp.concatenate(kept, axis=0)
         shape = (n1 // 2, 2, pitch, joined)
         p = pl.ds(i * (n1 // 2), n1 // 2)
         mid[p, :, :, 0:joined] = pltpu.roll(v, 1, 0).astype(BF).reshape(shape)
@@ -205,25 +218,25 @@
     m2 = n2 * pitch
     lhs = [mid[i // 2 : i // 2 + n2, i % 2].reshape(m2, 3 * joined) for i in range(4)]
     acc = jnp.dot(jnp.concatenate(lhs, axis=1), w2[...], preferred_element_type=jnp.float32)
-    v = jnp.maximum(acc + b2[...], 0.0)
-    at = lax.broadcasted_iota(jnp.int32, (m2, 2 * block), 0)
-    half = lax.broadcasted_iota(jnp.int32, (m2, 2 * block), 1) // block
-    row = group * tr - 1 + (at // pitch) * 2 + half
-    col = col0 + at % pitch
-    keep = (row >= 0) & (row < rows) & (col >= 0) & (col < cols)
-    v = jnp.where(keep, v, 0.0)
+    v = pltpu.roll(jnp.maximum(acc + b2[...], 0.0), SIDE, 0)
     cells[:, 0] = v[:, :block].reshape(n2, pitch, block)
     cells[:, 1] = v[:, block:].reshape(n2, pitch, block)
     pairs = tr // 2
     w = (wide - 2 * SIDE) // HALVES
     for sub in range(HALVES):
-        c = SIDE + sub * w
+        c = 2 * SIDE + sub * w
         even = cells[0:pairs, 1, c : c + w, :].astype(BF)
         odd = cells[1 : pairs + 1, 0, c : c + w, :].astype(BF)
-        top = cells[0, 0, c : c + w, :]
+        top = jnp.where(group > 0, cells[0, 0, c : c + w, :], 0.0)
         corner = jnp.broadcast_to(cells[pairs, 0, c - 1 : c, :], (w, block))
+        beside = cells[0:pairs, :, c - 1, :].reshape(tr, block)
+        if sub == 0:
+            corner = jnp.where(column > 0, corner, 0.0)
+            beside = jnp.where(column > 0, beside, 0.0)
+        row = lax.broadcasted_iota(jnp.int32, beside.shape, 0)
+        beside = jnp.where((row == 0) & (group == 0), 0.0, beside)
         edge = jnp.where(half_id == 0, top, corner).astype(BF)
-        beside = cells[0:pairs, :, c - 1, :].reshape(tr, block).astype(BF)
+        beside = beside.astype(BF)
         for h in range(HALVES):
 
             @pl.when(lax.rem(half_id + h, HALVES) == sub)
@@ -286,8 +299,13 @@
     groups = n_rows * HALVES
     total = n_rows * n_cols
     half = members // 2
-    tile_of = [2 * m if m < half else 2 * (members - 1 - m) + 1 for m in range(members)]
-    holder = [tile_of.index(j) for j in range(members)]
+    turn = 2 if members % 4 == 0 else 0
+
+    tile_of = [[(2 * m if m < half else 2 * (members - 1 - m) + 1) ^ t for m in range(members)] for t in (0, turn)]
+    holder = [[tiles.index(j) for j in range(members)] for tiles in tile_of]
+
+    def seat(g, j):
+        return g * members + holder[g // HALVES % 2][j]
 
     def local(lidar, camera, joined_weight, joined_bias, block_weight, block_bias, down_weight, down_bias, proj_weight, proj_bias):
         frames, sh, cols, lidar_ch = lidar.shape
@@ -313,11 +331,11 @@
             for g in range(groups):
                 for j in range(members):
                     if 0 <= g + by_group < groups and 0 <= j + by_column < members:
-                        pairs.append((g * members + holder[j], (g + by_group) * members + holder[j + by_column]))
+                        pairs.append((seat(g, j), seat(g + by_group, j + by_column)))
             return send(x, pairs)
 
         def column_of(m):
-            return jnp.where(m < half, 2 * m, 2 * (members - 1 - m) + 1)
+            return jnp.where(m < half, 2 * m, 2 * (members - 1 - m) + 1) ^ (turn * (group // HALVES % 2))
 
         joint = joined_weight.reshape(-1, joined)
         square = block_weight.reshape(-1, block)
@@ -355,7 +373,7 @@
         )(place.reshape(1).astype(jnp.int32), turned)
         lidar, packed = lax.optimization_barrier((lidar, packed))
         arrived = [
-            send(packed[p], [(s, ((s + p) % groups) * members + holder[s // groups]) for s in range(total)])
+            send(packed[p], [(s, seat((s + p) % groups, s // groups)) for s in range(total)])
             for p in range(groups)
         ]
         tail, head = pick(arrived, (group + 1) % groups, group, 0)
@@ -385,8 +403,9 @@
         half_rows = tr // 2
         n = HALVES * half_rows
         jd = rounded(w // 2, 8)
-        blocks = jax.ShapeDtypeStruct((RUN, pairs2, 2, w, block), BF)
-        flops = 2 * RUN * pitch * ((tr + 4) * w1.shape[0] * joined + pairs2 * w2.shape[0] * 2 * block)
+        blocks = jax.ShapeDtypeStruct((1, pairs2, 2, w, block), BF)
+        flops = 2 * pitch * ((tr + 4) * w1.shape[0] * joined + pairs2 * w2.shape[0] * 2 * block)
+        framed = lambda a: pl.BlockSpec((1,) + a.shape[1:], lambda f, p: (f,) + (0,) * (a.ndim - 1))
         encoded = None
         step = frames // CHUNKS
         for f0 in range(0, frames, step):
@@ -399,26 +418,15 @@
             last, head = pick(windows, (member + 1) % members, member, 1)
             above = across(last, 1, 0)
             below = across(head, -1, 0)
-            for f1 in range(f0, f0 + step, RUN):
-                framed = lambda a, lo: pl.BlockSpec((1,) + a.shape[1:], lambda f, p: (f + lo,) + (0,) * (a.ndim - 1))
-                lo = f1 - f0
+            for f1 in range(f0, f0 + step):
                 tiles = pl.pallas_call(
-                    lambda *refs: conv_kernel(*refs, parts=members, sh=sh, tr=tr, pitch=pitch, rows=rows, cols=cols),
-                    grid_spec=pltpu.PrefetchScalarGridSpec(
-                        num_scalar_prefetch=1,
-                        grid=(RUN,),
-                        in_specs=[framed(x, lo) for x in [*windows, above, below]] + [framed(cam, f1), whole(w1), whole(b1), whole(w2), whole(b2)],
-                        out_specs=[framed(blocks, 0)] * HALVES,
-                        scratch_shapes=[
-                            pltpu.VMEM((tr + 6, pitch, lidar_ch), BF),
-                            pltpu.VMEM((tr + 6, pitch, 3 * lidar_ch), BF),
-                            pltpu.VMEM(((tr + 4) // 2, 2, pitch, 3 * joined), BF),
-                            pltpu.VMEM((pairs2, 2, pitch, block), jnp.float32),
-                        ],
-                    ),
+                    functools.partial(conv_kernel, parts=members, sh=sh, tr=tr, pitch=pitch, rows=rows, cols=cols, at=f1 - f0, cam_at=f1),
+                    in_specs=[pl.BlockSpec(memory_space=pltpu.SMEM)] + [pl.BlockSpec(memory_space=pltpu.VMEM)] * (members + 7),
+                    out_specs=[pl.BlockSpec(memory_space=pltpu.VMEM)] * HALVES,
+                    scratch_shapes=conv_scratch(tr, pitch, lidar_ch, joined, block, pairs2),
                     out_shape=[blocks] * HALVES,
                     compiler_params=limit(28),
-                    cost_estimate=pl.CostEstimate(flops=flops, bytes_accessed=2 * 10**6 * RUN, transcendentals=0),
+                    cost_estimate=pl.CostEstimate(flops=flops, bytes_accessed=2 * 10**6, transcendentals=0),
                 )(pos, *windows, above, below, cam, w1, b1, w2, b2)
                 pieces = []
                 for h in range(HALVES):
@@ -426,15 +434,15 @@
                     for s in range(total):
                         r, c = divmod(s, n_cols)
                         k, m = divmod(c, members)
-                        pairs.append((s, r * n_cols + HALVES * tile_of[m] + (k + h) % HALVES))
+                        pairs.append((s, r * n_cols + HALVES * tile_of[r % 2][m] + (k + h) % HALVES))
                     pieces.append(send(tiles[h], pairs))
                 old = [] if encoded is None else [encoded]
                 encoded = pl.pallas_call(
                     lambda *refs: encode_kernel(*refs, parts=HALVES, half_rows=half_rows, w=w),
                     grid_spec=pltpu.PrefetchScalarGridSpec(
                         num_scalar_prefetch=1,
-                        grid=(RUN,),
-                        in_specs=[framed(x, 0) for x in pieces] + [whole(x) for x in (w3, b3, proj_weight, bp)] + [pl.BlockSpec(memory_space=pl.ANY)] * len(old),
+                        grid=(1,),
+                        in_specs=[framed(x) for x in pieces] + [whole(x) for x in (w3, b3, proj_weight, bp)] + [pl.BlockSpec(memory_space=pl.ANY)] * len(old),
                         out_specs=pl.BlockSpec((1, n, 2, w, 2 * block), lambda f, p, f1=f1: (f + f1, 0, 0, 0, 0)),
                         scratch_shapes=[
                             pltpu.VMEM((n + 1, 2, rounded(w + 1, 8) + 16, block), jnp.float32),
@@ -444,7 +452,7 @@
                     out_shape=jax.ShapeDtypeStruct((frames, n, 2, w, 2 * block), BF),
                     input_output_aliases={5 + HALVES: 0} if old else {},
                     compiler_params=limit(12),
-                    cost_estimate=pl.CostEstimate(flops=2 * RUN * n * jd * w3.shape[0] * 256, bytes_accessed=10**6 * RUN, transcendentals=0),
+                    cost_estimate=pl.CostEstimate(flops=2 * n * jd * w3.shape[0] * 256, bytes_accessed=10**6, transcendentals=0),
                 )(cindex.reshape(1).astype(jnp.int32), *pieces, w3, b3, proj_weight, bp, *old)
         return encoded.reshape(frames, 2 * n, w, 2 * block)
 

time: 147 us -> 141 us (0.959)
  the two profiles are of different devices: /device:TPU:0 before, /device:TPU:2 now
where the time goes in v2:
time: 141 us; the launch traced here: 140 us
  starting transfers between devices  78.5 us (56%)
  Pallas kernels  44 us (31%)
  waiting for transfers between devices  11.5 us (8%)
  local copies, waits for them, and re-layouts  5.71 us (4%)
    ppermute x24, starting transfers between devices, send(): return lax.ppermute(x, AXES, pairs)  78.5 us
    pallas_call x4, Pallas kernels, local(): pl.pallas_call(functools.partial(conv_kernel, parts=members, sh=sh, tr=tr...  26.3 us
    ppermute x24, waiting for transfers between devices, send(): return lax.ppermute(x, AXES, pairs)  11.5 us
    pallas_call x4, Pallas kernels, local(): pl.pallas_call(lambda *refs: encode_kernel(*refs, parts=HALVES, half_rows...  6.16 us
    pallas_call x1, Pallas kernels, local(): pl.pallas_call(lambda *refs: camera_unpack_kernel(*refs, groups=groups, s...  4.82 us
    dynamic_slice x1, local copies, waits for them, and re-layouts, local(): lax.dynamic_slice(padded, (f0, 0, column_of((member + d) % members) * tw,...  4.46 us
    pallas_call x3, Pallas kernels, pick(): pl.pallas_call(pick_kernel, grid_spec=pltpu.PrefetchScalarGridSpec(num_sc...  4.34 us
  transfers between devices with their start and end apart: 24, of which 2 were waited for; matrix products, arithmetic and copies ran while one was open for 3% of the time, Pallas kernels for 29%

profile of v2, /device:TPU:2, one launch (start us, length us, event | category | flops | bytes accessed | tf_op | source)
XLA Modules:
  0.0 140.4 jit_solution(4605400740409135347)
XLA Ops:
  1.2 2.1 %camera_pack.1 = (bf16[12,80,128]{2,1,0:T(8,128)(2,1)}, bf16[12,80,128]{2,1,0:T(8,128)(2,1)}, bf16[12,80,128]{2,1,0:T(8,128)(2,1)}, bf16[12,80,128]{2,1,0:T(8,128)(2,1)S(1)}) custom-call(s32[1]{0:T(128)} %bitcast.5.refs_0_, bf16[4,12,80,96]{3,2,1,0:T(8,128)(2,1)S(1)} %bitcast.27), custom_call_target="tpu_custom_call" | custom-call | tf_op jit(solution)/shard_map/camera_pack/pallas_call | solution.py:362
  3.3 3.4 %collective-permute-start.5 = (bf16[12,80,128]{2,1,0:T(8,128)(2,1)}, bf16[12,80,128]{2,1,0:T(8,128)(2,1)S(1)}, u32[]{:S(2)}, u32[]{:S(2)}) collective-permute-start(bf16[12,80,128]{2,1,0:T(8,128)(2,1)} %get-tuple-element.37), channel_id=1, source_target_pairs={{0,0},{2,8},{4,18},{6,26},{8,6},{10,14},{12,20},{14,28},{16,2},{18... | collective-permute-start | bytes 737288 | tf_op jit(solution)/shard_map/ppermute | solution.py:327
  6.7 3.7 %collective-permute-start.6 = (bf16[12,80,128]{2,1,0:T(8,128)(2,1)}, bf16[12,80,128]{2,1,0:T(8,128)(2,1)S(1)}, u32[]{:S(2)}, u32[]{:S(2)}) collective-permute-start(bf16[12,80,128]{2,1,0:T(8,128)(2,1)} %get-tuple-element.38), channel_id=1, source_target_pairs={{0,8},{2,18},{4,26},{6,0},{8,14},{10,20},{12,28},{14,6},{16,10},{1... | collective-permute-start | bytes 737288 | tf_op jit(solution)/shard_map/ppermute | solution.py:327
  10.3 4.5 %pad_dynamic-slice_fusion = (bf16[2,6,56,256]{3,2,1,0:T(8,128)(2,1)}, bf16[2,6,56,256]{3,2,1,0:T(8,128)(2,1)}, bf16[2,6,56,256]{3,2,1,0:T(8,128)(2,1)}, bf16[2,6...) fusion(s32[]{:T(128)S(6)} %select_n.129, ...), kind=kLoop, calls=%fused_computation | loop fusion | bytes 5111824 | tf_op jit(solution)/shard_map/dynamic_slice | solution.py:414
  16.5 4.6 %collective-permute-start.8 = (bf16[12,80,128]{2,1,0:T(8,128)(2,1)S(1)}, bf16[12,80,128]{2,1,0:T(8,128)(2,1)S(1)}, u32[]{:S(2)}, u32[]{:S(2)}) collective-permute-start(bf16[12,80,128]{2,1,0:T(8,128)(2,1)S(1)} %get-tuple-element.40), channel_id=1, source_target_pairs={{0,26},{2,0},{4,8},{6,18},{8,28},{10,6},{12,14},{14,20},{16,24},{1... | collective-permute-start | bytes 737288 | tf_op jit(solution)/shard_map/ppermute | solution.py:327
  22.9 9.9 %collective-permute-start.15 = (bf16[2,6,56,256]{3,2,1,0:T(8,128)(2,1)}, bf16[2,6,56,256]{3,2,1,0:T(8,128)(2,1)}, u32[]{:S(2)}, u32[]{:S(2)}) collective-permute-start(bf16[2,6,56,256]{3,2,1,0:T(8,128)(2,1)} %get-tuple-element.59), channel_id=1, source_target_pairs={{0,2},{2,4},{4,6},{6,0},{8,10},{10,12},{12,14},{14,8},{16,18},{18,... | collective-permute-start | bytes 1032200 | tf_op jit(solution)/shard_map/ppermute | solution.py:327
  32.9 2.0 %collective-permute-start.16 = (bf16[2,6,56,256]{3,2,1,0:T(8,128)(2,1)}, bf16[2,6,56,256]{3,2,1,0:T(8,128)(2,1)}, u32[]{:S(2)}, u32[]{:S(2)}) collective-permute-start(bf16[2,6,56,256]{3,2,1,0:T(8,128)(2,1)} %get-tuple-element.60), channel_id=1, source_target_pairs={{0,4},{2,6},{4,0},{6,2},{8,12},{10,14},{12,8},{14,10},{16,20},{18,... | collective-permute-start | bytes 1032200 | tf_op jit(solution)/shard_map/ppermute | solution.py:327
  36.5 7.5 %collective-permute-start.9 = (bf16[3,80,128]{2,1,0:T(8,128)(2,1)S(1)}, bf16[3,80,128]{2,1,0:T(8,128)(2,1)S(1)}, u32[]{:S(2)}, u32[]{:S(2)}) collective-permute-start(bf16[3,80,128]{2,1,0:T(8,128)(2,1)S(1)} %get-tuple-element.41), channel_id=1, source_target_pairs={{0,6},{6,2},{2,4},{8,14},{14,10},{10,12},{18,20},{20,16},{16,22},{... | collective-permute-start | bytes 184328 | tf_op jit(solution)/shard_map/ppermute | solution.py:327
  44.1 1.9 %collective-permute-start.10 = (bf16[2,80,128]{2,1,0:T(8,128)(2,1)S(1)}, bf16[2,80,128]{2,1,0:T(8,128)(2,1)S(1)}, u32[]{:S(2)}, u32[]{:S(2)}) collective-permute-start(bf16[2,80,128]{2,1,0:T(8,128)(2,1)S(1)} %get-tuple-element.42), channel_id=1, source_target_pairs={{6,0},{2,6},{4,2},{14,8},{10,14},{12,10},{20,18},{16,20},{22,16},{... | collective-permute-start | bytes 122888 | tf_op jit(solution)/shard_map/ppermute | solution.py:327
  47.9 9.1 %collective-permute-done.10.refs_6_ = bf16[2,80,128]{2,1,0:T(8,128)(2,1)S(1)} collective-permute-done((bf16[2,80,128]{2,1,0:T(8,128)(2,1)S(1)}, bf16[2,80,128]{2,1,0:T(8,128)(2,1)S(1)}, u32[]{:S(2)}, u32[]{:S(2)}) %collective-permute-start.10) | collective-permute-done | bytes 40992 | tf_op jit(solution)/shard_map/ppermute | solution.py:327
  57.0 2.5 %collective-permute-start.3 = (bf16[2,3,56,256]{3,2,1,0:T(8,128)(2,1)S(1)}, bf16[2,3,56,256]{3,2,1,0:T(8,128)(2,1)S(1)}, u32[]{:S(2)}, u32[]{:S(2)}) collective-permute-start(bf16[2,3,56,256]{3,2,1,0:T(8,128)(2,1)S(1)} %get-tuple-element.35), channel_id=1, source_target_pairs={{0,8},{6,14},{2,10},{4,12},{8,18},{14,20},{10,16},{12,22},{18,26},... | collective-permute-start | bytes 516104 | tf_op jit(solution)/shard_map/ppermute | solution.py:327
  59.6 6.0 %collective-permute-start.4 = (bf16[2,2,56,256]{3,2,1,0:T(8,128)(2,1)S(1)}, bf16[2,2,56,256]{3,2,1,0:T(8,128)(2,1)S(1)}, u32[]{:S(2)}, u32[]{:S(2)}) collective-permute-start(bf16[2,2,56,256]{3,2,1,0:T(8,128)(2,1)S(1)} %get-tuple-element.36), channel_id=1, source_target_pairs={{8,0},{14,6},{10,2},{12,4},{18,8},{20,14},{16,10},{22,12},{26,18},... | collective-permute-start | bytes 344072 | tf_op jit(solution)/shard_map/ppermute | solution.py:327
  66.1 4.8 %camera_unpack.1 = bf16[128,64,256]{2,1,0:T(8,128)(2,1)S(1)} custom-call(s32[1]{0:T(128)} %bitcast.1.refs_0_, bf16[12,80,128]{2,1,0:T(8,128)(2,1)S(1)} %collective-permute-done.5.refs_0_.refs_4_.refs_1_, bf16[12,80,128]{2,1,0:T(8,128)(2,1)S(1)} %collective-permute-done.6.refs_1_.refs_5_.refs_2_, ...), custom_call_target="tpu_custom_call" | custom-call | tf_op jit(solution)/shard_map/camera_unpack/pallas_call | solution.py:382
  72.8 1.9 %collective-permute-start.18 = (bf16[2,3,56,256]{3,2,1,0:T(8,128)(2,1)S(1)}, bf16[2,3,56,256]{3,2,1,0:T(8,128)(2,1)S(1)}, u32[]{:S(2)}, u32[]{:S(2)}) collective-permute-start(bf16[2,3,56,256]{3,2,1,0:T(8,128)(2,1)S(1)} %get-tuple-element.49), channel_id=1, source_target_pairs={{0,8},{6,14},{2,10},{4,12},{8,18},{14,20},{10,16},{12,22},{18,26},... | collective-permute-start | bytes 516104 | tf_op jit(solution)/shard_map/ppermute | solution.py:327
  74.7 6.6 %collective-permute-start.19 = (bf16[2,2,56,256]{3,2,1,0:T(8,128)(2,1)S(1)}, bf16[2,2,56,256]{3,2,1,0:T(8,128)(2,1)S(1)}, u32[]{:S(2)}, u32[]{:S(2)}) collective-permute-start(bf16[2,2,56,256]{3,2,1,0:T(8,128)(2,1)S(1)} %get-tuple-element.50), channel_id=1, source_target_pairs={{8,0},{14,6},{10,2},{12,4},{18,8},{20,14},{16,10},{22,12},{26,18},... | collective-permute-start | bytes 344072 | tf_op jit(solution)/shard_map/ppermute | solution.py:327
  81.4 6.6 %shard_map.103 = (bf16[1,13,2,24,128]{4,3,2,1,0:T(8,128)(2,1)S(1)}, bf16[1,13,2,24,128]{4,3,2,1,0:T(8,128)(2,1)S(1)}) custom-call(s32[4]{0:T(128)S(1)} %pad_add_fusion.pos, bf16[2,6,56,256]{3,2,1,0:T(8,128)(2,1)S(1)} %get-tuple-element.61.refs_0_.refs_4_, bf16[2,6,56,256]{3,2,1,0:T(8,128)(2,1)} %collective-permute-done.refs_1_.refs_5_, ...), custom_call_target="tpu_custom_call" | custom-call | flops 4127195136 | bytes 2000000 | tf_op jit(solution)/shard_map/pallas_call | solution.py:422
  89.9 6.4 %collective-permute-start.14 = (bf16[1,13,2,24,128]{4,3,2,1,0:T(8,128)(2,1)S(1)}, bf16[1,13,2,24,128]{4,3,2,1,0:T(8,128)(2,1)S(1)}, u32[]{:S(2)}, u32[]{:S(2)}) collective-permute-start(bf16[1,13,2,24,128]{4,3,2,1,0:T(8,128)(2,1)S(1)} %get-tuple-element.48), channel_id=1, source_target_pairs={{0,2},{2,10},{4,14},{6,6},{8,0},{10,8},{12,12},{14,4},{16,26},{18,... | collective-permute-start | bytes 479240 | tf_op jit(solution)/shard_map/ppermute | solution.py:327
  96.3 6.6 %shard_map.105 = (bf16[1,13,2,24,128]{4,3,2,1,0:T(8,128)(2,1)S(1)}, bf16[1,13,2,24,128]{4,3,2,1,0:T(8,128)(2,1)S(1)}) custom-call(s32[4]{0:T(128)S(1)} %pad_add_fusion.pos, bf16[2,6,56,256]{3,2,1,0:T(8,128)(2,1)S(1)} %get-tuple-element.58.refs_0_.refs_4_, bf16[2,6,56,256]{3,2,1,0:T(8,128)(2,1)} %collective-permute-done.15.refs_1_.refs_5_, ...), custom_call_target="tpu_custom_call" | custom-call | flops 4127195136 | bytes 2000000 | tf_op jit(solution)/shard_map/pallas_call | solution.py:422
  102.9 1.9 %collective-permute-start.20 = (bf16[1,13,2,24,128]{4,3,2,1,0:T(8,128)(2,1)S(1)}, bf16[1,13,2,24,128]{4,3,2,1,0:T(8,128)(2,1)S(1)}, u32[]{:S(2)}, u32[]{:S(2)}) collective-permute-start(bf16[1,13,2,24,128]{4,3,2,1,0:T(8,128)(2,1)S(1)} %get-tuple-element.51), channel_id=1, source_target_pairs={{0,0},{2,8},{4,12},{6,4},{8,2},{10,10},{12,14},{14,6},{16,24},{18,... | collective-permute-start | bytes 479240 | tf_op jit(solution)/shard_map/ppermute | solution.py:327
  104.9 2.1 %collective-permute-start.21 = (bf16[1,13,2,24,128]{4,3,2,1,0:T(8,128)(2,1)S(1)}, bf16[1,13,2,24,128]{4,3,2,1,0:T(8,128)(2,1)S(1)}, u32[]{:S(2)}, u32[]{:S(2)}) collective-permute-start(bf16[1,13,2,24,128]{4,3,2,1,0:T(8,128)(2,1)S(1)} %get-tuple-element.52), channel_id=1, source_target_pairs={{0,2},{2,10},{4,14},{6,6},{8,0},{10,8},{12,12},{14,4},{16,26},{18,... | collective-permute-start | bytes 479240 | tf_op jit(solution)/shard_map/ppermute | solution.py:327
  107.0 6.6 %shard_map.106 = (bf16[1,13,2,24,128]{4,3,2,1,0:T(8,128)(2,1)S(1)}, bf16[1,13,2,24,128]{4,3,2,1,0:T(8,128)(2,1)S(1)}) custom-call(s32[4]{0:T(128)S(1)} %pad_add_fusion.pos, bf16[2,6,56,256]{3,2,1,0:T(8,128)(2,1)S(1)} %get-tuple-element.58.refs_0_.refs_4_, bf16[2,6,56,256]{3,2,1,0:T(8,128)(2,1)} %collective-permute-done.15.refs_1_.refs_5_, ...), custom_call_target="tpu_custom_call" | custom-call | flops 4127195136 | bytes 2000000 | tf_op jit(solution)/shard_map/pallas_call | solution.py:422
  115.5 5.8 %collective-permute-start.23 = (bf16[1,13,2,24,128]{4,3,2,1,0:T(8,128)(2,1)S(1)}, bf16[1,13,2,24,128]{4,3,2,1,0:T(8,128)(2,1)S(1)}, u32[]{:S(2)}, u32[]{:S(2)}) collective-permute-start(bf16[1,13,2,24,128]{4,3,2,1,0:T(8,128)(2,1)S(1)} %get-tuple-element.54), channel_id=1, source_target_pairs={{0,2},{2,10},{4,14},{6,6},{8,0},{10,8},{12,12},{14,4},{16,26},{18,... | collective-permute-start | bytes 479240 | tf_op jit(solution)/shard_map/ppermute | solution.py:327
  121.4 6.6 %shard_map.102 = (bf16[1,13,2,24,128]{4,3,2,1,0:T(8,128)(2,1)S(1)}, bf16[1,13,2,24,128]{4,3,2,1,0:T(8,128)(2,1)S(1)}) custom-call(s32[4]{0:T(128)S(1)} %pad_add_fusion.pos, bf16[2,6,56,256]{3,2,1,0:T(8,128)(2,1)S(1)} %get-tuple-element.61.refs_0_.refs_4_, bf16[2,6,56,256]{3,2,1,0:T(8,128)(2,1)} %collective-permute-done.refs_1_.refs_5_, ...), custom_call_target="tpu_custom_call" | custom-call | flops 4127195136 | bytes 2000000 | tf_op jit(solution)/shard_map/pallas_call | solution.py:422
  136.5 2.4 %collective-permute-done.12.refs_2_ = bf16[1,13,2,24,128]{4,3,2,1,0:T(8,128)(2,1)S(1)} collective-permute-done((bf16[1,13,2,24,128]{4,3,2,1,0:T(8,128)(2,1)S(1)}, bf16[1,13,2,24,128]{4,3,2,1,0:T(8,128)(2,1)S(1)}, u32[]{:S(2)}, u32[]{:S(2)}) %collective-permute-start.12) | collective-permute-done | bytes 159776 | tf_op jit(solution)/shard_map/ppermute | solution.py:327
  (61 shorter events, 24.6 us)
Async XLA Ops:
  3.3 17.9 %collective-permute-start.5 = (bf16[12,80,128]{2,1,0:T(8,128)(2,1)}, bf16[12,80,128]{2,1,0:T(8,128)(2,1)S(1)}, u32[]{:S(2)}, u32[]{:S(2)}) collective-permute-start(bf16[12,80,128]{2,1,0:T(8,128)(2,1)} %get-tuple-element.37), channel_id=1, source_target_pairs={{0,0},{2,8},{4,18},{6,26},{8,6},{10,14},{12,20},{14,28},{16,2},{18... | collective-permute-start | bytes 737288 | tf_op jit(solution)/shard_map/ppermute | solution.py:327
  6.7 15.6 %collective-permute-start.6 = (bf16[12,80,128]{2,1,0:T(8,128)(2,1)}, bf16[12,80,128]{2,1,0:T(8,128)(2,1)S(1)}, u32[]{:S(2)}, u32[]{:S(2)}) collective-permute-start(bf16[12,80,128]{2,1,0:T(8,128)(2,1)} %get-tuple-element.38), channel_id=1, source_target_pairs={{0,8},{2,18},{4,26},{6,0},{8,14},{10,20},{12,28},{14,6},{16,10},{1... | collective-permute-start | bytes 737288 | tf_op jit(solution)/shard_map/ppermute | solution.py:327
  14.8 20.1 %collective-permute-start = (bf16[2,6,56,256]{3,2,1,0:T(8,128)(2,1)}, bf16[2,6,56,256]{3,2,1,0:T(8,128)(2,1)}, u32[]{:S(2)}, u32[]{:S(2)}) collective-permute-start(bf16[2,6,56,256]{3,2,1,0:T(8,128)(2,1)} %get-tuple-element.56), channel_id=1, source_target_pairs={{0,2},{2,4},{4,6},{6,0},{8,10},{10,12},{12,14},{14,8},{16,18},{18,... | collective-permute-start | bytes 1032200 | tf_op jit(solution)/shard_map/ppermute | solution.py:327
  14.8 8.1 %collective-permute-start.7 = (bf16[12,80,128]{2,1,0:T(8,128)(2,1)}, bf16[12,80,128]{2,1,0:T(8,128)(2,1)S(1)}, u32[]{:S(2)}, u32[]{:S(2)}) collective-permute-start(bf16[12,80,128]{2,1,0:T(8,128)(2,1)} %get-tuple-element.39), channel_id=1, source_target_pairs={{0,18},{2,26},{4,0},{6,8},{8,20},{10,28},{12,6},{14,14},{16,16},{1... | collective-permute-start | bytes 737288 | tf_op jit(solution)/shard_map/ppermute | solution.py:327
  16.5 16.3 %collective-permute-start.8 = (bf16[12,80,128]{2,1,0:T(8,128)(2,1)S(1)}, bf16[12,80,128]{2,1,0:T(8,128)(2,1)S(1)}, u32[]{:S(2)}, u32[]{:S(2)}) collective-permute-start(bf16[12,80,128]{2,1,0:T(8,128)(2,1)S(1)} %get-tuple-element.40), channel_id=1, source_target_pairs={{0,26},{2,0},{4,8},{6,18},{8,28},{10,6},{12,14},{14,20},{16,24},{1... | collective-permute-start | bytes 737288 | tf_op jit(solution)/shard_map/ppermute | solution.py:327
  21.1 15.4 %collective-permute-start.1 = (bf16[2,6,56,256]{3,2,1,0:T(8,128)(2,1)}, bf16[2,6,56,256]{3,2,1,0:T(8,128)(2,1)}, u32[]{:S(2)}, u32[]{:S(2)}) collective-permute-start(bf16[2,6,56,256]{3,2,1,0:T(8,128)(2,1)} %get-tuple-element.57), channel_id=1, source_target_pairs={{0,4},{2,6},{4,0},{6,2},{8,12},{10,14},{12,8},{14,10},{16,20},{18,... | collective-permute-start | bytes 1032200 | tf_op jit(solution)/shard_map/ppermute | solution.py:327
  22.3 21.8 %collective-permute-start.2 = (bf16[2,6,56,256]{3,2,1,0:T(8,128)(2,1)}, bf16[2,6,56,256]{3,2,1,0:T(8,128)(2,1)}, u32[]{:S(2)}, u32[]{:S(2)}) collective-permute-start(bf16[2,6,56,256]{3,2,1,0:T(8,128)(2,1)} %get-tuple-element.62), channel_id=1, source_target_pairs={{0,6},{2,0},{4,2},{6,4},{8,14},{10,8},{12,10},{14,12},{16,22},{18,... | collective-permute-start | bytes 1032200 | tf_op jit(solution)/shard_map/ppermute | solution.py:327
  22.9 48.0 %collective-permute-start.15 = (bf16[2,6,56,256]{3,2,1,0:T(8,128)(2,1)}, bf16[2,6,56,256]{3,2,1,0:T(8,128)(2,1)}, u32[]{:S(2)}, u32[]{:S(2)}) collective-permute-start(bf16[2,6,56,256]{3,2,1,0:T(8,128)(2,1)} %get-tuple-element.59), channel_id=1, source_target_pairs={{0,2},{2,4},{4,6},{6,0},{8,10},{10,12},{12,14},{14,8},{16,18},{18,... | collective-permute-start | bytes 1032200 | tf_op jit(solution)/shard_map/ppermute | solution.py:327
  32.9 38.1 %collective-permute-start.16 = (bf16[2,6,56,256]{3,2,1,0:T(8,128)(2,1)}, bf16[2,6,56,256]{3,2,1,0:T(8,128)(2,1)}, u32[]{:S(2)}, u32[]{:S(2)}) collective-permute-start(bf16[2,6,56,256]{3,2,1,0:T(8,128)(2,1)} %get-tuple-element.60), channel_id=1, source_target_pairs={{0,4},{2,6},{4,0},{6,2},{8,12},{10,14},{12,8},{14,10},{16,20},{18,... | collective-permute-start | bytes 1032200 | tf_op jit(solution)/shard_map/ppermute | solution.py:327
  34.8 36.1 %collective-permute-start.17 = (bf16[2,6,56,256]{3,2,1,0:T(8,128)(2,1)}, bf16[2,6,56,256]{3,2,1,0:T(8,128)(2,1)}, u32[]{:S(2)}, u32[]{:S(2)}) collective-permute-start(bf16[2,6,56,256]{3,2,1,0:T(8,128)(2,1)} %get-tuple-element.55), channel_id=1, source_target_pairs={{0,6},{2,0},{4,2},{6,4},{8,14},{10,8},{12,10},{14,12},{16,22},{18,... | collective-permute-start | bytes 1032200 | tf_op jit(solution)/shard_map/ppermute | solution.py:327
  36.5 23.1 %collective-permute-start.9 = (bf16[3,80,128]{2,1,0:T(8,128)(2,1)S(1)}, bf16[3,80,128]{2,1,0:T(8,128)(2,1)S(1)}, u32[]{:S(2)}, u32[]{:S(2)}) collective-permute-start(bf16[3,80,128]{2,1,0:T(8,128)(2,1)S(1)} %get-tuple-element.41), channel_id=1, source_target_pairs={{0,6},{6,2},{2,4},{8,14},{14,10},{10,12},{18,20},{20,16},{16,22},{... | collective-permute-start | bytes 184328 | tf_op jit(solution)/shard_map/ppermute | solution.py:327
  44.1 13.0 %collective-permute-start.10 = (bf16[2,80,128]{2,1,0:T(8,128)(2,1)S(1)}, bf16[2,80,128]{2,1,0:T(8,128)(2,1)S(1)}, u32[]{:S(2)}, u32[]{:S(2)}) collective-permute-start(bf16[2,80,128]{2,1,0:T(8,128)(2,1)S(1)} %get-tuple-element.42), channel_id=1, source_target_pairs={{6,0},{2,6},{4,2},{14,8},{10,14},{12,10},{20,18},{16,20},{22,16},{... | collective-permute-start | bytes 122888 | tf_op jit(solution)/shard_map/ppermute | solution.py:327
  57.0 24.3 %collective-permute-start.3 = (bf16[2,3,56,256]{3,2,1,0:T(8,128)(2,1)S(1)}, bf16[2,3,56,256]{3,2,1,0:T(8,128)(2,1)S(1)}, u32[]{:S(2)}, u32[]{:S(2)}) collective-permute-start(bf16[2,3,56,256]{3,2,1,0:T(8,128)(2,1)S(1)} %get-tuple-element.35), channel_id=1, source_target_pairs={{0,8},{6,14},{2,10},{4,12},{8,18},{14,20},{10,16},{12,22},{18,26},... | collective-permute-start | bytes 516104 | tf_op jit(solution)/shard_map/ppermute | solution.py:327
  59.6 21.8 %collective-permute-start.4 = (bf16[2,2,56,256]{3,2,1,0:T(8,128)(2,1)S(1)}, bf16[2,2,56,256]{3,2,1,0:T(8,128)(2,1)S(1)}, u32[]{:S(2)}, u32[]{:S(2)}) collective-permute-start(bf16[2,2,56,256]{3,2,1,0:T(8,128)(2,1)S(1)} %get-tuple-element.36), channel_id=1, source_target_pairs={{8,0},{14,6},{10,2},{12,4},{18,8},{20,14},{16,10},{22,12},{26,18},... | collective-permute-start | bytes 344072 | tf_op jit(solution)/shard_map/ppermute | solution.py:327
  72.8 23.5 %collective-permute-start.18 = (bf16[2,3,56,256]{3,2,1,0:T(8,128)(2,1)S(1)}, bf16[2,3,56,256]{3,2,1,0:T(8,128)(2,1)S(1)}, u32[]{:S(2)}, u32[]{:S(2)}) collective-permute-start(bf16[2,3,56,256]{3,2,1,0:T(8,128)(2,1)S(1)} %get-tuple-element.49), channel_id=1, source_target_pairs={{0,8},{6,14},{2,10},{4,12},{8,18},{14,20},{10,16},{12,22},{18,26},... | collective-permute-start | bytes 516104 | tf_op jit(solution)/shard_map/ppermute | solution.py:327
  74.7 21.6 %collective-permute-start.19 = (bf16[2,2,56,256]{3,2,1,0:T(8,128)(2,1)S(1)}, bf16[2,2,56,256]{3,2,1,0:T(8,128)(2,1)S(1)}, u32[]{:S(2)}, u32[]{:S(2)}) collective-permute-start(bf16[2,2,56,256]{3,2,1,0:T(8,128)(2,1)S(1)} %get-tuple-element.50), channel_id=1, source_target_pairs={{8,0},{14,6},{10,2},{12,4},{18,8},{20,14},{16,10},{22,12},{26,18},... | collective-permute-start | bytes 344072 | tf_op jit(solution)/shard_map/ppermute | solution.py:327
  88.0 47.0 %collective-permute-start.13 = (bf16[1,13,2,24,128]{4,3,2,1,0:T(8,128)(2,1)S(1)}, bf16[1,13,2,24,128]{4,3,2,1,0:T(8,128)(2,1)S(1)}, u32[]{:S(2)}, u32[]{:S(2)}) collective-permute-start(bf16[1,13,2,24,128]{4,3,2,1,0:T(8,128)(2,1)S(1)} %get-tuple-element.47), channel_id=1, source_target_pairs={{0,0},{2,8},{4,12},{6,4},{8,2},{10,10},{12,14},{14,6},{16,24},{18,... | collective-permute-start | bytes 479240 | tf_op jit(solution)/shard_map/ppermute | solution.py:327
  89.9 45.1 %collective-permute-start.14 = (bf16[1,13,2,24,128]{4,3,2,1,0:T(8,128)(2,1)S(1)}, bf16[1,13,2,24,128]{4,3,2,1,0:T(8,128)(2,1)S(1)}, u32[]{:S(2)}, u32[]{:S(2)}) collective-permute-start(bf16[1,13,2,24,128]{4,3,2,1,0:T(8,128)(2,1)S(1)} %get-tuple-element.48), channel_id=1, source_target_pairs={{0,2},{2,10},{4,14},{6,6},{8,0},{10,8},{12,12},{14,4},{16,26},{18,... | collective-permute-start | bytes 479240 | tf_op jit(solution)/shard_map/ppermute | solution.py:327
  102.9 12.6 %collective-permute-start.20 = (bf16[1,13,2,24,128]{4,3,2,1,0:T(8,128)(2,1)S(1)}, bf16[1,13,2,24,128]{4,3,2,1,0:T(8,128)(2,1)S(1)}, u32[]{:S(2)}, u32[]{:S(2)}) collective-permute-start(bf16[1,13,2,24,128]{4,3,2,1,0:T(8,128)(2,1)S(1)} %get-tuple-element.51), channel_id=1, source_target_pairs={{0,0},{2,8},{4,12},{6,4},{8,2},{10,10},{12,14},{14,6},{16,24},{18,... | collective-permute-start | bytes 479240 | tf_op jit(solution)/shard_map/ppermute | solution.py:327
  104.9 28.6 %collective-permute-start.21 = (bf16[1,13,2,24,128]{4,3,2,1,0:T(8,128)(2,1)S(1)}, bf16[1,13,2,24,128]{4,3,2,1,0:T(8,128)(2,1)S(1)}, u32[]{:S(2)}, u32[]{:S(2)}) collective-permute-start(bf16[1,13,2,24,128]{4,3,2,1,0:T(8,128)(2,1)S(1)} %get-tuple-element.52), channel_id=1, source_target_pairs={{0,2},{2,10},{4,14},{6,6},{8,0},{10,8},{12,12},{14,4},{16,26},{18,... | collective-permute-start | bytes 479240 | tf_op jit(solution)/shard_map/ppermute | solution.py:327
  113.6 14.4 %collective-permute-start.22 = (bf16[1,13,2,24,128]{4,3,2,1,0:T(8,128)(2,1)S(1)}, bf16[1,13,2,24,128]{4,3,2,1,0:T(8,128)(2,1)S(1)}, u32[]{:S(2)}, u32[]{:S(2)}) collective-permute-start(bf16[1,13,2,24,128]{4,3,2,1,0:T(8,128)(2,1)S(1)} %get-tuple-element.53), channel_id=1, source_target_pairs={{0,0},{2,8},{4,12},{6,4},{8,2},{10,10},{12,14},{14,6},{16,24},{18,... | collective-permute-start | bytes 479240 | tf_op jit(solution)/shard_map/ppermute | solution.py:327
  115.5 14.4 %collective-permute-start.23 = (bf16[1,13,2,24,128]{4,3,2,1,0:T(8,128)(2,1)S(1)}, bf16[1,13,2,24,128]{4,3,2,1,0:T(8,128)(2,1)S(1)}, u32[]{:S(2)}, u32[]{:S(2)}) collective-permute-start(bf16[1,13,2,24,128]{4,3,2,1,0:T(8,128)(2,1)S(1)} %get-tuple-element.54), channel_id=1, source_target_pairs={{0,2},{2,10},{4,14},{6,6},{8,0},{10,8},{12,12},{14,4},{16,26},{18,... | collective-permute-start | bytes 479240 | tf_op jit(solution)/shard_map/ppermute | solution.py:327
  128.0 8.5 %collective-permute-start.11 = (bf16[1,13,2,24,128]{4,3,2,1,0:T(8,128)(2,1)S(1)}, bf16[1,13,2,24,128]{4,3,2,1,0:T(8,128)(2,1)S(1)}, u32[]{:S(2)}, u32[]{:S(2)}) collective-permute-start(bf16[1,13,2,24,128]{4,3,2,1,0:T(8,128)(2,1)S(1)} %get-tuple-element.45), channel_id=1, source_target_pairs={{0,0},{2,8},{4,12},{6,4},{8,2},{10,10},{12,14},{14,6},{16,24},{18,... | collective-permute-start | bytes 479240 | tf_op jit(solution)/shard_map/ppermute | solution.py:327
  129.9 9.0 %collective-permute-start.12 = (bf16[1,13,2,24,128]{4,3,2,1,0:T(8,128)(2,1)S(1)}, bf16[1,13,2,24,128]{4,3,2,1,0:T(8,128)(2,1)S(1)}, u32[]{:S(2)}, u32[]{:S(2)}) collective-permute-start(bf16[1,13,2,24,128]{4,3,2,1,0:T(8,128)(2,1)S(1)} %get-tuple-element.46), channel_id=1, source_target_pairs={{0,2},{2,10},{4,14},{6,6},{8,0},{10,8},{12,12},{14,4},{16,26},{18,... | collective-permute-start | bytes 479240 | tf_op jit(solution)/shard_map/ppermute | solution.py:327
  (9 other events, 167.7 us)

commit v3 on v2

--- a/solution.py
+++ b/solution.py
@@ -49,40 +49,75 @@
     w2[0:gap, block:] = jnp.zeros((gap, block), BF)
 
 
-def camera_pack_kernel(pos, x, *outs, tr, span):
+def camera_pack_kernel(pos, x, *refs, tr, span):
     frames, sc, ch, rows = x.shape
-    groups = len(outs)
+    groups = len(refs) // 2
+    outs, rims = refs[:groups], refs[groups:]
     width = frames * span
     place = pos[0]
     row = lax.broadcasted_iota(jnp.int32, (rows, width), 0)
     lane = lax.broadcasted_iota(jnp.int32, (rows, width), 1)
-    picks = []
+
+    def picks(f, targets):
+        parts = []
+        for target in targets:
+            start = target * tr - UP
+            parts.append(jnp.where(row + f * span == lane + start, jnp.where(lane // span == f, 1.0, 0.0), 0.0).astype(BF))
+        return jnp.concatenate(parts, axis=1)
+
+    main, rim = None, None
+    rightmost = lax.rem(place, groups) == groups - 1
     for f in range(frames):
-        parts = []
-        for p in range(groups):
-            start = lax.rem(place + p, groups) * tr - UP
-            parts.append(jnp.where(row + f * span == lane + start, jnp.where(lane // span == f, 1.0, 0.0), 0.0).astype(BF))
-        picks.append(jnp.concatenate(parts, axis=1))
-    y = None
-    for f in range(frames):
-        part = jnp.dot(x[f].reshape(sc * ch, rows), picks[f], preferred_element_type=jnp.float32)
-        y = part if y is None else y + part
+        pick = picks(f, [lax.rem(place + p, groups) for p in range(groups)])
+        part = jnp.dot(x[f].reshape(sc * ch, rows), pick, preferred_element_type=jnp.float32)
+        main = part if main is None else main + part
+        pick = picks(f, [lax.rem(e + jnp.where(rightmost, 0, 1), groups) for e in range(groups)])
+        border = jnp.where(rightmost, x[f, sc - UP : sc].astype(jnp.float32), x[f, 0:UP].astype(jnp.float32)).astype(BF)
+        part = jnp.dot(border.reshape(UP * ch, rows), pick, preferred_element_type=jnp.float32)
+        rim = part if rim is None else rim + part
     for p in range(groups):
-        outs[p][...] = y[:, p * width : (p + 1) * width].astype(BF).reshape(sc, ch, width)
+        outs[p][...] = main[:, p * width : (p + 1) * width].astype(BF).reshape(sc, ch, width)
+        rims[p][...] = rim[:, p * width : (p + 1) * width].astype(BF).reshape(UP, ch, width)
+
+
+def window_kernel(pos, x, *outs, tw):
+    n = x.shape[2] // tw
+    wide = tw + 2 * SIDE
+    edge = jnp.zeros((x.shape[1], SIDE, x.shape[3]), BF)
+    for d in range(len(outs)):
+        for c in range(n):
+
+            @pl.when(pos[d] == c)
+            def _():
+                lo, hi = max(c * tw - SIDE, 0), min((c + 1) * tw + SIDE, n * tw)
+                at = lo - (c * tw - SIDE)
+                if at:
+                    outs[d][0, :, 0:at, :] = edge
+                if at + hi - lo < wide:
+                    outs[d][0, :, at + hi - lo :, :] = edge
+                outs[d][0, :, at : at + hi - lo, :] = x[0, :, lo:hi, :]
 
 
 def camera_unpack_kernel(pos, *refs, groups, sc, cam_ch):
-    strips = refs[:groups]
-    left, right, out, stage, cells = refs[groups:]
+    strips, rims = refs[:groups], refs[groups : 2 * groups]
+    out, stage, cells = refs[2 * groups :]
     group = pos[0]
-    lanes = left.shape[2]
+    lanes = stage.shape[2]
     pitch = cells.shape[1]
     for p in range(groups):
         q = lax.rem(group - p + groups, groups)
         stage[pl.ds(UP + q * sc, sc)] = strips[p][...]
-    stage[0:UP] = left[...]
     n = UP + groups * sc + DOWN
-    stage[n - DOWN : n] = right[...]
+    for e in range(groups):
+
+        @pl.when(group == e)
+        def _():
+            stage[0:UP] = rims[e][...]
+
+        @pl.when(group == (e + 1) % groups)
+        def _():
+            stage[n - DOWN : n] = rims[e][0:DOWN]
+
     lead = SIDE - UP
     cells[:, 0:8, :] = jnp.zeros((lanes, 8, 128), jnp.float32)
     low = (lead + n) // 8 * 8
@@ -359,32 +394,30 @@
         lanes = frames * span
         turned = jnp.transpose(camera, (0, 2, 3, 1))
         strip = jax.ShapeDtypeStruct((sc, cam_ch, lanes), BF)
+        rim = jax.ShapeDtypeStruct((UP, cam_ch, lanes), BF)
         packed = pl.pallas_call(
             lambda *refs: camera_pack_kernel(*refs, tr=tr, span=span),
             grid_spec=pltpu.PrefetchScalarGridSpec(
                 num_scalar_prefetch=1,
                 grid=(1,),
                 in_specs=[whole(turned)],
-                out_specs=[whole(strip)] * groups,
+                out_specs=[whole(strip)] * groups + [whole(rim)] * groups,
             ),
-            out_shape=[strip] * groups,
+            out_shape=[strip] * groups + [rim] * groups,
             compiler_params=limit(14),
             name="camera_pack",
         )(place.reshape(1).astype(jnp.int32), turned)
-        lidar, packed = lax.optimization_barrier((lidar, packed))
-        arrived = [
-            send(packed[p], [(s, seat((s + p) % groups, s // groups)) for s in range(total)])
-            for p in range(groups)
-        ]
-        tail, head = pick(arrived, (group + 1) % groups, group, 0)
-        left = across(tail, 0, 1)
-        right = across(head, 0, -1)
+        arrived = [send(packed[p], [(s, seat((s + p) % groups, s // groups)) for s in range(total)]) for p in range(groups)]
+        for e in range(groups):
+            pairs = [(groups * j + groups - 1, seat(e, j + 1)) for j in range(members - 1)]
+            pairs += [(groups * j, seat((e + 1) % groups, j - 1)) for j in range(1, members)]
+            arrived.append(send(packed[groups + e], pairs))
         cam = pl.pallas_call(
             lambda *refs: camera_unpack_kernel(*refs, groups=groups, sc=sc, cam_ch=cam_ch),
             grid_spec=pltpu.PrefetchScalarGridSpec(
                 num_scalar_prefetch=1,
                 grid=(1,),
-                in_specs=[whole(x) for x in arrived] + [whole(left), whole(right)],
+                in_specs=[whole(x) for x in arrived],
                 out_specs=pl.BlockSpec((lanes, pitch, rounded(3 * cam_ch, 256)), lambda i, p: (0, 0, 0)),
                 scratch_shapes=[
                     pltpu.VMEM((tw + UP + DOWN, cam_ch, lanes), BF),
@@ -394,10 +427,9 @@
             out_shape=jax.ShapeDtypeStruct((lanes, pitch, rounded(3 * cam_ch, 256)), BF),
             compiler_params=limit(16),
             name="camera_unpack",
-        )(group.reshape(1).astype(jnp.int32), *arrived, left, right)
+        )(group.reshape(1).astype(jnp.int32), *arrived)
         cam = cam.reshape(frames, span, pitch, -1)
 
-        padded = jnp.pad(lidar, ((0, 0), (0, 0), (SIDE, SIDE), (0, 0)))
         pos = jnp.stack([group, member, kgroup, column_of(member)]).astype(jnp.int32)
         pairs2 = (tr + 2) // 2
         half_rows = tr // 2
@@ -409,12 +441,24 @@
         encoded = None
         step = frames // CHUNKS
         for f0 in range(0, frames, step):
-            windows = []
-            for d in range(members):
-                x = lax.dynamic_slice(padded, (f0, 0, column_of((member + d) % members) * tw, 0), (step, sh, wide, lidar_ch))
-                if d:
-                    x = send(x, [(g * members + j, g * members + (j + d) % members) for g in range(groups) for j in range(members)])
-                windows.append(x)
+            source = lidar if not f0 else lax.optimization_barrier((lidar, packed[0]))[0]
+            window = jax.ShapeDtypeStruct((step, sh, wide, lidar_ch), BF)
+            windows = pl.pallas_call(
+                functools.partial(window_kernel, tw=tw),
+                grid_spec=pltpu.PrefetchScalarGridSpec(
+                    num_scalar_prefetch=1,
+                    grid=(step,),
+                    in_specs=[pl.BlockSpec((1, sh, cols, lidar_ch), lambda f, p, f0=f0: (f + f0, 0, 0, 0))],
+                    out_specs=[framed(window)] * members,
+                ),
+                out_shape=[window] * members,
+                compiler_params=limit(6),
+                name="windows",
+            )(jnp.stack([column_of((member + d) % members) for d in range(members)]).astype(jnp.int32), source)
+            windows = [windows[0]] + [
+                send(windows[d], [(g * members + m, g * members + (m + d) % members) for g in range(groups) for m in range(members)])
+                for d in range(1, members)
+            ]
             last, head = pick(windows, (member + 1) % members, member, 1)
             above = across(last, 1, 0)
             below = across(head, -1, 0)

time: 141 us -> 136 us (0.965)
  the two profiles are of different devices: /device:TPU:2 before, /device:TPU:0 now
where the time goes in v3:
time: 136 us; the launch traced here: 133 us
  starting transfers between devices  77.2 us (57%)
  Pallas kernels  44.9 us (33%)
  local copies, waits for them, and re-layouts  5.48 us (4%)
  waiting for transfers between devices  4.83 us (4%)
    ppermute x26, starting transfers between devices, send(): return lax.ppermute(x, AXES, pairs)  77.2 us
    pallas_call x4, Pallas kernels, local(): pl.pallas_call(functools.partial(conv_kernel, parts=members, sh=sh, tr=tr...  25 us
    pallas_call x4, Pallas kernels, local(): pl.pallas_call(lambda *refs: encode_kernel(*refs, parts=HALVES, half_rows...  6.16 us
    pallas_call x1, Pallas kernels, local(): pl.pallas_call(lambda *refs: camera_unpack_kernel(*refs, groups=groups, s...  5.89 us
    unnamed x40, local copies, waits for them, and re-layouts  5.48 us
    ppermute x26, waiting for transfers between devices, send(): return lax.ppermute(x, AXES, pairs)  4.83 us
    pallas_call x2, Pallas kernels, local(): pl.pallas_call(functools.partial(window_kernel, tw=tw), grid_spec=pltpu.P...  2.78 us
  transfers between devices with their start and end apart: 26, of which 3 were waited for; matrix products, arithmetic and copies ran while one was open for 0% of the time, Pallas kernels for 31%

profile of v3, /device:TPU:0, one launch (start us, length us, event | category | flops | bytes accessed | tf_op | source)
XLA Modules:
  0.0 133.3 jit_solution(14828112610426963524)
XLA Ops:
  1.2 2.2 %camera_pack.1 = (bf16[12,80,128]{2,1,0:T(8,128)(2,1)S(1)}, bf16[12,80,128]{2,1,0:T(8,128)(2,1)S(1)}, bf16[12,80,128]{2,1,0:T(8,128)(2,1)}, bf16[12,80,128]{2,1,...) custom-call(s32[1]{0:T(128)} %bitcast.9.refs_0_, ...), custom_call_target="tpu_custom_call" | custom-call | tf_op jit(solution)/shard_map/camera_pack/pallas_call | solution.py:398
  4.7 6.8 %collective-permute-start.6 = (bf16[12,80,128]{2,1,0:T(8,128)(2,1)S(1)}, bf16[12,80,128]{2,1,0:T(8,128)(2,1)S(1)}, u32[]{:S(2)}, u32[]{:S(2)}) collective-permute-start(bf16[12,80,128]{2,1,0:T(8,128)(2,1)S(1)} %get-tuple-element.44), channel_id=1, source_target_pairs={{0,8},{2,18},{4,26},{6,0},{8,14},{10,20},{12,28},{14,6},{16,10},{1... | collective-permute-start | bytes 737288 | tf_op jit(solution)/shard_map/ppermute | solution.py:362
  14.3 1.7 %copy-done = bf16[4,6,192,256]{3,2,1,0:T(8,128)(2,1)S(1)} copy-done((bf16[4,6,192,256]{3,2,1,0:T(8,128)(2,1)S(1)}, bf16[4,6,192,256]{3,2,1,0:T(8,128)(2,1)}, u32[]{:S(2)}) %copy-start) | copy-done | bytes 2359320
  17.6 2.2 %collective-permute-start = (bf16[2,6,56,256]{3,2,1,0:T(8,128)(2,1)S(1)}, bf16[2,6,56,256]{3,2,1,0:T(8,128)(2,1)S(1)}, u32[]{:S(2)}, u32[]{:S(2)}) collective-permute-start(bf16[2,6,56,256]{3,2,1,0:T(8,128)(2,1)S(1)} %get-tuple-element.39), channel_id=1, source_target_pairs={{0,2},{2,4},{4,6},{6,0},{8,10},{10,12},{12,14},{14,8},{16,18},{18,... | collective-permute-start | bytes 1032200 | tf_op jit(solution)/shard_map/ppermute | solution.py:362
  20.5 7.1 %collective-permute-start.1 = (bf16[2,6,56,256]{3,2,1,0:T(8,128)(2,1)S(1)}, bf16[2,6,56,256]{3,2,1,0:T(8,128)(2,1)S(1)}, u32[]{:S(2)}, u32[]{:S(2)}) collective-permute-start(bf16[2,6,56,256]{3,2,1,0:T(8,128)(2,1)S(1)} %get-tuple-element.40), channel_id=1, source_target_pairs={{0,4},{2,6},{4,0},{6,2},{8,12},{10,14},{12,8},{14,10},{16,20},{18,... | collective-permute-start | bytes 1032200 | tf_op jit(solution)/shard_map/ppermute | solution.py:362
  29.7 4.3 %collective-permute-start.7 = (bf16[12,80,128]{2,1,0:T(8,128)(2,1)}, bf16[12,80,128]{2,1,0:T(8,128)(2,1)}, u32[]{:S(2)}, u32[]{:S(2)}) collective-permute-start(bf16[12,80,128]{2,1,0:T(8,128)(2,1)} %get-tuple-element.45), channel_id=1, source_target_pairs={{0,18},{2,26},{4,0},{6,8},{8,20},{10,28},{12,6},{14,14},{16,16},{1... | collective-permute-start | bytes 737288 | tf_op jit(solution)/shard_map/ppermute | solution.py:362
  35.2 1.8 %windows.3 = (bf16[2,6,56,256]{3,2,1,0:T(8,128)(2,1)S(1)}, bf16[2,6,56,256]{3,2,1,0:T(8,128)(2,1)}, bf16[2,6,56,256]{3,2,1,0:T(8,128)(2,1)}, bf16[2,6,56,256]{3,2,1,0:T(8,128)(2,1)}) custom-call(s32[4]{0:T(128)S(1)} %pad_add_fusion.1.pos, bf16[4,6,192,256]{3,2,1,0:T(8,128)(2,1)S(1)} %copy-done), custom_call_target="tpu_custom_call" | custom-call | tf_op jit(solution)/shard_map/windows/pallas_call | solution.py:446
  38.5 2.0 %collective-permute-start.18 = (bf16[2,6,56,256]{3,2,1,0:T(8,128)(2,1)}, bf16[2,6,56,256]{3,2,1,0:T(8,128)(2,1)}, u32[]{:S(2)}, u32[]{:S(2)}) collective-permute-start(bf16[2,6,56,256]{3,2,1,0:T(8,128)(2,1)} %get-tuple-element.59), channel_id=1, source_target_pairs={{0,4},{2,6},{4,0},{6,2},{8,12},{10,14},{12,8},{14,10},{16,20},{18,... | collective-permute-start | bytes 1032200 | tf_op jit(solution)/shard_map/ppermute | solution.py:362
  40.5 2.8 %collective-permute-done.2.refs_3_.refs_7_ = bf16[2,6,56,256]{3,2,1,0:T(8,128)(2,1)S(1)} collective-permute-done((bf16[2,6,56,256]{3,2,1,0:T(8,128)(2,1)S(1)}, bf16[2,6,56,256]{3,2,1,0:T(8,128)(2,1)S(1)}, u32[]{:S(2)}, u32[]{:S(2)}) %collective-permute-start.2) | collective-permute-done | bytes 344096 | tf_op jit(solution)/shard_map/ppermute | solution.py:362
  43.4 3.4 %collective-permute-start.19 = (bf16[2,6,56,256]{3,2,1,0:T(8,128)(2,1)}, bf16[2,6,56,256]{3,2,1,0:T(8,128)(2,1)}, u32[]{:S(2)}, u32[]{:S(2)}) collective-permute-start(bf16[2,6,56,256]{3,2,1,0:T(8,128)(2,1)} %get-tuple-element.60), channel_id=1, source_target_pairs={{0,6},{2,0},{4,2},{6,4},{8,14},{10,8},{12,10},{14,12},{16,22},{18,... | collective-permute-start | bytes 1032200 | tf_op jit(solution)/shard_map/ppermute | solution.py:362
  47.5 1.6 %collective-permute-done.7.refs_3_ = bf16[12,80,128]{2,1,0:T(8,128)(2,1)} collective-permute-done((bf16[12,80,128]{2,1,0:T(8,128)(2,1)}, bf16[12,80,128]{2,1,0:T(8,128)(2,1)}, u32[]{:S(2)}, u32[]{:S(2)}) %collective-permute-start.7) | collective-permute-done | bytes 245792 | tf_op jit(solution)/shard_map/ppermute | solution.py:362
  49.2 5.8 %collective-permute-start.3 = (bf16[2,3,56,256]{3,2,1,0:T(8,128)(2,1)S(1)}, bf16[2,3,56,256]{3,2,1,0:T(8,128)(2,1)S(1)}, u32[]{:S(2)}, u32[]{:S(2)}) collective-permute-start(bf16[2,3,56,256]{3,2,1,0:T(8,128)(2,1)S(1)} %get-tuple-element.42), channel_id=1, source_target_pairs={{0,8},{6,14},{2,10},{4,12},{8,18},{14,20},{10,16},{12,22},{18,26},... | collective-permute-start | bytes 516104 | tf_op jit(solution)/shard_map/ppermute | solution.py:362
  56.8 5.9 %camera_unpack.1 = bf16[128,64,256]{2,1,0:T(8,128)(2,1)S(1)} custom-call(s32[1]{0:T(128)} %bitcast.1.refs_0_, bf16[12,80,128]{2,1,0:T(8,128)(2,1)S(1)} %collective-permute-done.5.refs_1_, bf16[12,80,128]{2,1,0:T(8,128)(2,1)S(1)} %copy-done.7, bf16[12,80,128]{2,1,0:T(8,128)(2,1)} %collective-permute-done.7.refs_3_, ...), custom_call_target="tpu_custom_call" | custom-call | tf_op jit(solution)/shard_map/camera_unpack/pallas_call | solution.py:415
  63.1 1.9 %shard_map.103 = (bf16[2,3,56,256]{3,2,1,0:T(8,128)(2,1)S(1)}, bf16[2,2,56,256]{3,2,1,0:T(8,128)(2,1)S(1)}) custom-call(s32[2]{0:T(128)S(1)} %pad_add_fusion.2.pos, bf16[2,6,56,256]{3,2,1,0:T(8,128)(2,1)S(1)} %get-tuple-element.57.refs_0_.refs_4_, bf16[2,6,56,256]{3,2,1,0:T(8,128)(2,1)} %collective-permute-done.17.refs_1_.refs_5_, ...), custom_call_target="tpu_custom_call" | custom-call | tf_op jit(solution)/shard_map/pallas_call | solution.py:172
  64.9 9.1 %collective-permute-start.20 = (bf16[2,3,56,256]{3,2,1,0:T(8,128)(2,1)S(1)}, bf16[2,3,56,256]{3,2,1,0:T(8,128)(2,1)S(1)}, u32[]{:S(2)}, u32[]{:S(2)}) collective-permute-start(bf16[2,3,56,256]{3,2,1,0:T(8,128)(2,1)S(1)} %get-tuple-element.61), channel_id=1, source_target_pairs={{0,8},{6,14},{2,10},{4,12},{8,18},{14,20},{10,16},{12,22},{18,26},... | collective-permute-start | bytes 516104 | tf_op jit(solution)/shard_map/ppermute | solution.py:362
  75.4 5.9 %shard_map.102 = (bf16[1,13,2,24,128]{4,3,2,1,0:T(8,128)(2,1)S(1)}, bf16[1,13,2,24,128]{4,3,2,1,0:T(8,128)(2,1)S(1)}) custom-call(s32[4]{0:T(128)S(1)} %pad_add_fusion.pos, bf16[2,6,56,256]{3,2,1,0:T(8,128)(2,1)S(1)} %get-tuple-element.38.refs_0_.refs_4_, bf16[2,6,56,256]{3,2,1,0:T(8,128)(2,1)S(1)} %collective-permute-done.refs_1_.refs_5_, ...), custom_call_target="tpu_custom_call" | custom-call | flops 4127195136 | bytes 2000000 | tf_op jit(solution)/shard_map/pallas_call | solution.py:466
  82.0 8.6 %collective-permute-start.16 = (bf16[1,13,2,24,128]{4,3,2,1,0:T(8,128)(2,1)S(1)}, bf16[1,13,2,24,128]{4,3,2,1,0:T(8,128)(2,1)S(1)}, u32[]{:S(2)}, u32[]{:S(2)}) collective-permute-start(bf16[1,13,2,24,128]{4,3,2,1,0:T(8,128)(2,1)S(1)} %get-tuple-element.56), channel_id=1, source_target_pairs={{0,2},{2,10},{4,14},{6,6},{8,0},{10,8},{12,12},{14,4},{16,26},{18,... | collective-permute-start | bytes 479240 | tf_op jit(solution)/shard_map/ppermute | solution.py:362
  90.6 6.6 %shard_map.104 = (bf16[1,13,2,24,128]{4,3,2,1,0:T(8,128)(2,1)S(1)}, bf16[1,13,2,24,128]{4,3,2,1,0:T(8,128)(2,1)S(1)}) custom-call(s32[4]{0:T(128)S(1)} %pad_add_fusion.pos, bf16[2,6,56,256]{3,2,1,0:T(8,128)(2,1)S(1)} %get-tuple-element.57.refs_0_.refs_4_, bf16[2,6,56,256]{3,2,1,0:T(8,128)(2,1)} %collective-permute-done.17.refs_1_.refs_5_, ...), custom_call_target="tpu_custom_call" | custom-call | flops 4127195136 | bytes 2000000 | tf_op jit(solution)/shard_map/pallas_call | solution.py:466
  97.9 5.0 %collective-permute-start.23 = (bf16[1,13,2,24,128]{4,3,2,1,0:T(8,128)(2,1)S(1)}, bf16[1,13,2,24,128]{4,3,2,1,0:T(8,128)(2,1)S(1)}, u32[]{:S(2)}, u32[]{:S(2)}) collective-permute-start(bf16[1,13,2,24,128]{4,3,2,1,0:T(8,128)(2,1)S(1)} %get-tuple-element.64), channel_id=1, source_target_pairs={{0,2},{2,10},{4,14},{6,6},{8,0},{10,8},{12,12},{14,4},{16,26},{18,... | collective-permute-start | bytes 479240 | tf_op jit(solution)/shard_map/ppermute | solution.py:362
  102.9 6.6 %shard_map.105 = (bf16[1,13,2,24,128]{4,3,2,1,0:T(8,128)(2,1)S(1)}, bf16[1,13,2,24,128]{4,3,2,1,0:T(8,128)(2,1)S(1)}) custom-call(s32[4]{0:T(128)S(1)} %pad_add_fusion.pos, bf16[2,6,56,256]{3,2,1,0:T(8,128)(2,1)S(1)} %get-tuple-element.57.refs_0_.refs_4_, bf16[2,6,56,256]{3,2,1,0:T(8,128)(2,1)} %collective-permute-done.17.refs_1_.refs_5_, ...), custom_call_target="tpu_custom_call" | custom-call | flops 4127195136 | bytes 2000000 | tf_op jit(solution)/shard_map/pallas_call | solution.py:466
  110.2 5.6 %collective-permute-start.25 = (bf16[1,13,2,24,128]{4,3,2,1,0:T(8,128)(2,1)S(1)}, bf16[1,13,2,24,128]{4,3,2,1,0:T(8,128)(2,1)S(1)}, u32[]{:S(2)}, u32[]{:S(2)}) collective-permute-start(bf16[1,13,2,24,128]{4,3,2,1,0:T(8,128)(2,1)S(1)} %get-tuple-element.66), channel_id=1, source_target_pairs={{0,2},{2,10},{4,14},{6,6},{8,0},{10,8},{12,12},{14,4},{16,26},{18,... | collective-permute-start | bytes 479240 | tf_op jit(solution)/shard_map/ppermute | solution.py:362
  115.8 5.9 %shard_map.101 = (bf16[1,13,2,24,128]{4,3,2,1,0:T(8,128)(2,1)S(1)}, bf16[1,13,2,24,128]{4,3,2,1,0:T(8,128)(2,1)S(1)}) custom-call(s32[4]{0:T(128)S(1)} %pad_add_fusion.pos, bf16[2,6,56,256]{3,2,1,0:T(8,128)(2,1)S(1)} %get-tuple-element.38.refs_0_.refs_4_, bf16[2,6,56,256]{3,2,1,0:T(8,128)(2,1)S(1)} %collective-permute-done.refs_1_.refs_5_, ...), custom_call_target="tpu_custom_call" | custom-call | flops 4127195136 | bytes 2000000 | tf_op jit(solution)/shard_map/pallas_call | solution.py:466
  122.4 4.7 %collective-permute-start.14 = (bf16[1,13,2,24,128]{4,3,2,1,0:T(8,128)(2,1)S(1)}, bf16[1,13,2,24,128]{4,3,2,1,0:T(8,128)(2,1)S(1)}, u32[]{:S(2)}, u32[]{:S(2)}) collective-permute-start(bf16[1,13,2,24,128]{4,3,2,1,0:T(8,128)(2,1)S(1)} %get-tuple-element.54), channel_id=1, source_target_pairs={{0,2},{2,10},{4,14},{6,6},{8,0},{10,8},{12,12},{14,4},{16,26},{18,... | collective-permute-start | bytes 479240 | tf_op jit(solution)/shard_map/ppermute | solution.py:362
  127.1 1.5 %shard_map.106.refs_7_ = bf16[4,24,2,24,256]{4,3,2,1,0:T(8,128)(2,1)} custom-call(s32[1]{0:T(128)} %bitcast.refs_0_, bf16[1,13,2,24,128]{4,3,2,1,0:T(8,128)(2,1)S(1)} %collective-permute-done.24.refs_1_, bf16[1,13,2,24,128]{4,3,2,1,0:T(8,128)(2,1)S(1)} %collective-permute-done.25.refs_2_, bf16[1152,256]{1,0:T(8,128)(2,1)S(1)} %bitcast.21, ...), custom_call_target="tpu_custom_call" | custom-call | flops 226492416 | bytes 1000000 | tf_op jit(solution)/shard_map/pallas_call | solution.py:484
  (87 shorter events, 23.8 us)
Async XLA Ops:
  3.4 9.6 %collective-permute-start.9 = (bf16[3,80,128]{2,1,0:T(8,128)(2,1)S(1)}, bf16[3,80,128]{2,1,0:T(8,128)(2,1)S(1)}, u32[]{:S(2)}, u32[]{:S(2)}) collective-permute-start(bf16[3,80,128]{2,1,0:T(8,128)(2,1)S(1)} %get-tuple-element.47), channel_id=1, source_target_pairs={{6,6},{14,2},{22,4},{8,8},{16,14},{24,10},{7,7},{15,3},{23,5},{9,9... | collective-permute-start | bytes 184328 | tf_op jit(solution)/shard_map/ppermute | solution.py:362
  4.0 25.7 %collective-permute-start.5 = (bf16[12,80,128]{2,1,0:T(8,128)(2,1)S(1)}, bf16[12,80,128]{2,1,0:T(8,128)(2,1)S(1)}, u32[]{:S(2)}, u32[]{:S(2)}) collective-permute-start(bf16[12,80,128]{2,1,0:T(8,128)(2,1)S(1)} %get-tuple-element.36), channel_id=1, source_target_pairs={{0,0},{2,8},{4,18},{6,26},{8,6},{10,14},{12,20},{14,28},{16,2},{18... | collective-permute-start | bytes 737288 | tf_op jit(solution)/shard_map/ppermute | solution.py:362
  4.7 29.3 %collective-permute-start.6 = (bf16[12,80,128]{2,1,0:T(8,128)(2,1)S(1)}, bf16[12,80,128]{2,1,0:T(8,128)(2,1)S(1)}, u32[]{:S(2)}, u32[]{:S(2)}) collective-permute-start(bf16[12,80,128]{2,1,0:T(8,128)(2,1)S(1)} %get-tuple-element.44), channel_id=1, source_target_pairs={{0,8},{2,18},{4,26},{6,0},{8,14},{10,20},{12,28},{14,6},{16,10},{1... | collective-permute-start | bytes 737288 | tf_op jit(solution)/shard_map/ppermute | solution.py:362
  13.0 14.6 %collective-permute-start.12 = (bf16[3,80,128]{2,1,0:T(8,128)(2,1)S(1)}, bf16[3,80,128]{2,1,0:T(8,128)(2,1)S(1)}, u32[]{:S(2)}, u32[]{:S(2)}) collective-permute-start(bf16[3,80,128]{2,1,0:T(8,128)(2,1)S(1)} %get-tuple-element.50), channel_id=1, source_target_pairs={{6,28},{14,24},{22,30},{8,0},{16,6},{24,2},{7,29},{15,25},{23,31},... | collective-permute-start | bytes 184328 | tf_op jit(solution)/shard_map/ppermute | solution.py:362
  17.6 19.4 %collective-permute-start = (bf16[2,6,56,256]{3,2,1,0:T(8,128)(2,1)S(1)}, bf16[2,6,56,256]{3,2,1,0:T(8,128)(2,1)S(1)}, u32[]{:S(2)}, u32[]{:S(2)}) collective-permute-start(bf16[2,6,56,256]{3,2,1,0:T(8,128)(2,1)S(1)} %get-tuple-element.39), channel_id=1, source_target_pairs={{0,2},{2,4},{4,6},{6,0},{8,10},{10,12},{12,14},{14,8},{16,18},{18,... | collective-permute-start | bytes 1032200 | tf_op jit(solution)/shard_map/ppermute | solution.py:362
  20.5 18.1 %collective-permute-start.1 = (bf16[2,6,56,256]{3,2,1,0:T(8,128)(2,1)S(1)}, bf16[2,6,56,256]{3,2,1,0:T(8,128)(2,1)S(1)}, u32[]{:S(2)}, u32[]{:S(2)}) collective-permute-start(bf16[2,6,56,256]{3,2,1,0:T(8,128)(2,1)S(1)} %get-tuple-element.40), channel_id=1, source_target_pairs={{0,4},{2,6},{4,0},{6,2},{8,12},{10,14},{12,8},{14,10},{16,20},{18,... | collective-permute-start | bytes 1032200 | tf_op jit(solution)/shard_map/ppermute | solution.py:362
  28.2 15.2 %collective-permute-start.2 = (bf16[2,6,56,256]{3,2,1,0:T(8,128)(2,1)S(1)}, bf16[2,6,56,256]{3,2,1,0:T(8,128)(2,1)S(1)}, u32[]{:S(2)}, u32[]{:S(2)}) collective-permute-start(bf16[2,6,56,256]{3,2,1,0:T(8,128)(2,1)S(1)} %get-tuple-element.41), channel_id=1, source_target_pairs={{0,6},{2,0},{4,2},{6,4},{8,14},{10,8},{12,10},{14,12},{16,22},{18,... | collective-permute-start | bytes 1032200 | tf_op jit(solution)/shard_map/ppermute | solution.py:362
  29.7 19.5 %collective-permute-start.7 = (bf16[12,80,128]{2,1,0:T(8,128)(2,1)}, bf16[12,80,128]{2,1,0:T(8,128)(2,1)}, u32[]{:S(2)}, u32[]{:S(2)}) collective-permute-start(bf16[12,80,128]{2,1,0:T(8,128)(2,1)} %get-tuple-element.45), channel_id=1, source_target_pairs={{0,18},{2,26},{4,0},{6,8},{8,20},{10,28},{12,6},{14,14},{16,16},{1... | collective-permute-start | bytes 737288 | tf_op jit(solution)/shard_map/ppermute | solution.py:362
  34.7 20.3 %collective-permute-start.8 = (bf16[12,80,128]{2,1,0:T(8,128)(2,1)}, bf16[12,80,128]{2,1,0:T(8,128)(2,1)}, u32[]{:S(2)}, u32[]{:S(2)}) collective-permute-start(bf16[12,80,128]{2,1,0:T(8,128)(2,1)} %get-tuple-element.46), channel_id=1, source_target_pairs={{0,26},{2,0},{4,8},{6,18},{8,28},{10,6},{12,14},{14,20},{16,24},{1... | collective-permute-start | bytes 737288 | tf_op jit(solution)/shard_map/ppermute | solution.py:362
  37.0 25.7 %collective-permute-start.17 = (bf16[2,6,56,256]{3,2,1,0:T(8,128)(2,1)}, bf16[2,6,56,256]{3,2,1,0:T(8,128)(2,1)}, u32[]{:S(2)}, u32[]{:S(2)}) collective-permute-start(bf16[2,6,56,256]{3,2,1,0:T(8,128)(2,1)} %get-tuple-element.58), channel_id=1, source_target_pairs={{0,2},{2,4},{4,6},{6,0},{8,10},{10,12},{12,14},{14,8},{16,18},{18,... | collective-permute-start | bytes 1032200 | tf_op jit(solution)/shard_map/ppermute | solution.py:362
  38.5 24.2 %collective-permute-start.18 = (bf16[2,6,56,256]{3,2,1,0:T(8,128)(2,1)}, bf16[2,6,56,256]{3,2,1,0:T(8,128)(2,1)}, u32[]{:S(2)}, u32[]{:S(2)}) collective-permute-start(bf16[2,6,56,256]{3,2,1,0:T(8,128)(2,1)} %get-tuple-element.59), channel_id=1, source_target_pairs={{0,4},{2,6},{4,0},{6,2},{8,12},{10,14},{12,8},{14,10},{16,20},{18,... | collective-permute-start | bytes 1032200 | tf_op jit(solution)/shard_map/ppermute | solution.py:362
  43.4 19.7 %collective-permute-start.19 = (bf16[2,6,56,256]{3,2,1,0:T(8,128)(2,1)}, bf16[2,6,56,256]{3,2,1,0:T(8,128)(2,1)}, u32[]{:S(2)}, u32[]{:S(2)}) collective-permute-start(bf16[2,6,56,256]{3,2,1,0:T(8,128)(2,1)} %get-tuple-element.60), channel_id=1, source_target_pairs={{0,6},{2,0},{4,2},{6,4},{8,14},{10,8},{12,10},{14,12},{16,22},{18,... | collective-permute-start | bytes 1032200 | tf_op jit(solution)/shard_map/ppermute | solution.py:362
  49.2 26.2 %collective-permute-start.3 = (bf16[2,3,56,256]{3,2,1,0:T(8,128)(2,1)S(1)}, bf16[2,3,56,256]{3,2,1,0:T(8,128)(2,1)S(1)}, u32[]{:S(2)}, u32[]{:S(2)}) collective-permute-start(bf16[2,3,56,256]{3,2,1,0:T(8,128)(2,1)S(1)} %get-tuple-element.42), channel_id=1, source_target_pairs={{0,8},{6,14},{2,10},{4,12},{8,18},{14,20},{10,16},{12,22},{18,26},... | collective-permute-start | bytes 516104 | tf_op jit(solution)/shard_map/ppermute | solution.py:362
  55.0 20.4 %collective-permute-start.4 = (bf16[2,2,56,256]{3,2,1,0:T(8,128)(2,1)S(1)}, bf16[2,2,56,256]{3,2,1,0:T(8,128)(2,1)S(1)}, u32[]{:S(2)}, u32[]{:S(2)}) collective-permute-start(bf16[2,2,56,256]{3,2,1,0:T(8,128)(2,1)S(1)} %get-tuple-element.43), channel_id=1, source_target_pairs={{8,0},{14,6},{10,2},{12,4},{18,8},{20,14},{16,10},{22,12},{26,18},... | collective-permute-start | bytes 344072 | tf_op jit(solution)/shard_map/ppermute | solution.py:362
  64.9 25.7 %collective-permute-start.20 = (bf16[2,3,56,256]{3,2,1,0:T(8,128)(2,1)S(1)}, bf16[2,3,56,256]{3,2,1,0:T(8,128)(2,1)S(1)}, u32[]{:S(2)}, u32[]{:S(2)}) collective-permute-start(bf16[2,3,56,256]{3,2,1,0:T(8,128)(2,1)S(1)} %get-tuple-element.61), channel_id=1, source_target_pairs={{0,8},{6,14},{2,10},{4,12},{8,18},{14,20},{10,16},{12,22},{18,26},... | collective-permute-start | bytes 516104 | tf_op jit(solution)/shard_map/ppermute | solution.py:362
  74.1 16.5 %collective-permute-start.21 = (bf16[2,2,56,256]{3,2,1,0:T(8,128)(2,1)S(1)}, bf16[2,2,56,256]{3,2,1,0:T(8,128)(2,1)S(1)}, u32[]{:S(2)}, u32[]{:S(2)}) collective-permute-start(bf16[2,2,56,256]{3,2,1,0:T(8,128)(2,1)S(1)} %get-tuple-element.62), channel_id=1, source_target_pairs={{8,0},{14,6},{10,2},{12,4},{18,8},{20,14},{16,10},{22,12},{26,18},... | collective-permute-start | bytes 344072 | tf_op jit(solution)/shard_map/ppermute | solution.py:362
  81.3 48.9 %collective-permute-start.15 = (bf16[1,13,2,24,128]{4,3,2,1,0:T(8,128)(2,1)S(1)}, bf16[1,13,2,24,128]{4,3,2,1,0:T(8,128)(2,1)S(1)}, u32[]{:S(2)}, u32[]{:S(2)}) collective-permute-start(bf16[1,13,2,24,128]{4,3,2,1,0:T(8,128)(2,1)S(1)} %get-tuple-element.55), channel_id=1, source_target_pairs={{0,0},{2,8},{4,12},{6,4},{8,2},{10,10},{12,14},{14,6},{16,24},{18,... | collective-permute-start | bytes 479240 | tf_op jit(solution)/shard_map/ppermute | solution.py:362
  82.0 48.2 %collective-permute-start.16 = (bf16[1,13,2,24,128]{4,3,2,1,0:T(8,128)(2,1)S(1)}, bf16[1,13,2,24,128]{4,3,2,1,0:T(8,128)(2,1)S(1)}, u32[]{:S(2)}, u32[]{:S(2)}) collective-permute-start(bf16[1,13,2,24,128]{4,3,2,1,0:T(8,128)(2,1)S(1)} %get-tuple-element.56), channel_id=1, source_target_pairs={{0,2},{2,10},{4,14},{6,6},{8,0},{10,8},{12,12},{14,4},{16,26},{18,... | collective-permute-start | bytes 479240 | tf_op jit(solution)/shard_map/ppermute | solution.py:362
  97.2 12.9 %collective-permute-start.22 = (bf16[1,13,2,24,128]{4,3,2,1,0:T(8,128)(2,1)S(1)}, bf16[1,13,2,24,128]{4,3,2,1,0:T(8,128)(2,1)S(1)}, u32[]{:S(2)}, u32[]{:S(2)}) collective-permute-start(bf16[1,13,2,24,128]{4,3,2,1,0:T(8,128)(2,1)S(1)} %get-tuple-element.63), channel_id=1, source_target_pairs={{0,0},{2,8},{4,12},{6,4},{8,2},{10,10},{12,14},{14,6},{16,24},{18,... | collective-permute-start | bytes 479240 | tf_op jit(solution)/shard_map/ppermute | solution.py:362
  97.9 30.8 %collective-permute-start.23 = (bf16[1,13,2,24,128]{4,3,2,1,0:T(8,128)(2,1)S(1)}, bf16[1,13,2,24,128]{4,3,2,1,0:T(8,128)(2,1)S(1)}, u32[]{:S(2)}, u32[]{:S(2)}) collective-permute-start(bf16[1,13,2,24,128]{4,3,2,1,0:T(8,128)(2,1)S(1)} %get-tuple-element.64), channel_id=1, source_target_pairs={{0,2},{2,10},{4,14},{6,6},{8,0},{10,8},{12,12},{14,4},{16,26},{18,... | collective-permute-start | bytes 479240 | tf_op jit(solution)/shard_map/ppermute | solution.py:362
  109.4 12.3 %collective-permute-start.24 = (bf16[1,13,2,24,128]{4,3,2,1,0:T(8,128)(2,1)S(1)}, bf16[1,13,2,24,128]{4,3,2,1,0:T(8,128)(2,1)S(1)}, u32[]{:S(2)}, u32[]{:S(2)}) collective-permute-start(bf16[1,13,2,24,128]{4,3,2,1,0:T(8,128)(2,1)S(1)} %get-tuple-element.65), channel_id=1, source_target_pairs={{0,0},{2,8},{4,12},{6,4},{8,2},{10,10},{12,14},{14,6},{16,24},{18,... | collective-permute-start | bytes 479240 | tf_op jit(solution)/shard_map/ppermute | solution.py:362
  110.2 12.2 %collective-permute-start.25 = (bf16[1,13,2,24,128]{4,3,2,1,0:T(8,128)(2,1)S(1)}, bf16[1,13,2,24,128]{4,3,2,1,0:T(8,128)(2,1)S(1)}, u32[]{:S(2)}, u32[]{:S(2)}) collective-permute-start(bf16[1,13,2,24,128]{4,3,2,1,0:T(8,128)(2,1)S(1)} %get-tuple-element.66), channel_id=1, source_target_pairs={{0,2},{2,10},{4,14},{6,6},{8,0},{10,8},{12,12},{14,4},{16,26},{18,... | collective-permute-start | bytes 479240 | tf_op jit(solution)/shard_map/ppermute | solution.py:362
  121.7 10.1 %collective-permute-start.13 = (bf16[1,13,2,24,128]{4,3,2,1,0:T(8,128)(2,1)S(1)}, bf16[1,13,2,24,128]{4,3,2,1,0:T(8,128)(2,1)S(1)}, u32[]{:S(2)}, u32[]{:S(2)}) collective-permute-start(bf16[1,13,2,24,128]{4,3,2,1,0:T(8,128)(2,1)S(1)} %get-tuple-element.53), channel_id=1, source_target_pairs={{0,0},{2,8},{4,12},{6,4},{8,2},{10,10},{12,14},{14,6},{16,24},{18,... | collective-permute-start | bytes 479240 | tf_op jit(solution)/shard_map/ppermute | solution.py:362
  122.4 9.4 %collective-permute-start.14 = (bf16[1,13,2,24,128]{4,3,2,1,0:T(8,128)(2,1)S(1)}, bf16[1,13,2,24,128]{4,3,2,1,0:T(8,128)(2,1)S(1)}, u32[]{:S(2)}, u32[]{:S(2)}) collective-permute-start(bf16[1,13,2,24,128]{4,3,2,1,0:T(8,128)(2,1)S(1)} %get-tuple-element.54), channel_id=1, source_target_pairs={{0,2},{2,10},{4,14},{6,6},{8,0},{10,8},{12,12},{14,4},{16,26},{18,... | collective-permute-start | bytes 479240 | tf_op jit(solution)/shard_map/ppermute | solution.py:362
  (22 other events, 212.2 us)

commit v4 on v3

--- a/solution.py
+++ b/solution.py
@@ -9,7 +9,7 @@
 
 
 AXES = ("rows", "cols")
-CHUNKS = 2
+CHUNKS = 1
 HALVES = 2
 SIDE = 4
 UP, DOWN = 3, 2
@@ -187,11 +187,11 @@
     ]
 
 
-def conv_kernel(pos, *refs, parts, sh, tr, pitch, rows, cols, at, cam_at):
+def conv_kernel(pos, *refs, parts, sh, tr, pitch, rows, cols, at, out_at, many):
     windows = refs[:parts]
     above, below, camera, w1, b1, w2, b2 = refs[parts : parts + 7]
-    outs = refs[parts + 7 : parts + 7 + HALVES]
-    tile, taps, mid, cells, inside = refs[parts + 7 + HALVES :]
+    outs = refs[-5 - HALVES : -5]
+    tile, taps, mid, cells, inside = refs[-5:]
     group, member, half_id, column = pos[0], pos[1], pos[2], pos[3]
     wide = windows[0].shape[2]
     lidar = windows[0].shape[3]
@@ -205,81 +205,88 @@
     col = lax.broadcasted_iota(jnp.int32, inside.shape, 0) + col0
     inside[...] = jnp.where((col >= 0) & (col < cols), 1.0, 0.0)
 
-    tile[0:UP, 0:wide, :] = above[at]
-    for d in range(parts):
-        source = lax.rem(member - d + parts, parts)
-        tile[pl.ds(UP + source * sh, sh), 0:wide, :] = windows[d][at]
-    tile[UP + tr : UP + tr + DOWN, 0:wide, :] = below[at]
-
-    step = 6
-    flat = step * pitch
-
-    def shift(i, _):
-        r = i * step
-        x = tile[pl.ds(r, step)].reshape(flat, lidar).astype(jnp.float32)
-        taps[pl.ds(r, step), :, 0:lidar] = pltpu.roll(x, 1, 0).astype(BF).reshape(step, pitch, lidar)
-        taps[pl.ds(r, step), :, lidar:] = pltpu.roll(x, flat - 1, 0).astype(BF).reshape(step, pitch, lidar)
+    def frame(f, _):
+        tile[0:UP, 0:wide, :] = above[at + f]
+        for d in range(parts):
+            source = lax.rem(member - d + parts, parts)
+            tile[pl.ds(UP + source * sh, sh), 0:wide, :] = windows[d][at + f]
+        tile[UP + tr : UP + tr + DOWN, 0:wide, :] = below[at + f]
+
+        step = 6
+        flat = step * pitch
+
+        def shift(i, _):
+            r = i * step
+            x = tile[pl.ds(r, step)].reshape(flat, lidar).astype(jnp.float32)
+            taps[pl.ds(r, step), :, 0:lidar] = pltpu.roll(x, 1, 0).astype(BF).reshape(step, pitch, lidar)
+            taps[pl.ds(r, step), :, lidar:] = pltpu.roll(x, flat - 1, 0).astype(BF).reshape(step, pitch, lidar)
+            return 0
+
+        lax.fori_loop(0, (tr + 6) // step, shift, 0)
+
+        n1 = (tr + 4) // 2
+        m1 = n1 * pitch
+
+        def first(i, _):
+            r = i * n1
+            lhs = []
+            for dy in range(3):
+                lhs.append(tile[pl.ds(r + dy, n1)].reshape(m1, lidar))
+                lhs.append(taps[pl.ds(r + dy, n1)].reshape(m1, 2 * lidar))
+                lhs.append(camera[at + f, pl.ds(r + dy, n1)].reshape(m1, camera.shape[3]))
+            acc = jnp.dot(jnp.concatenate(lhs, axis=1), w1[...], preferred_element_type=jnp.float32)
+            v = jnp.maximum(acc + b1[...], 0.0).reshape(n1, pitch, joined)
+            kept = []
+            for y in range(n1):
+                row = group * tr - 2 + r + y
+                kept.append(v[y] * (inside[...] * jnp.where((row >= 0) & (row < rows), 1.0, 0.0)))
+            v = jnp.concatenate(kept, axis=0)
+            shape = (n1 // 2, 2, pitch, joined)
+            p = pl.ds(i * (n1 // 2), n1 // 2)
+            mid[p, :, :, 0:joined] = pltpu.roll(v, 1, 0).astype(BF).reshape(shape)
+            mid[p, :, :, joined : 2 * joined] = v.astype(BF).reshape(shape)
+            mid[p, :, :, 2 * joined :] = pltpu.roll(v, m1 - 1, 0).astype(BF).reshape(shape)
+            return 0
+
+        lax.fori_loop(0, (tr + 4) // n1, first, 0)
+
+        n2 = (tr + 2) // 2
+        m2 = n2 * pitch
+        lhs = [mid[i // 2 : i // 2 + n2, i % 2].reshape(m2, 3 * joined) for i in range(4)]
+        acc = jnp.dot(jnp.concatenate(lhs, axis=1), w2[...], preferred_element_type=jnp.float32)
+        v = pltpu.roll(jnp.maximum(acc + b2[...], 0.0), SIDE, 0)
+        cells[:, 0] = v[:, :block].reshape(n2, pitch, block)
+        cells[:, 1] = v[:, block:].reshape(n2, pitch, block)
+        pairs = tr // 2
+        w = (wide - 2 * SIDE) // HALVES
+        for sub in range(HALVES):
+            c = 2 * SIDE + sub * w
+            even = cells[0:pairs, 1, c : c + w, :].astype(BF)
+            odd = cells[1 : pairs + 1, 0, c : c + w, :].astype(BF)
+            top = jnp.where(group > 0, cells[0, 0, c : c + w, :], 0.0)
+            corner = jnp.broadcast_to(cells[pairs, 0, c - 1 : c, :], (w, block))
+            beside = cells[0:pairs, :, c - 1, :].reshape(tr, block)
+            if sub == 0:
+                corner = jnp.where(column > 0, corner, 0.0)
+                beside = jnp.where(column > 0, beside, 0.0)
+            row = lax.broadcasted_iota(jnp.int32, beside.shape, 0)
+            beside = jnp.where((row == 0) & (group == 0), 0.0, beside)
+            edge = jnp.where(half_id == 0, top, corner).astype(BF)
+            beside = beside.astype(BF)
+            for h in range(HALVES):
+
+                @pl.when(lax.rem(half_id + h, HALVES) == sub)
+                def _():
+                    outs[h][out_at + f, 0:pairs, 0] = even
+                    outs[h][out_at + f, 0:pairs, 1] = odd
+                    outs[h][out_at + f, pairs, 0] = edge
+                    outs[h][out_at + f, pairs, 1] = beside
         return 0
 
-    lax.fori_loop(0, (tr + 6) // step, shift, 0)
-
-    n1 = (tr + 4) // 2
-    m1 = n1 * pitch
-
-    def first(i, _):
-        r = i * n1
-        lhs = []
-        for dy in range(3):
-            lhs.append(tile[pl.ds(r + dy, n1)].reshape(m1, lidar))
-            lhs.append(taps[pl.ds(r + dy, n1)].reshape(m1, 2 * lidar))
-            lhs.append(camera[cam_at, pl.ds(r + dy, n1)].reshape(m1, camera.shape[3]))
-        acc = jnp.dot(jnp.concatenate(lhs, axis=1), w1[...], preferred_element_type=jnp.float32)
-        v = jnp.maximum(acc + b1[...], 0.0).reshape(n1, pitch, joined)
-        kept = []
-        for y in range(n1):
-            row = group * tr - 2 + r + y
-            kept.append(v[y] * (inside[...] * jnp.where((row >= 0) & (row < rows), 1.0, 0.0)))
-        v = jnp.concatenate(kept, axis=0)
-        shape = (n1 // 2, 2, pitch, joined)
-        p = pl.ds(i * (n1 // 2), n1 // 2)
-        mid[p, :, :, 0:joined] = pltpu.roll(v, 1, 0).astype(BF).reshape(shape)
-        mid[p, :, :, joined : 2 * joined] = v.astype(BF).reshape(shape)
-        mid[p, :, :, 2 * joined :] = pltpu.roll(v, m1 - 1, 0).astype(BF).reshape(shape)
-        return 0
-
-    lax.fori_loop(0, (tr + 4) // n1, first, 0)
-
-    n2 = (tr + 2) // 2
-    m2 = n2 * pitch
-    lhs = [mid[i // 2 : i // 2 + n2, i % 2].reshape(m2, 3 * joined) for i in range(4)]
-    acc = jnp.dot(jnp.concatenate(lhs, axis=1), w2[...], preferred_element_type=jnp.float32)
-    v = pltpu.roll(jnp.maximum(acc + b2[...], 0.0), SIDE, 0)
-    cells[:, 0] = v[:, :block].reshape(n2, pitch, block)
-    cells[:, 1] = v[:, block:].reshape(n2, pitch, block)
-    pairs = tr // 2
-    w = (wide - 2 * SIDE) // HALVES
-    for sub in range(HALVES):
-        c = 2 * SIDE + sub * w
-        even = cells[0:pairs, 1, c : c + w, :].astype(BF)
-        odd = cells[1 : pairs + 1, 0, c : c + w, :].astype(BF)
-        top = jnp.where(group > 0, cells[0, 0, c : c + w, :], 0.0)
-        corner = jnp.broadcast_to(cells[pairs, 0, c - 1 : c, :], (w, block))
-        beside = cells[0:pairs, :, c - 1, :].reshape(tr, block)
-        if sub == 0:
-            corner = jnp.where(column > 0, corner, 0.0)
-            beside = jnp.where(column > 0, beside, 0.0)
-        row = lax.broadcasted_iota(jnp.int32, beside.shape, 0)
-        beside = jnp.where((row == 0) & (group == 0), 0.0, beside)
-        edge = jnp.where(half_id == 0, top, corner).astype(BF)
-        beside = beside.astype(BF)
-        for h in range(HALVES):
-
-            @pl.when(lax.rem(half_id + h, HALVES) == sub)
-            def _():
-                outs[h][0, 0:pairs, 0] = even
-                outs[h][0, 0:pairs, 1] = odd
-                outs[h][0, pairs, 0] = edge
-                outs[h][0, pairs, 1] = beside
+    if many == 1:
+        frame(0, 0)
+    else:
+        lax.fori_loop(0, many, frame, 0)
 
 
 def encode_kernel(pos, *refs, parts, half_rows, w):
@@ -435,7 +442,6 @@
         half_rows = tr // 2
         n = HALVES * half_rows
         jd = rounded(w // 2, 8)
-        blocks = jax.ShapeDtypeStruct((1, pairs2, 2, w, block), BF)
         flops = 2 * pitch * ((tr + 4) * w1.shape[0] * joined + pairs2 * w2.shape[0] * 2 * block)
         framed = lambda a: pl.BlockSpec((1,) + a.shape[1:], lambda f, p: (f,) + (0,) * (a.ndim - 1))
         encoded = None
@@ -462,32 +468,42 @@
             last, head = pick(windows, (member + 1) % members, member, 1)
             above = across(last, 1, 0)
             below = across(head, -1, 0)
-            for f1 in range(f0, f0 + step):
-                tiles = pl.pallas_call(
-                    functools.partial(conv_kernel, parts=members, sh=sh, tr=tr, pitch=pitch, rows=rows, cols=cols, at=f1 - f0, cam_at=f1),
-                    in_specs=[pl.BlockSpec(memory_space=pltpu.SMEM)] + [pl.BlockSpec(memory_space=pltpu.VMEM)] * (members + 7),
-                    out_specs=[pl.BlockSpec(memory_space=pltpu.VMEM)] * HALVES,
-                    scratch_shapes=conv_scratch(tr, pitch, lidar_ch, joined, block, pairs2),
-                    out_shape=[blocks] * HALVES,
-                    compiler_params=limit(28),
-                    cost_estimate=pl.CostEstimate(flops=flops, bytes_accessed=2 * 10**6, transcendentals=0),
-                )(pos, *windows, above, below, cam, w1, b1, w2, b2)
+            shifts = []
+            for h in range(HALVES):
+                shift = []
+                for s in range(total):
+                    r, c = divmod(s, n_cols)
+                    k, m = divmod(c, members)
+                    shift.append((s, r * n_cols + HALVES * tile_of[r % 2][m] + (k + h) % HALVES))
+                shifts.append(shift)
+            vmem = pl.BlockSpec(memory_space=pltpu.VMEM)
+            batch = step // 2 if step % 2 == 0 else step
+            for b0 in range(0, step, batch):
+                blocks = jax.ShapeDtypeStruct((batch, pairs2, 2, w, block), BF)
+                runs = [(0, batch)] if b0 == 0 else [(f, 1) for f in range(batch)]
+                tiles = []
+                for f1, many in runs:
+                    tiles = pl.pallas_call(
+                        functools.partial(conv_kernel, parts=members, sh=sh, tr=tr, pitch=pitch, rows=rows, cols=cols, at=b0 + f1, out_at=f1, many=many),
+                        in_specs=[pl.BlockSpec(memory_space=pltpu.SMEM)] + [vmem] * (members + 7 + len(tiles)),
+                        out_specs=[vmem] * HALVES,
+                        scratch_shapes=conv_scratch(tr, pitch, lidar_ch, joined, block, pairs2),
+                        out_shape=[blocks] * HALVES,
+                        input_output_aliases={members + 8 + h: h for h in range(HALVES)} if tiles else {},
+                        compiler_params=limit(20),
+                        cost_estimate=pl.CostEstimate(flops=flops * many, bytes_accessed=2 * 10**6, transcendentals=0),
+                    )(pos, *windows, above, below, cam, w1, b1, w2, b2, *tiles)
                 pieces = []
                 for h in range(HALVES):
-                    pairs = []
-                    for s in range(total):
-                        r, c = divmod(s, n_cols)
-                        k, m = divmod(c, members)
-                        pairs.append((s, r * n_cols + HALVES * tile_of[r % 2][m] + (k + h) % HALVES))
-                    pieces.append(send(tiles[h], pairs))
+                    pieces.append(send(tiles[h], shifts[h]))
                 old = [] if encoded is None else [encoded]
                 encoded = pl.pallas_call(
                     lambda *refs: encode_kernel(*refs, parts=HALVES, half_rows=half_rows, w=w),
                     grid_spec=pltpu.PrefetchScalarGridSpec(
                         num_scalar_prefetch=1,
-                        grid=(1,),
+                        grid=(batch,),
                         in_specs=[framed(x) for x in pieces] + [whole(x) for x in (w3, b3, proj_weight, bp)] + [pl.BlockSpec(memory_space=pl.ANY)] * len(old),
-                        out_specs=pl.BlockSpec((1, n, 2, w, 2 * block), lambda f, p, f1=f1: (f + f1, 0, 0, 0, 0)),
+                        out_specs=pl.BlockSpec((1, n, 2, w, 2 * block), lambda f, p, lo=f0 + b0: (f + lo, 0, 0, 0, 0)),
                         scratch_shapes=[
                             pltpu.VMEM((n + 1, 2, rounded(w + 1, 8) + 16, block), jnp.float32),
                             pltpu.VMEM((n, 2 * jd, block), jnp.float32),
@@ -496,7 +512,7 @@
                     out_shape=jax.ShapeDtypeStruct((frames, n, 2, w, 2 * block), BF),
                     input_output_aliases={5 + HALVES: 0} if old else {},
                     compiler_params=limit(12),
-                    cost_estimate=pl.CostEstimate(flops=2 * n * jd * w3.shape[0] * 256, bytes_accessed=10**6, transcendentals=0),
+                    cost_estimate=pl.CostEstimate(flops=2 * batch * n * jd * w3.shape[0] * 256, bytes_accessed=batch * 10**6, transcendentals=0),
                 )(cindex.reshape(1).astype(jnp.int32), *pieces, w3, b3, proj_weight, bp, *old)
         return encoded.reshape(frames, 2 * n, w, 2 * block)
 

time: 136 us -> 154 us (1.13); the launches traced: 133 us -> 153 us
  waiting for transfers between devices: 4.83 us -> 47.1 us
  starting transfers between devices: 77.2 us -> 58.2 us
  Pallas kernels: 44.9 us -> 41 us
    ppermute x26 -> x17, waiting for transfers between devices: 4.83 us -> 47.1 us  [send(): return lax.ppermute(x, AXES, pairs)]
    ppermute x26 -> x17, starting transfers between devices: 77.2 us -> 58.2 us  [send(): return lax.ppermute(x, AXES, pairs)]
    pallas_call x4 -> x2, Pallas kernels: 6.16 us -> 4.52 us  [local(): pl.pallas_call(lambda *refs: encode_kernel(*refs, parts=HALVES, half_rows...]
    unnamed x40 -> x28, local copies, waits for them, and re-layouts: 5.48 us -> 6.16 us
    pallas_call x4 -> x3, Pallas kernels: 25 us -> 24.9 us  [local(): pl.pallas_call(functools.partial(conv_kernel, parts=members, sh=sh, tr=tr...]
  transfers between devices with their start and end apart: 26 -> 17, of which waited for: 3 -> 4; matrix products, arithmetic and copies ran while one was open for 0% -> 0% of each run, Pallas kernels for 31% -> 17%
where the time goes in v4:
time: 154 us; the launch traced here: 153 us
  starting transfers between devices  58.2 us (38%)
  waiting for transfers between devices  47.1 us (31%)
  Pallas kernels  41 us (27%)
  local copies, waits for them, and re-layouts  6.16 us (4%)
    ppermute x17, starting transfers between devices, send(): return lax.ppermute(x, AXES, pairs)  58.2 us
    ppermute x17, waiting for transfers between devices, send(): return lax.ppermute(x, AXES, pairs)  47.1 us
    pallas_call x3, Pallas kernels, local(): pl.pallas_call(functools.partial(conv_kernel, parts=members, sh=sh, tr=tr...  24.9 us
    unnamed x28, local copies, waits for them, and re-layouts  6.16 us
    pallas_call x1, Pallas kernels, local(): pl.pallas_call(lambda *refs: camera_unpack_kernel(*refs, groups=groups, s...  6 us
    pallas_call x2, Pallas kernels, local(): pl.pallas_call(lambda *refs: encode_kernel(*refs, parts=HALVES, half_rows...  4.52 us
  transfers between devices with their start and end apart: 17, of which 4 were waited for; matrix products, arithmetic and copies ran while one was open for 0% of the time, Pallas kernels for 17%

profile of v4, /device:TPU:0, one launch (start us, length us, event | category | flops | bytes accessed | tf_op | source)
XLA Modules:
  0.0 153.1 jit_solution(11082800227335083750)
XLA Ops:
  0.1 1.7 %copy-done = bf16[4,6,192,256]{3,2,1,0:T(8,128)(2,1)S(1)} copy-done((bf16[4,6,192,256]{3,2,1,0:T(8,128)(2,1)S(1)}, bf16[4,6,192,256]{3,2,1,0:T(8,128)(2,1)}, u32[]{:S(2)}) %copy-start) | copy-done | bytes 2359320
  1.7 1.4 windows.1
  3.2 3.0 %collective-permute-start = (bf16[4,6,56,256]{3,2,1,0:T(8,128)(2,1)S(1)}, bf16[4,6,56,256]{3,2,1,0:T(8,128)(2,1)S(1)}, u32[]{:S(2)}, u32[]{:S(2)}) collective-permute-start(bf16[4,6,56,256]{3,2,1,0:T(8,128)(2,1)S(1)} %get-tuple-element.28), channel_id=1, source_target_pairs={{0,2},{2,4},{4,6},{6,0},{8,10},{10,12},{12,14},{14,8},{16,18},{18,... | collective-permute-start | bytes 2064392 | tf_op jit(solution)/shard_map/ppermute | solution.py:369
  6.2 1.6 %collective-permute-start.1 = (bf16[4,6,56,256]{3,2,1,0:T(8,128)(2,1)S(1)}, bf16[4,6,56,256]{3,2,1,0:T(8,128)(2,1)S(1)}, u32[]{:S(2)}, u32[]{:S(2)}) collective-permute-start(bf16[4,6,56,256]{3,2,1,0:T(8,128)(2,1)S(1)} %get-tuple-element.29), channel_id=1, source_target_pairs={{0,4},{2,6},{4,0},{6,2},{8,12},{10,14},{12,8},{14,10},{16,20},{18,... | collective-permute-start | bytes 2064392 | tf_op jit(solution)/shard_map/ppermute | solution.py:369
  7.8 1.4 collective-permute-start.2
  9.2 2.3 %camera_pack.1 = (bf16[12,80,128]{2,1,0:T(8,128)(2,1)S(1)}, bf16[12,80,128]{2,1,0:T(8,128)(2,1)}, bf16[12,80,128]{2,1,0:T(8,128)(2,1)}, bf16[12,80,128]{2,1,0:T(...) custom-call(s32[1]{0:T(128)} %bitcast.10.refs_0_, ...), custom_call_target="tpu_custom_call" | custom-call | tf_op jit(solution)/shard_map/camera_pack/pallas_call | solution.py:405
  12.9 28.0 %collective-permute-done.refs_1_.refs_5_ = bf16[4,6,56,256]{3,2,1,0:T(8,128)(2,1)S(1)} collective-permute-done((bf16[4,6,56,256]{3,2,1,0:T(8,128)(2,1)S(1)}, bf16[4,6,56,256]{3,2,1,0:T(8,128)(2,1)S(1)}, u32[]{:S(2)}, u32[]{:S(2)}) %collective-permute-start) | collective-permute-done | bytes 688160 | tf_op jit(solution)/shard_map/ppermute | solution.py:369
  40.9 1.6 %shard_map.100 = (bf16[4,3,56,256]{3,2,1,0:T(8,128)(2,1)}, bf16[4,2,56,256]{3,2,1,0:T(8,128)(2,1)}) custom-call(s32[2]{0:T(128)S(1)} %pad_add_fusion.2.pos, bf16[4,6,56,256]{3,2,1,0:T(8,128)(2,1)S(1)} %get-tuple-element.27.refs_0_.refs_4_, bf16[4,6,56,256]{3,2,1,0:T(8,128)(2,1)S(1)} %collective-permute-done.refs_1_.refs_5_, ...), custom_call_target="tpu_custom_call" | custom-call | tf_op jit(solution)/shard_map/pallas_call | solution.py:172
  42.5 2.1 %collective-permute-start.3 = (bf16[4,3,56,256]{3,2,1,0:T(8,128)(2,1)}, bf16[4,3,56,256]{3,2,1,0:T(8,128)(2,1)}, u32[]{:S(2)}, u32[]{:S(2)}) collective-permute-start(bf16[4,3,56,256]{3,2,1,0:T(8,128)(2,1)} %get-tuple-element.31), channel_id=1, source_target_pairs={{0,8},{6,14},{2,10},{4,12},{8,18},{14,20},{10,16},{12,22},{18,26},... | collective-permute-start | bytes 1032200 | tf_op jit(solution)/shard_map/ppermute | solution.py:369
  47.3 14.5 %collective-permute-start.6 = (bf16[12,80,128]{2,1,0:T(8,128)(2,1)}, bf16[12,80,128]{2,1,0:T(8,128)(2,1)}, u32[]{:S(2)}, u32[]{:S(2)}) collective-permute-start(bf16[12,80,128]{2,1,0:T(8,128)(2,1)} %get-tuple-element.34), channel_id=1, source_target_pairs={{0,8},{2,18},{4,26},{6,0},{8,14},{10,20},{12,28},{14,6},{16,10},{1... | collective-permute-start | bytes 737288 | tf_op jit(solution)/shard_map/ppermute | solution.py:369
  61.8 4.7 %collective-permute-start.7 = (bf16[12,80,128]{2,1,0:T(8,128)(2,1)}, bf16[12,80,128]{2,1,0:T(8,128)(2,1)}, u32[]{:S(2)}, u32[]{:S(2)}) collective-permute-start(bf16[12,80,128]{2,1,0:T(8,128)(2,1)} %get-tuple-element.35), channel_id=1, source_target_pairs={{0,18},{2,26},{4,0},{6,8},{8,20},{10,28},{12,6},{14,14},{16,16},{1... | collective-permute-start | bytes 737288 | tf_op jit(solution)/shard_map/ppermute | solution.py:369
  67.2 3.5 %collective-permute-start.8 = (bf16[12,80,128]{2,1,0:T(8,128)(2,1)}, bf16[12,80,128]{2,1,0:T(8,128)(2,1)}, u32[]{:S(2)}, u32[]{:S(2)}) collective-permute-start(bf16[12,80,128]{2,1,0:T(8,128)(2,1)} %get-tuple-element.36), channel_id=1, source_target_pairs={{0,26},{2,0},{4,8},{6,18},{8,28},{10,6},{12,14},{14,20},{16,24},{1... | collective-permute-start | bytes 737288 | tf_op jit(solution)/shard_map/ppermute | solution.py:369
  72.7 1.4 copy-done.2
  74.6 2.5 %collective-permute-done.8.refs_4_ = bf16[12,80,128]{2,1,0:T(8,128)(2,1)} collective-permute-done((bf16[12,80,128]{2,1,0:T(8,128)(2,1)}, bf16[12,80,128]{2,1,0:T(8,128)(2,1)}, u32[]{:S(2)}, u32[]{:S(2)}) %collective-permute-start.8) | collective-permute-done | bytes 245792 | tf_op jit(solution)/shard_map/ppermute | solution.py:369
  78.8 6.0 %camera_unpack.1 = bf16[128,64,256]{2,1,0:T(8,128)(2,1)S(1)} custom-call(s32[1]{0:T(128)} %bitcast.1.refs_0_, bf16[12,80,128]{2,1,0:T(8,128)(2,1)S(1)} %copy-done.7, bf16[12,80,128]{2,1,0:T(8,128)(2,1)} %collective-permute-done.6.refs_2_, bf16[12,80,128]{2,1,0:T(8,128)(2,1)} %collective-permute-done.7.refs_3_, ...), custom_call_target="tpu_custom_call" | custom-call | tf_op jit(solution)/shard_map/camera_unpack/pallas_call | solution.py:422
  84.9 4.5 %collective-permute-done.4.refs_5_ = bf16[4,2,56,256]{3,2,1,0:T(8,128)(2,1)} collective-permute-done((bf16[4,2,56,256]{3,2,1,0:T(8,128)(2,1)}, bf16[4,2,56,256]{3,2,1,0:T(8,128)(2,1)}, u32[]{:S(2)}, u32[]{:S(2)}) %collective-permute-start.4) | collective-permute-done | bytes 229408 | tf_op jit(solution)/shard_map/ppermute | solution.py:369
  89.4 11.8 %shard_map.103 = (bf16[2,13,2,24,128]{4,3,2,1,0:T(8,128)(2,1)S(1)}, bf16[2,13,2,24,128]{4,3,2,1,0:T(8,128)(2,1)S(1)}) custom-call(s32[4]{0:T(128)S(1)} %pad_add_fusion.pos, bf16[4,6,56,256]{3,2,1,0:T(8,128)(2,1)S(1)} %get-tuple-element.27.refs_0_.refs_4_, bf16[4,6,56,256]{3,2,1,0:T(8,128)(2,1)S(1)} %collective-permute-done.refs_1_.refs_5_, ...), custom_call_target="tpu_custom_call" | custom-call | flops 8254390272 | bytes 2000000 | tf_op jit(solution)/shard_map/pallas_call | solution.py:486
  101.9 9.1 %collective-permute-start.16 = (bf16[2,13,2,24,128]{4,3,2,1,0:T(8,128)(2,1)S(1)}, bf16[2,13,2,24,128]{4,3,2,1,0:T(8,128)(2,1)S(1)}, u32[]{:S(2)}, u32[]{:S(2)}) collective-permute-start(bf16[2,13,2,24,128]{4,3,2,1,0:T(8,128)(2,1)S(1)} %get-tuple-element.48), channel_id=1, source_target_pairs={{0,2},{2,10},{4,14},{6,6},{8,0},{10,8},{12,12},{14,4},{16,26},{18,... | collective-permute-start | bytes 958472 | tf_op jit(solution)/shard_map/ppermute | solution.py:369
  111.0 6.6 %shard_map.101 = (bf16[2,13,2,24,128]{4,3,2,1,0:T(8,128)(2,1)S(1)}, bf16[2,13,2,24,128]{4,3,2,1,0:T(8,128)(2,1)S(1)}) custom-call(s32[4]{0:T(128)S(1)} %pad_add_fusion.pos, bf16[4,6,56,256]{3,2,1,0:T(8,128)(2,1)S(1)} %get-tuple-element.27.refs_0_.refs_4_, bf16[4,6,56,256]{3,2,1,0:T(8,128)(2,1)S(1)} %collective-permute-done.refs_1_.refs_5_, ...), custom_call_target="tpu_custom_call" | custom-call | flops 4127195136 | bytes 2000000 | tf_op jit(solution)/shard_map/pallas_call | solution.py:486
  117.6 6.5 %shard_map.102 = (bf16[2,13,2,24,128]{4,3,2,1,0:T(8,128)(2,1)S(1)}, bf16[2,13,2,24,128]{4,3,2,1,0:T(8,128)(2,1)S(1)}) custom-call(s32[4]{0:T(128)S(1)} %pad_add_fusion.pos, bf16[4,6,56,256]{3,2,1,0:T(8,128)(2,1)S(1)} %get-tuple-element.27.refs_0_.refs_4_, ...), custom_call_target="tpu_custom_call", output_to_operand_aliasing={{0}: (12, {}), {1}: (13, {})} | custom-call | flops 4127195136 | bytes 2000000 | tf_op jit(solution)/shard_map/pallas_call | solution.py:486
  124.8 11.6 %collective-permute-start.14 = (bf16[2,13,2,24,128]{4,3,2,1,0:T(8,128)(2,1)S(1)}, bf16[2,13,2,24,128]{4,3,2,1,0:T(8,128)(2,1)S(1)}, u32[]{:S(2)}, u32[]{:S(2)}) collective-permute-start(bf16[2,13,2,24,128]{4,3,2,1,0:T(8,128)(2,1)S(1)} %get-tuple-element.46), channel_id=1, source_target_pairs={{0,2},{2,10},{4,14},{6,6},{8,0},{10,8},{12,12},{14,4},{16,26},{18,... | collective-permute-start | bytes 958472 | tf_op jit(solution)/shard_map/ppermute | solution.py:369
  136.5 2.3 %shard_map.104.refs_7_ = bf16[4,24,2,24,256]{4,3,2,1,0:T(8,128)(2,1)} custom-call(s32[1]{0:T(128)} %bitcast.refs_0_, bf16[2,13,2,24,128]{4,3,2,1,0:T(8,128)(2,1)S(1)} %collective-permute-done.15.refs_1_, bf16[2,13,2,24,128]{4,3,2,1,0:T(8,128)(2,1)S(1)} %collective-permute-done.16.refs_2_, bf16[1152,256]{1,0:T(8,128)(2,1)S(1)} %bitcast.24, ...), custom_call_target="tpu_custom_call" | custom-call | flops 452984832 | bytes 2000000 | tf_op jit(solution)/shard_map/pallas_call | solution.py:500
  138.8 12.0 %collective-permute-done.14.refs_2_ = bf16[2,13,2,24,128]{4,3,2,1,0:T(8,128)(2,1)S(1)} collective-permute-done((bf16[2,13,2,24,128]{4,3,2,1,0:T(8,128)(2,1)S(1)}, bf16[2,13,2,24,128]{4,3,2,1,0:T(8,128)(2,1)S(1)}, u32[]{:S(2)}, u32[]{:S(2)}) %collective-permute-start.14) | collective-permute-done | bytes 319520 | tf_op jit(solution)/shard_map/ppermute | solution.py:369
  150.8 2.2 %shard_map.105 = bf16[4,24,2,24,256]{4,3,2,1,0:T(8,128)(2,1)} custom-call(s32[1]{0:T(128)} %bitcast.refs_0_, bf16[2,13,2,24,128]{4,3,2,1,0:T(8,128)(2,1)S(1)} %collective-permute-done.13.refs_1_, bf16[2,13,2,24,128]{4,3,2,1,0:T(8,128)(2,1)S(1)} %collective-permute-done.14.refs_2_, bf16[1152,256]{1,0:T(8,128)(2,1)S(1)} %bitcast.25, ...), custom_call_target="tpu_custom_call", output_to_operand_aliasing={{}: (7, {})} | custom-call | flops 452984832 | bytes 2000000 | tf_op jit(solution)/shard_map/pallas_call | solution.py:500
  (52 shorter events, 10.3 us)
Async XLA Ops:
  3.2 37.7 %collective-permute-start = (bf16[4,6,56,256]{3,2,1,0:T(8,128)(2,1)S(1)}, bf16[4,6,56,256]{3,2,1,0:T(8,128)(2,1)S(1)}, u32[]{:S(2)}, u32[]{:S(2)}) collective-permute-start(bf16[4,6,56,256]{3,2,1,0:T(8,128)(2,1)S(1)} %get-tuple-element.28), channel_id=1, source_target_pairs={{0,2},{2,4},{4,6},{6,0},{8,10},{10,12},{12,14},{14,8},{16,18},{18,... | collective-permute-start | bytes 2064392 | tf_op jit(solution)/shard_map/ppermute | solution.py:369
  6.2 34.7 %collective-permute-start.1 = (bf16[4,6,56,256]{3,2,1,0:T(8,128)(2,1)S(1)}, bf16[4,6,56,256]{3,2,1,0:T(8,128)(2,1)S(1)}, u32[]{:S(2)}, u32[]{:S(2)}) collective-permute-start(bf16[4,6,56,256]{3,2,1,0:T(8,128)(2,1)S(1)} %get-tuple-element.29), channel_id=1, source_target_pairs={{0,4},{2,6},{4,0},{6,2},{8,12},{10,14},{12,8},{14,10},{16,20},{18,... | collective-permute-start | bytes 2064392 | tf_op jit(solution)/shard_map/ppermute | solution.py:369
  7.8 33.1 %collective-permute-start.2 = (bf16[4,6,56,256]{3,2,1,0:T(8,128)(2,1)S(1)}, bf16[4,6,56,256]{3,2,1,0:T(8,128)(2,1)S(1)}, u32[]{:S(2)}, u32[]{:S(2)}) collective-permute-start(bf16[4,6,56,256]{3,2,1,0:T(8,128)(2,1)S(1)} %get-tuple-element.30), channel_id=1, source_target_pairs={{0,6},{2,0},{4,2},{6,4},{8,14},{10,8},{12,10},{14,12},{16,22},{18,... | collective-permute-start | bytes 2064392 | tf_op jit(solution)/shard_map/ppermute | solution.py:369
  11.5 59.3 %collective-permute-start.5 = (bf16[12,80,128]{2,1,0:T(8,128)(2,1)S(1)}, bf16[12,80,128]{2,1,0:T(8,128)(2,1)S(1)}, u32[]{:S(2)}, u32[]{:S(2)}) collective-permute-start(bf16[12,80,128]{2,1,0:T(8,128)(2,1)S(1)} %get-tuple-element.33), channel_id=1, source_target_pairs={{0,0},{2,8},{4,18},{6,26},{8,6},{10,14},{12,20},{14,28},{16,2},{18... | collective-permute-start | bytes 737288 | tf_op jit(solution)/shard_map/ppermute | solution.py:369
  12.1 33.8 %collective-permute-start.9 = (bf16[3,80,128]{2,1,0:T(8,128)(2,1)S(1)}, bf16[3,80,128]{2,1,0:T(8,128)(2,1)S(1)}, u32[]{:S(2)}, u32[]{:S(2)}) collective-permute-start(bf16[3,80,128]{2,1,0:T(8,128)(2,1)S(1)} %get-tuple-element.37), channel_id=1, source_target_pairs={{6,6},{14,2},{22,4},{8,8},{16,14},{24,10},{7,7},{15,3},{23,5},{9,9... | collective-permute-start | bytes 184328 | tf_op jit(solution)/shard_map/ppermute | solution.py:369
  40.9 31.8 %copy-start.4 = (bf16[3,3,256,128]{3,2,1,0:T(8,128)(2,1)S(1)}, bf16[3,3,256,128]{3,2,1,0:T(8,128)(2,1)}, u32[]{:S(2)}) copy-start(bf16[3,3,256,128]{3,2,1,0:T(8,128)(2,1)} %param.14) | copy-start | bytes 1769476
  40.9 33.6 %copy-start.13 = (f32[128]{0:T(128)S(1)}, f32[128]{0:T(128)}, u32[]{:S(2)}) copy-start(f32[128]{0:T(128)} %param.15) | copy-start | bytes 1540
  42.5 46.8 %collective-permute-start.3 = (bf16[4,3,56,256]{3,2,1,0:T(8,128)(2,1)}, bf16[4,3,56,256]{3,2,1,0:T(8,128)(2,1)}, u32[]{:S(2)}, u32[]{:S(2)}) collective-permute-start(bf16[4,3,56,256]{3,2,1,0:T(8,128)(2,1)} %get-tuple-element.31), channel_id=1, source_target_pairs={{0,8},{6,14},{2,10},{4,12},{8,18},{14,20},{10,16},{12,22},{18,26},... | collective-permute-start | bytes 1032200 | tf_op jit(solution)/shard_map/ppermute | solution.py:369
  44.6 2.6 %collective-permute-start.10 = (bf16[3,80,128]{2,1,0:T(8,128)(2,1)S(1)}, bf16[3,80,128]{2,1,0:T(8,128)(2,1)S(1)}, u32[]{:S(2)}, u32[]{:S(2)}) collective-permute-start(bf16[3,80,128]{2,1,0:T(8,128)(2,1)S(1)} %get-tuple-element.38), channel_id=1, source_target_pairs={{6,14},{14,10},{22,12},{8,18},{16,20},{24,16},{7,15},{15,11},{23,1... | collective-permute-start | bytes 184328 | tf_op jit(solution)/shard_map/ppermute | solution.py:369
  45.3 16.5 %collective-permute-start.11 = (bf16[3,80,128]{2,1,0:T(8,128)(2,1)S(1)}, bf16[3,80,128]{2,1,0:T(8,128)(2,1)S(1)}, u32[]{:S(2)}, u32[]{:S(2)}) collective-permute-start(bf16[3,80,128]{2,1,0:T(8,128)(2,1)S(1)} %get-tuple-element.39), channel_id=1, source_target_pairs={{6,20},{14,16},{22,22},{8,26},{16,28},{24,24},{7,21},{15,17},{23,2... | collective-permute-start | bytes 184328 | tf_op jit(solution)/shard_map/ppermute | solution.py:369
  46.0 20.6 %collective-permute-start.12 = (bf16[3,80,128]{2,1,0:T(8,128)(2,1)S(1)}, bf16[3,80,128]{2,1,0:T(8,128)(2,1)S(1)}, u32[]{:S(2)}, u32[]{:S(2)}) collective-permute-start(bf16[3,80,128]{2,1,0:T(8,128)(2,1)S(1)} %get-tuple-element.40), channel_id=1, source_target_pairs={{6,28},{14,24},{22,30},{8,0},{16,6},{24,2},{7,29},{15,25},{23,31},... | collective-permute-start | bytes 184328 | tf_op jit(solution)/shard_map/ppermute | solution.py:369
  47.3 27.3 %collective-permute-start.6 = (bf16[12,80,128]{2,1,0:T(8,128)(2,1)}, bf16[12,80,128]{2,1,0:T(8,128)(2,1)}, u32[]{:S(2)}, u32[]{:S(2)}) collective-permute-start(bf16[12,80,128]{2,1,0:T(8,128)(2,1)} %get-tuple-element.34), channel_id=1, source_target_pairs={{0,8},{2,18},{4,26},{6,0},{8,14},{10,20},{12,28},{14,6},{16,10},{1... | collective-permute-start | bytes 737288 | tf_op jit(solution)/shard_map/ppermute | solution.py:369
  61.8 12.8 %collective-permute-start.7 = (bf16[12,80,128]{2,1,0:T(8,128)(2,1)}, bf16[12,80,128]{2,1,0:T(8,128)(2,1)}, u32[]{:S(2)}, u32[]{:S(2)}) collective-permute-start(bf16[12,80,128]{2,1,0:T(8,128)(2,1)} %get-tuple-element.35), channel_id=1, source_target_pairs={{0,18},{2,26},{4,0},{6,8},{8,20},{10,28},{12,6},{14,14},{16,16},{1... | collective-permute-start | bytes 737288 | tf_op jit(solution)/shard_map/ppermute | solution.py:369
  67.2 9.9 %collective-permute-start.8 = (bf16[12,80,128]{2,1,0:T(8,128)(2,1)}, bf16[12,80,128]{2,1,0:T(8,128)(2,1)}, u32[]{:S(2)}, u32[]{:S(2)}) collective-permute-start(bf16[12,80,128]{2,1,0:T(8,128)(2,1)} %get-tuple-element.36), channel_id=1, source_target_pairs={{0,26},{2,0},{4,8},{6,18},{8,28},{10,6},{12,14},{14,20},{16,24},{1... | collective-permute-start | bytes 737288 | tf_op jit(solution)/shard_map/ppermute | solution.py:369
  71.4 18.0 %collective-permute-start.4 = (bf16[4,2,56,256]{3,2,1,0:T(8,128)(2,1)}, bf16[4,2,56,256]{3,2,1,0:T(8,128)(2,1)}, u32[]{:S(2)}, u32[]{:S(2)}) collective-permute-start(bf16[4,2,56,256]{3,2,1,0:T(8,128)(2,1)} %get-tuple-element.32), channel_id=1, source_target_pairs={{8,0},{14,6},{10,2},{12,4},{18,8},{20,14},{16,10},{22,12},{26,18},... | collective-permute-start | bytes 688136 | tf_op jit(solution)/shard_map/ppermute | solution.py:369
  74.6 14.8 %copy-start.12 = (f32[256]{0:T(256)S(1)}, f32[256]{0:T(256)}, u32[]{:S(2)}) copy-start(f32[256]{0:T(256)} %param.13) | copy-start | bytes 3076
  101.2 35.3 %collective-permute-start.15 = (bf16[2,13,2,24,128]{4,3,2,1,0:T(8,128)(2,1)S(1)}, bf16[2,13,2,24,128]{4,3,2,1,0:T(8,128)(2,1)S(1)}, u32[]{:S(2)}, u32[]{:S(2)}) collective-permute-start(bf16[2,13,2,24,128]{4,3,2,1,0:T(8,128)(2,1)S(1)} %get-tuple-element.47), channel_id=1, source_target_pairs={{0,0},{2,8},{4,12},{6,4},{8,2},{10,10},{12,14},{14,6},{16,24},{18,... | collective-permute-start | bytes 958472 | tf_op jit(solution)/shard_map/ppermute | solution.py:369
  101.9 34.6 %collective-permute-start.16 = (bf16[2,13,2,24,128]{4,3,2,1,0:T(8,128)(2,1)S(1)}, bf16[2,13,2,24,128]{4,3,2,1,0:T(8,128)(2,1)S(1)}, u32[]{:S(2)}, u32[]{:S(2)}) collective-permute-start(bf16[2,13,2,24,128]{4,3,2,1,0:T(8,128)(2,1)S(1)} %get-tuple-element.48), channel_id=1, source_target_pairs={{0,2},{2,10},{4,14},{6,6},{8,0},{10,8},{12,12},{14,4},{16,26},{18,... | collective-permute-start | bytes 958472 | tf_op jit(solution)/shard_map/ppermute | solution.py:369
  117.6 18.9 %copy-start.1 = (bf16[3,3,128,256]{3,2,1,0:T(8,128)(2,1)S(1)}, bf16[3,3,128,256]{3,2,1,0:T(8,128)(2,1)}, u32[]{:S(2)}) copy-start(bf16[3,3,128,256]{3,2,1,0:T(8,128)(2,1)} %param.16) | copy-start | bytes 1769476
  117.6 18.9 %copy-start.5 = (bf16[256,128]{1,0:T(8,128)(2,1)S(1)}, bf16[256,128]{1,0:T(8,128)(2,1)}, u32[]{:S(2)}) copy-start(bf16[256,128]{1,0:T(8,128)(2,1)} %refs_5_.3) | copy-start | bytes 196612
  117.6 18.9 %copy-start.10 = (f32[256]{0:T(256)S(1)}, f32[256]{0:T(256)}, u32[]{:S(2)}) copy-start(f32[256]{0:T(256)} %param.17) | copy-start | bytes 3076
  117.6 18.9 %copy-start.11 = (f32[128]{0:T(128)S(1)}, f32[128]{0:T(128)}, u32[]{:S(2)}) copy-start(f32[128]{0:T(128)} %param.19) | copy-start | bytes 1540
  124.1 14.7 %collective-permute-start.13 = (bf16[2,13,2,24,128]{4,3,2,1,0:T(8,128)(2,1)S(1)}, bf16[2,13,2,24,128]{4,3,2,1,0:T(8,128)(2,1)S(1)}, u32[]{:S(2)}, u32[]{:S(2)}) collective-permute-start(bf16[2,13,2,24,128]{4,3,2,1,0:T(8,128)(2,1)S(1)} %get-tuple-element.45), channel_id=1, source_target_pairs={{0,0},{2,8},{4,12},{6,4},{8,2},{10,10},{12,14},{14,6},{16,24},{18,... | collective-permute-start | bytes 958472 | tf_op jit(solution)/shard_map/ppermute | solution.py:369
  124.8 26.0 %collective-permute-start.14 = (bf16[2,13,2,24,128]{4,3,2,1,0:T(8,128)(2,1)S(1)}, bf16[2,13,2,24,128]{4,3,2,1,0:T(8,128)(2,1)S(1)}, u32[]{:S(2)}, u32[]{:S(2)}) collective-permute-start(bf16[2,13,2,24,128]{4,3,2,1,0:T(8,128)(2,1)S(1)} %get-tuple-element.46), channel_id=1, source_target_pairs={{0,2},{2,10},{4,14},{6,6},{8,0},{10,8},{12,12},{14,4},{16,26},{18,... | collective-permute-start | bytes 958472 | tf_op jit(solution)/shard_map/ppermute | solution.py:369
  (7 other events, 13.6 us)

commit v5 on v4

--- a/solution.py
+++ b/solution.py
@@ -9,7 +9,7 @@
 
 
 AXES = ("rows", "cols")
-CHUNKS = 1
+CHUNKS = 2
 HALVES = 2
 SIDE = 4
 UP, DOWN = 3, 2
@@ -187,7 +187,7 @@
     ]
 
 
-def conv_kernel(pos, *refs, parts, sh, tr, pitch, rows, cols, at, out_at, many):
+def conv_kernel(pos, *refs, parts, sh, tr, pitch, rows, cols, at, cam_at, out_at, many):
     windows = refs[:parts]
     above, below, camera, w1, b1, w2, b2 = refs[parts : parts + 7]
     outs = refs[-5 - HALVES : -5]
@@ -233,7 +233,7 @@
             for dy in range(3):
                 lhs.append(tile[pl.ds(r + dy, n1)].reshape(m1, lidar))
                 lhs.append(taps[pl.ds(r + dy, n1)].reshape(m1, 2 * lidar))
-                lhs.append(camera[at + f, pl.ds(r + dy, n1)].reshape(m1, camera.shape[3]))
+                lhs.append(camera[cam_at + f, pl.ds(r + dy, n1)].reshape(m1, camera.shape[3]))
             acc = jnp.dot(jnp.concatenate(lhs, axis=1), w1[...], preferred_element_type=jnp.float32)
             v = jnp.maximum(acc + b1[...], 0.0).reshape(n1, pitch, joined)
             kept = []
@@ -459,7 +459,6 @@
                 ),
                 out_shape=[window] * members,
                 compiler_params=limit(6),
-                name="windows",
             )(jnp.stack([column_of((member + d) % members) for d in range(members)]).astype(jnp.int32), source)
             windows = [windows[0]] + [
                 send(windows[d], [(g * members + m, g * members + (m + d) % members) for g in range(groups) for m in range(members)])
@@ -477,14 +476,14 @@
                     shift.append((s, r * n_cols + HALVES * tile_of[r % 2][m] + (k + h) % HALVES))
                 shifts.append(shift)
             vmem = pl.BlockSpec(memory_space=pltpu.VMEM)
-            batch = step // 2 if step % 2 == 0 else step
+            batch = step
             for b0 in range(0, step, batch):
                 blocks = jax.ShapeDtypeStruct((batch, pairs2, 2, w, block), BF)
-                runs = [(0, batch)] if b0 == 0 else [(f, 1) for f in range(batch)]
+                runs = [(f, 1) for f in range(batch)]
                 tiles = []
                 for f1, many in runs:
                     tiles = pl.pallas_call(
-                        functools.partial(conv_kernel, parts=members, sh=sh, tr=tr, pitch=pitch, rows=rows, cols=cols, at=b0 + f1, out_at=f1, many=many),
+                        functools.partial(conv_kernel, parts=members, sh=sh, tr=tr, pitch=pitch, rows=rows, cols=cols, at=b0 + f1, cam_at=f0 + b0 + f1, out_at=f1, many=many),
                         in_specs=[pl.BlockSpec(memory_space=pltpu.SMEM)] + [vmem] * (members + 7 + len(tiles)),
                         out_specs=[vmem] * HALVES,
                         scratch_shapes=conv_scratch(tr, pitch, lidar_ch, joined, block, pairs2),

time: 154 us -> 129 us (0.84)
  waiting for transfers between devices: 47.1 us -> 12.8 us
  starting transfers between devices: 58.2 us -> 65.6 us
  Pallas kernels: 41 us -> 43.3 us
    ppermute x17 -> x22, waiting for transfers between devices: 47.1 us -> 12.8 us  [send(): return lax.ppermute(x, AXES, pairs)]
    ppermute x17 -> x22, starting transfers between devices: 58.2 us -> 65.6 us  [send(): return lax.ppermute(x, AXES, pairs)]
    unnamed x28 -> x40, local copies, waits for them, and re-layouts: 6.16 us -> 5.46 us
    pallas_call x3 -> x4, Pallas kernels: 24.9 us -> 25 us  [local(): pl.pallas_call(functools.partial(conv_kernel, parts=members, sh=sh, tr=tr...]
  transfers between devices with their start and end apart: 17 -> 22, of which waited for: 4 -> 4; matrix products, arithmetic and copies ran while one was open for 0% -> 0% of each run, Pallas kernels for 17% -> 30%
where the time goes in v5:
time: 129 us; the launch traced here: 128 us
  starting transfers between devices  65.6 us (51%)
  Pallas kernels  43.3 us (34%)
  waiting for transfers between devices  12.8 us (10%)
  local copies, waits for them, and re-layouts  5.46 us (4%)
    ppermute x22, starting transfers between devices, send(): return lax.ppermute(x, AXES, pairs)  65.6 us
    pallas_call x4, Pallas kernels, local(): pl.pallas_call(functools.partial(conv_kernel, parts=members, sh=sh, tr=tr...  25 us
    ppermute x22, waiting for transfers between devices, send(): return lax.ppermute(x, AXES, pairs)  12.8 us
    pallas_call x1, Pallas kernels, local(): pl.pallas_call(lambda *refs: camera_unpack_kernel(*refs, groups=groups, s...  5.89 us
    unnamed x40, local copies, waits for them, and re-layouts  5.46 us
    pallas_call x2, Pallas kernels, local(): pl.pallas_call(lambda *refs: encode_kernel(*refs, parts=HALVES, half_rows...  4.52 us
    pallas_call x2, Pallas kernels, local(): pl.pallas_call(functools.partial(window_kernel, tw=tw), grid_spec=pltpu.P...  2.78 us
  transfers between devices with their start and end apart: 22, of which 4 were waited for; matrix products, arithmetic and copies ran while one was open for 0% of the time, Pallas kernels for 30%

profile of v5, /device:TPU:0, one launch (start us, length us, event | category | flops | bytes accessed | tf_op | source)
XLA Modules:
  0.0 128.0 jit_solution(17466921971649735881)
XLA Ops:
  1.2 2.2 %camera_pack.1 = (bf16[12,80,128]{2,1,0:T(8,128)(2,1)S(1)}, bf16[12,80,128]{2,1,0:T(8,128)(2,1)S(1)}, bf16[12,80,128]{2,1,0:T(8,128)(2,1)}, bf16[12,80,128]{2,1,...) custom-call(s32[1]{0:T(128)} %bitcast.9.refs_0_, ...), custom_call_target="tpu_custom_call" | custom-call | tf_op jit(solution)/shard_map/camera_pack/pallas_call | solution.py:405
  4.7 6.8 %collective-permute-start.6 = (bf16[12,80,128]{2,1,0:T(8,128)(2,1)S(1)}, bf16[12,80,128]{2,1,0:T(8,128)(2,1)S(1)}, u32[]{:S(2)}, u32[]{:S(2)}) collective-permute-start(bf16[12,80,128]{2,1,0:T(8,128)(2,1)S(1)} %get-tuple-element.44), channel_id=1, source_target_pairs={{0,8},{2,18},{4,26},{6,0},{8,14},{10,20},{12,28},{14,6},{16,10},{1... | collective-permute-start | bytes 737288 | tf_op jit(solution)/shard_map/ppermute | solution.py:369
  14.3 1.7 %copy-done = bf16[4,6,192,256]{3,2,1,0:T(8,128)(2,1)S(1)} copy-done((bf16[4,6,192,256]{3,2,1,0:T(8,128)(2,1)S(1)}, bf16[4,6,192,256]{3,2,1,0:T(8,128)(2,1)}, u32[]{:S(2)}) %copy-start) | copy-done | bytes 2359320
  17.6 2.2 %collective-permute-start.15 = (bf16[2,6,56,256]{3,2,1,0:T(8,128)(2,1)S(1)}, bf16[2,6,56,256]{3,2,1,0:T(8,128)(2,1)S(1)}, u32[]{:S(2)}, u32[]{:S(2)}) collective-permute-start(bf16[2,6,56,256]{3,2,1,0:T(8,128)(2,1)S(1)} %get-tuple-element.58), channel_id=1, source_target_pairs={{0,2},{2,4},{4,6},{6,0},{8,10},{10,12},{12,14},{14,8},{16,18},{18,... | collective-permute-start | bytes 1032200 | tf_op jit(solution)/shard_map/ppermute | solution.py:369
  20.4 7.1 %collective-permute-start.16 = (bf16[2,6,56,256]{3,2,1,0:T(8,128)(2,1)S(1)}, bf16[2,6,56,256]{3,2,1,0:T(8,128)(2,1)S(1)}, u32[]{:S(2)}, u32[]{:S(2)}) collective-permute-start(bf16[2,6,56,256]{3,2,1,0:T(8,128)(2,1)S(1)} %get-tuple-element.59), channel_id=1, source_target_pairs={{0,4},{2,6},{4,0},{6,2},{8,12},{10,14},{12,8},{14,10},{16,20},{18,... | collective-permute-start | bytes 1032200 | tf_op jit(solution)/shard_map/ppermute | solution.py:369
  29.7 4.3 %collective-permute-start.7 = (bf16[12,80,128]{2,1,0:T(8,128)(2,1)}, bf16[12,80,128]{2,1,0:T(8,128)(2,1)}, u32[]{:S(2)}, u32[]{:S(2)}) collective-permute-start(bf16[12,80,128]{2,1,0:T(8,128)(2,1)} %get-tuple-element.45), channel_id=1, source_target_pairs={{0,18},{2,26},{4,0},{6,8},{8,20},{10,28},{12,6},{14,14},{16,16},{1... | collective-permute-start | bytes 737288 | tf_op jit(solution)/shard_map/ppermute | solution.py:369
  35.2 1.8 %shard_map.100 = (bf16[2,6,56,256]{3,2,1,0:T(8,128)(2,1)S(1)}, bf16[2,6,56,256]{3,2,1,0:T(8,128)(2,1)}, bf16[2,6,56,256]{3,2,1,0:T(8,128)(2,1)}, bf16[2,6,56,256]{3,2,1,0:T(8,128)(2,1)}) custom-call(s32[4]{0:T(128)S(1)} %pad_add_fusion.1.pos, bf16[4,6,192,256]{3,2,1,0:T(8,128)(2,1)S(1)} %copy-done), custom_call_target="tpu_custom_call" | custom-call | tf_op jit(solution)/shard_map/pallas_call | solution.py:452
  38.5 2.0 %collective-permute-start.1 = (bf16[2,6,56,256]{3,2,1,0:T(8,128)(2,1)}, bf16[2,6,56,256]{3,2,1,0:T(8,128)(2,1)}, u32[]{:S(2)}, u32[]{:S(2)}) collective-permute-start(bf16[2,6,56,256]{3,2,1,0:T(8,128)(2,1)} %get-tuple-element.40), channel_id=1, source_target_pairs={{0,4},{2,6},{4,0},{6,2},{8,12},{10,14},{12,8},{14,10},{16,20},{18,... | collective-permute-start | bytes 1032200 | tf_op jit(solution)/shard_map/ppermute | solution.py:369
  40.5 2.8 %collective-permute-done.17.refs_3_.refs_7_ = bf16[2,6,56,256]{3,2,1,0:T(8,128)(2,1)S(1)} collective-permute-done((bf16[2,6,56,256]{3,2,1,0:T(8,128)(2,1)S(1)}, bf16[2,6,56,256]{3,2,1,0:T(8,128)(2,1)S(1)}, u32[]{:S(2)}, u32[]{:S(2)}) %collective-permute-start.17) | collective-permute-done | bytes 344096 | tf_op jit(solution)/shard_map/ppermute | solution.py:369
  43.3 3.4 %collective-permute-start.2 = (bf16[2,6,56,256]{3,2,1,0:T(8,128)(2,1)}, bf16[2,6,56,256]{3,2,1,0:T(8,128)(2,1)}, u32[]{:S(2)}, u32[]{:S(2)}) collective-permute-start(bf16[2,6,56,256]{3,2,1,0:T(8,128)(2,1)} %get-tuple-element.41), channel_id=1, source_target_pairs={{0,6},{2,0},{4,2},{6,4},{8,14},{10,8},{12,10},{14,12},{16,22},{18,... | collective-permute-start | bytes 1032200 | tf_op jit(solution)/shard_map/ppermute | solution.py:369
  47.5 1.7 %collective-permute-done.7.refs_3_ = bf16[12,80,128]{2,1,0:T(8,128)(2,1)} collective-permute-done((bf16[12,80,128]{2,1,0:T(8,128)(2,1)}, bf16[12,80,128]{2,1,0:T(8,128)(2,1)}, u32[]{:S(2)}, u32[]{:S(2)}) %collective-permute-start.7) | collective-permute-done | bytes 245792 | tf_op jit(solution)/shard_map/ppermute | solution.py:369
  49.2 5.8 %collective-permute-start.18 = (bf16[2,3,56,256]{3,2,1,0:T(8,128)(2,1)S(1)}, bf16[2,3,56,256]{3,2,1,0:T(8,128)(2,1)S(1)}, u32[]{:S(2)}, u32[]{:S(2)}) collective-permute-start(bf16[2,3,56,256]{3,2,1,0:T(8,128)(2,1)S(1)} %get-tuple-element.61), channel_id=1, source_target_pairs={{0,8},{6,14},{2,10},{4,12},{8,18},{14,20},{10,16},{12,22},{18,26},... | collective-permute-start | bytes 516104 | tf_op jit(solution)/shard_map/ppermute | solution.py:369
  56.8 5.9 %camera_unpack.1 = bf16[128,64,256]{2,1,0:T(8,128)(2,1)S(1)} custom-call(s32[1]{0:T(128)} %bitcast.1.refs_0_, bf16[12,80,128]{2,1,0:T(8,128)(2,1)S(1)} %collective-permute-done.5.refs_1_, bf16[12,80,128]{2,1,0:T(8,128)(2,1)S(1)} %copy-done.7, bf16[12,80,128]{2,1,0:T(8,128)(2,1)} %collective-permute-done.7.refs_3_, ...), custom_call_target="tpu_custom_call" | custom-call | tf_op jit(solution)/shard_map/camera_unpack/pallas_call | solution.py:422
  63.1 1.9 %shard_map.101 = (bf16[2,3,56,256]{3,2,1,0:T(8,128)(2,1)S(1)}, bf16[2,2,56,256]{3,2,1,0:T(8,128)(2,1)S(1)}) custom-call(s32[2]{0:T(128)S(1)} %pad_add_fusion.2.pos, bf16[2,6,56,256]{3,2,1,0:T(8,128)(2,1)S(1)} %get-tuple-element.38.refs_0_.refs_4_, bf16[2,6,56,256]{3,2,1,0:T(8,128)(2,1)} %collective-permute-done.refs_1_.refs_5_, ...), custom_call_target="tpu_custom_call" | custom-call | tf_op jit(solution)/shard_map/pallas_call | solution.py:172
  64.9 9.1 %collective-permute-start.3 = (bf16[2,3,56,256]{3,2,1,0:T(8,128)(2,1)S(1)}, bf16[2,3,56,256]{3,2,1,0:T(8,128)(2,1)S(1)}, u32[]{:S(2)}, u32[]{:S(2)}) collective-permute-start(bf16[2,3,56,256]{3,2,1,0:T(8,128)(2,1)S(1)} %get-tuple-element.42), channel_id=1, source_target_pairs={{0,8},{6,14},{2,10},{4,12},{8,18},{14,20},{10,16},{12,22},{18,26},... | collective-permute-start | bytes 516104 | tf_op jit(solution)/shard_map/ppermute | solution.py:369
  75.4 5.9 %shard_map.106 = (bf16[2,13,2,24,128]{4,3,2,1,0:T(8,128)(2,1)S(1)}, bf16[2,13,2,24,128]{4,3,2,1,0:T(8,128)(2,1)S(1)}) custom-call(s32[4]{0:T(128)S(1)} %pad_add_fusion.pos, bf16[2,6,56,256]{3,2,1,0:T(8,128)(2,1)S(1)} %get-tuple-element.57.refs_0_.refs_4_, bf16[2,6,56,256]{3,2,1,0:T(8,128)(2,1)S(1)} %collective-permute-done.15.refs_1_.refs_5_, ...), custom_call_target="tpu_custom_call" | custom-call | flops 4127195136 | bytes 2000000 | tf_op jit(solution)/shard_map/pallas_call | solution.py:485
  81.3 5.9 %shard_map.107 = (bf16[2,13,2,24,128]{4,3,2,1,0:T(8,128)(2,1)S(1)}, bf16[2,13,2,24,128]{4,3,2,1,0:T(8,128)(2,1)S(1)}) custom-call(s32[4]{0:T(128)S(1)} %pad_add_fusion.pos, bf16[2,6,56,256]{3,2,1,0:T(8,128)(2,1)S(1)} %get-tuple-element.57.refs_0_.refs_4_, ...), custom_call_target="tpu_custom_call", output_to_operand_aliasing={{0}: (12, {}), {1}: (13, {})} | custom-call | flops 4127195136 | bytes 2000000 | tf_op jit(solution)/shard_map/pallas_call | solution.py:485
  87.9 8.7 %collective-permute-start.21 = (bf16[2,13,2,24,128]{4,3,2,1,0:T(8,128)(2,1)S(1)}, bf16[2,13,2,24,128]{4,3,2,1,0:T(8,128)(2,1)S(1)}, u32[]{:S(2)}, u32[]{:S(2)}) collective-permute-start(bf16[2,13,2,24,128]{4,3,2,1,0:T(8,128)(2,1)S(1)} %get-tuple-element.66), channel_id=1, source_target_pairs={{0,2},{2,10},{4,14},{6,6},{8,0},{10,8},{12,12},{14,4},{16,26},{18,... | collective-permute-start | bytes 958472 | tf_op jit(solution)/shard_map/ppermute | solution.py:369
  96.7 6.6 %shard_map.102 = (bf16[2,13,2,24,128]{4,3,2,1,0:T(8,128)(2,1)S(1)}, bf16[2,13,2,24,128]{4,3,2,1,0:T(8,128)(2,1)S(1)}) custom-call(s32[4]{0:T(128)S(1)} %pad_add_fusion.pos, bf16[2,6,56,256]{3,2,1,0:T(8,128)(2,1)S(1)} %get-tuple-element.38.refs_0_.refs_4_, bf16[2,6,56,256]{3,2,1,0:T(8,128)(2,1)} %collective-permute-done.refs_1_.refs_5_, ...), custom_call_target="tpu_custom_call" | custom-call | flops 4127195136 | bytes 2000000 | tf_op jit(solution)/shard_map/pallas_call | solution.py:485
  103.4 6.6 %shard_map.103 = (bf16[2,13,2,24,128]{4,3,2,1,0:T(8,128)(2,1)S(1)}, bf16[2,13,2,24,128]{4,3,2,1,0:T(8,128)(2,1)S(1)}) custom-call(s32[4]{0:T(128)S(1)} %pad_add_fusion.pos, bf16[2,6,56,256]{3,2,1,0:T(8,128)(2,1)S(1)} %get-tuple-element.38.refs_0_.refs_4_, ...), custom_call_target="tpu_custom_call", output_to_operand_aliasing={{0}: (12, {}), {1}: (13, {})} | custom-call | flops 4127195136 | bytes 2000000 | tf_op jit(solution)/shard_map/pallas_call | solution.py:485
  110.7 4.8 %collective-permute-start.14 = (bf16[2,13,2,24,128]{4,3,2,1,0:T(8,128)(2,1)S(1)}, bf16[2,13,2,24,128]{4,3,2,1,0:T(8,128)(2,1)S(1)}, u32[]{:S(2)}, u32[]{:S(2)}) collective-permute-start(bf16[2,13,2,24,128]{4,3,2,1,0:T(8,128)(2,1)S(1)} %get-tuple-element.56), channel_id=1, source_target_pairs={{0,2},{2,10},{4,14},{6,6},{8,0},{10,8},{12,12},{14,4},{16,26},{18,... | collective-permute-start | bytes 958472 | tf_op jit(solution)/shard_map/ppermute | solution.py:369
  115.5 2.3 %shard_map.108.refs_7_ = bf16[4,24,2,24,256]{4,3,2,1,0:T(8,128)(2,1)} custom-call(s32[1]{0:T(128)} %bitcast.refs_0_, bf16[2,13,2,24,128]{4,3,2,1,0:T(8,128)(2,1)S(1)} %collective-permute-done.20.refs_1_, bf16[2,13,2,24,128]{4,3,2,1,0:T(8,128)(2,1)S(1)} %collective-permute-done.21.refs_2_, bf16[1152,256]{1,0:T(8,128)(2,1)S(1)} %bitcast.25, ...), custom_call_target="tpu_custom_call" | custom-call | flops 452984832 | bytes 2000000 | tf_op jit(solution)/shard_map/pallas_call | solution.py:499
  117.8 8.0 %collective-permute-done.14.refs_2_ = bf16[2,13,2,24,128]{4,3,2,1,0:T(8,128)(2,1)S(1)} collective-permute-done((bf16[2,13,2,24,128]{4,3,2,1,0:T(8,128)(2,1)S(1)}, bf16[2,13,2,24,128]{4,3,2,1,0:T(8,128)(2,1)S(1)}, u32[]{:S(2)}, u32[]{:S(2)}) %collective-permute-start.14) | collective-permute-done | bytes 319520 | tf_op jit(solution)/shard_map/ppermute | solution.py:369
  125.8 2.2 %shard_map.109 = bf16[4,24,2,24,256]{4,3,2,1,0:T(8,128)(2,1)} custom-call(s32[1]{0:T(128)} %bitcast.refs_0_, bf16[2,13,2,24,128]{4,3,2,1,0:T(8,128)(2,1)S(1)} %collective-permute-done.13.refs_1_, bf16[2,13,2,24,128]{4,3,2,1,0:T(8,128)(2,1)S(1)} %collective-permute-done.14.refs_2_, bf16[1152,256]{1,0:T(8,128)(2,1)S(1)} %bitcast.26, ...), custom_call_target="tpu_custom_call", output_to_operand_aliasing={{}: (7, {})} | custom-call | flops 452984832 | bytes 2000000 | tf_op jit(solution)/shard_map/pallas_call | solution.py:499
  (77 shorter events, 17.9 us)
Async XLA Ops:
  3.4 9.6 %collective-permute-start.9 = (bf16[3,80,128]{2,1,0:T(8,128)(2,1)S(1)}, bf16[3,80,128]{2,1,0:T(8,128)(2,1)S(1)}, u32[]{:S(2)}, u32[]{:S(2)}) collective-permute-start(bf16[3,80,128]{2,1,0:T(8,128)(2,1)S(1)} %get-tuple-element.47), channel_id=1, source_target_pairs={{6,6},{14,2},{22,4},{8,8},{16,14},{24,10},{7,7},{15,3},{23,5},{9,9... | collective-permute-start | bytes 184328 | tf_op jit(solution)/shard_map/ppermute | solution.py:369
  4.0 25.7 %collective-permute-start.5 = (bf16[12,80,128]{2,1,0:T(8,128)(2,1)S(1)}, bf16[12,80,128]{2,1,0:T(8,128)(2,1)S(1)}, u32[]{:S(2)}, u32[]{:S(2)}) collective-permute-start(bf16[12,80,128]{2,1,0:T(8,128)(2,1)S(1)} %get-tuple-element.36), channel_id=1, source_target_pairs={{0,0},{2,8},{4,18},{6,26},{8,6},{10,14},{12,20},{14,28},{16,2},{18... | collective-permute-start | bytes 737288 | tf_op jit(solution)/shard_map/ppermute | solution.py:369
  4.7 29.3 %collective-permute-start.6 = (bf16[12,80,128]{2,1,0:T(8,128)(2,1)S(1)}, bf16[12,80,128]{2,1,0:T(8,128)(2,1)S(1)}, u32[]{:S(2)}, u32[]{:S(2)}) collective-permute-start(bf16[12,80,128]{2,1,0:T(8,128)(2,1)S(1)} %get-tuple-element.44), channel_id=1, source_target_pairs={{0,8},{2,18},{4,26},{6,0},{8,14},{10,20},{12,28},{14,6},{16,10},{1... | collective-permute-start | bytes 737288 | tf_op jit(solution)/shard_map/ppermute | solution.py:369
  11.5 5.5 %collective-permute-start.10 = (bf16[3,80,128]{2,1,0:T(8,128)(2,1)S(1)}, bf16[3,80,128]{2,1,0:T(8,128)(2,1)S(1)}, u32[]{:S(2)}, u32[]{:S(2)}) collective-permute-start(bf16[3,80,128]{2,1,0:T(8,128)(2,1)S(1)} %get-tuple-element.48), channel_id=1, source_target_pairs={{6,14},{14,10},{22,12},{8,18},{16,20},{24,16},{7,15},{15,11},{23,1... | collective-permute-start | bytes 184328 | tf_op jit(solution)/shard_map/ppermute | solution.py:369
  12.1 7.7 %collective-permute-start.11 = (bf16[3,80,128]{2,1,0:T(8,128)(2,1)S(1)}, bf16[3,80,128]{2,1,0:T(8,128)(2,1)S(1)}, u32[]{:S(2)}, u32[]{:S(2)}) collective-permute-start(bf16[3,80,128]{2,1,0:T(8,128)(2,1)S(1)} %get-tuple-element.49), channel_id=1, source_target_pairs={{6,20},{14,16},{22,22},{8,26},{16,28},{24,24},{7,21},{15,17},{23,2... | collective-permute-start | bytes 184328 | tf_op jit(solution)/shard_map/ppermute | solution.py:369
  12.9 21.7 %copy-start.8 = (bf16[3,80,128]{2,1,0:T(8,128)(2,1)}, bf16[3,80,128]{2,1,0:T(8,128)(2,1)S(1)}, u32[]{:S(2)}) copy-start(bf16[3,80,128]{2,1,0:T(8,128)(2,1)S(1)} %collective-permute-done.9.refs_5_) | copy-start | bytes 184324
  13.0 14.6 %collective-permute-start.12 = (bf16[3,80,128]{2,1,0:T(8,128)(2,1)S(1)}, bf16[3,80,128]{2,1,0:T(8,128)(2,1)S(1)}, u32[]{:S(2)}, u32[]{:S(2)}) collective-permute-start(bf16[3,80,128]{2,1,0:T(8,128)(2,1)S(1)} %get-tuple-element.50), channel_id=1, source_target_pairs={{6,28},{14,24},{22,30},{8,0},{16,6},{24,2},{7,29},{15,25},{23,31},... | collective-permute-start | bytes 184328 | tf_op jit(solution)/shard_map/ppermute | solution.py:369
  17.6 19.4 %collective-permute-start.15 = (bf16[2,6,56,256]{3,2,1,0:T(8,128)(2,1)S(1)}, bf16[2,6,56,256]{3,2,1,0:T(8,128)(2,1)S(1)}, u32[]{:S(2)}, u32[]{:S(2)}) collective-permute-start(bf16[2,6,56,256]{3,2,1,0:T(8,128)(2,1)S(1)} %get-tuple-element.58), channel_id=1, source_target_pairs={{0,2},{2,4},{4,6},{6,0},{8,10},{10,12},{12,14},{14,8},{16,18},{18,... | collective-permute-start | bytes 1032200 | tf_op jit(solution)/shard_map/ppermute | solution.py:369
  20.4 18.1 %collective-permute-start.16 = (bf16[2,6,56,256]{3,2,1,0:T(8,128)(2,1)S(1)}, bf16[2,6,56,256]{3,2,1,0:T(8,128)(2,1)S(1)}, u32[]{:S(2)}, u32[]{:S(2)}) collective-permute-start(bf16[2,6,56,256]{3,2,1,0:T(8,128)(2,1)S(1)} %get-tuple-element.59), channel_id=1, source_target_pairs={{0,4},{2,6},{4,0},{6,2},{8,12},{10,14},{12,8},{14,10},{16,20},{18,... | collective-permute-start | bytes 1032200 | tf_op jit(solution)/shard_map/ppermute | solution.py:369
  28.1 15.2 %collective-permute-start.17 = (bf16[2,6,56,256]{3,2,1,0:T(8,128)(2,1)S(1)}, bf16[2,6,56,256]{3,2,1,0:T(8,128)(2,1)S(1)}, u32[]{:S(2)}, u32[]{:S(2)}) collective-permute-start(bf16[2,6,56,256]{3,2,1,0:T(8,128)(2,1)S(1)} %get-tuple-element.60), channel_id=1, source_target_pairs={{0,6},{2,0},{4,2},{6,4},{8,14},{10,8},{12,10},{14,12},{16,22},{18,... | collective-permute-start | bytes 1032200 | tf_op jit(solution)/shard_map/ppermute | solution.py:369
  29.7 19.5 %collective-permute-start.7 = (bf16[12,80,128]{2,1,0:T(8,128)(2,1)}, bf16[12,80,128]{2,1,0:T(8,128)(2,1)}, u32[]{:S(2)}, u32[]{:S(2)}) collective-permute-start(bf16[12,80,128]{2,1,0:T(8,128)(2,1)} %get-tuple-element.45), channel_id=1, source_target_pairs={{0,18},{2,26},{4,0},{6,8},{8,20},{10,28},{12,6},{14,14},{16,16},{1... | collective-permute-start | bytes 737288 | tf_op jit(solution)/shard_map/ppermute | solution.py:369
  34.7 21.7 %copy-start.2 = (bf16[3,3,336,256]{3,2,1,0:T(8,128)(2,1)S(1)}, bf16[3,3,336,256]{3,2,1,0:T(8,128)(2,1)}, u32[]{:S(2)}) copy-start(bf16[3,3,336,256]{3,2,1,0:T(8,128)(2,1)} %param.12) | copy-start | bytes 4644868
  34.7 20.3 %collective-permute-start.8 = (bf16[12,80,128]{2,1,0:T(8,128)(2,1)}, bf16[12,80,128]{2,1,0:T(8,128)(2,1)}, u32[]{:S(2)}, u32[]{:S(2)}) collective-permute-start(bf16[12,80,128]{2,1,0:T(8,128)(2,1)} %get-tuple-element.46), channel_id=1, source_target_pairs={{0,26},{2,0},{4,8},{6,18},{8,28},{10,6},{12,14},{14,20},{16,24},{1... | collective-permute-start | bytes 737288 | tf_op jit(solution)/shard_map/ppermute | solution.py:369
  37.0 25.7 %collective-permute-start = (bf16[2,6,56,256]{3,2,1,0:T(8,128)(2,1)}, bf16[2,6,56,256]{3,2,1,0:T(8,128)(2,1)}, u32[]{:S(2)}, u32[]{:S(2)}) collective-permute-start(bf16[2,6,56,256]{3,2,1,0:T(8,128)(2,1)} %get-tuple-element.39), channel_id=1, source_target_pairs={{0,2},{2,4},{4,6},{6,0},{8,10},{10,12},{12,14},{14,8},{16,18},{18,... | collective-permute-start | bytes 1032200 | tf_op jit(solution)/shard_map/ppermute | solution.py:369
  38.5 24.2 %collective-permute-start.1 = (bf16[2,6,56,256]{3,2,1,0:T(8,128)(2,1)}, bf16[2,6,56,256]{3,2,1,0:T(8,128)(2,1)}, u32[]{:S(2)}, u32[]{:S(2)}) collective-permute-start(bf16[2,6,56,256]{3,2,1,0:T(8,128)(2,1)} %get-tuple-element.40), channel_id=1, source_target_pairs={{0,4},{2,6},{4,0},{6,2},{8,12},{10,14},{12,8},{14,10},{16,20},{18,... | collective-permute-start | bytes 1032200 | tf_op jit(solution)/shard_map/ppermute | solution.py:369
  43.3 19.7 %collective-permute-start.2 = (bf16[2,6,56,256]{3,2,1,0:T(8,128)(2,1)}, bf16[2,6,56,256]{3,2,1,0:T(8,128)(2,1)}, u32[]{:S(2)}, u32[]{:S(2)}) collective-permute-start(bf16[2,6,56,256]{3,2,1,0:T(8,128)(2,1)} %get-tuple-element.41), channel_id=1, source_target_pairs={{0,6},{2,0},{4,2},{6,4},{8,14},{10,8},{12,10},{14,12},{16,22},{18,... | collective-permute-start | bytes 1032200 | tf_op jit(solution)/shard_map/ppermute | solution.py:369
  49.2 26.2 %collective-permute-start.18 = (bf16[2,3,56,256]{3,2,1,0:T(8,128)(2,1)S(1)}, bf16[2,3,56,256]{3,2,1,0:T(8,128)(2,1)S(1)}, u32[]{:S(2)}, u32[]{:S(2)}) collective-permute-start(bf16[2,3,56,256]{3,2,1,0:T(8,128)(2,1)S(1)} %get-tuple-element.61), channel_id=1, source_target_pairs={{0,8},{6,14},{2,10},{4,12},{8,18},{14,20},{10,16},{12,22},{18,26},... | collective-permute-start | bytes 516104 | tf_op jit(solution)/shard_map/ppermute | solution.py:369
  55.0 20.4 %collective-permute-start.19 = (bf16[2,2,56,256]{3,2,1,0:T(8,128)(2,1)S(1)}, bf16[2,2,56,256]{3,2,1,0:T(8,128)(2,1)S(1)}, u32[]{:S(2)}, u32[]{:S(2)}) collective-permute-start(bf16[2,2,56,256]{3,2,1,0:T(8,128)(2,1)S(1)} %get-tuple-element.62), channel_id=1, source_target_pairs={{8,0},{14,6},{10,2},{12,4},{18,8},{20,14},{16,10},{22,12},{26,18},... | collective-permute-start | bytes 344072 | tf_op jit(solution)/shard_map/ppermute | solution.py:369
  64.9 31.8 %collective-permute-start.3 = (bf16[2,3,56,256]{3,2,1,0:T(8,128)(2,1)S(1)}, bf16[2,3,56,256]{3,2,1,0:T(8,128)(2,1)S(1)}, u32[]{:S(2)}, u32[]{:S(2)}) collective-permute-start(bf16[2,3,56,256]{3,2,1,0:T(8,128)(2,1)S(1)} %get-tuple-element.42), channel_id=1, source_target_pairs={{0,8},{6,14},{2,10},{4,12},{8,18},{14,20},{10,16},{12,22},{18,26},... | collective-permute-start | bytes 516104 | tf_op jit(solution)/shard_map/ppermute | solution.py:369
  74.1 22.6 %collective-permute-start.4 = (bf16[2,2,56,256]{3,2,1,0:T(8,128)(2,1)S(1)}, bf16[2,2,56,256]{3,2,1,0:T(8,128)(2,1)S(1)}, u32[]{:S(2)}, u32[]{:S(2)}) collective-permute-start(bf16[2,2,56,256]{3,2,1,0:T(8,128)(2,1)S(1)} %get-tuple-element.43), channel_id=1, source_target_pairs={{8,0},{14,6},{10,2},{12,4},{18,8},{20,14},{16,10},{22,12},{26,18},... | collective-permute-start | bytes 344072 | tf_op jit(solution)/shard_map/ppermute | solution.py:369
  87.3 28.2 %collective-permute-start.20 = (bf16[2,13,2,24,128]{4,3,2,1,0:T(8,128)(2,1)S(1)}, bf16[2,13,2,24,128]{4,3,2,1,0:T(8,128)(2,1)S(1)}, u32[]{:S(2)}, u32[]{:S(2)}) collective-permute-start(bf16[2,13,2,24,128]{4,3,2,1,0:T(8,128)(2,1)S(1)} %get-tuple-element.65), channel_id=1, source_target_pairs={{0,0},{2,8},{4,12},{6,4},{8,2},{10,10},{12,14},{14,6},{16,24},{18,... | collective-permute-start | bytes 958472 | tf_op jit(solution)/shard_map/ppermute | solution.py:369
  87.9 27.5 %collective-permute-start.21 = (bf16[2,13,2,24,128]{4,3,2,1,0:T(8,128)(2,1)S(1)}, bf16[2,13,2,24,128]{4,3,2,1,0:T(8,128)(2,1)S(1)}, u32[]{:S(2)}, u32[]{:S(2)}) collective-permute-start(bf16[2,13,2,24,128]{4,3,2,1,0:T(8,128)(2,1)S(1)} %get-tuple-element.66), channel_id=1, source_target_pairs={{0,2},{2,10},{4,14},{6,6},{8,0},{10,8},{12,12},{14,4},{16,26},{18,... | collective-permute-start | bytes 958472 | tf_op jit(solution)/shard_map/ppermute | solution.py:369
  110.0 7.8 %collective-permute-start.13 = (bf16[2,13,2,24,128]{4,3,2,1,0:T(8,128)(2,1)S(1)}, bf16[2,13,2,24,128]{4,3,2,1,0:T(8,128)(2,1)S(1)}, u32[]{:S(2)}, u32[]{:S(2)}) collective-permute-start(bf16[2,13,2,24,128]{4,3,2,1,0:T(8,128)(2,1)S(1)} %get-tuple-element.55), channel_id=1, source_target_pairs={{0,0},{2,8},{4,12},{6,4},{8,2},{10,10},{12,14},{14,6},{16,24},{18,... | collective-permute-start | bytes 958472 | tf_op jit(solution)/shard_map/ppermute | solution.py:369
  110.7 15.1 %collective-permute-start.14 = (bf16[2,13,2,24,128]{4,3,2,1,0:T(8,128)(2,1)S(1)}, bf16[2,13,2,24,128]{4,3,2,1,0:T(8,128)(2,1)S(1)}, u32[]{:S(2)}, u32[]{:S(2)}) collective-permute-start(bf16[2,13,2,24,128]{4,3,2,1,0:T(8,128)(2,1)S(1)} %get-tuple-element.56), channel_id=1, source_target_pairs={{0,2},{2,10},{4,14},{6,6},{8,0},{10,8},{12,12},{14,4},{16,26},{18,... | collective-permute-start | bytes 958472 | tf_op jit(solution)/shard_map/ppermute | solution.py:369
  (18 other events, 136.2 us)

commit v6 on v5

--- a/solution.py
+++ b/solution.py
@@ -9,7 +9,7 @@
 
 
 AXES = ("rows", "cols")
-CHUNKS = 2
+CHUNKS = 1
 HALVES = 2
 SIDE = 4
 UP, DOWN = 3, 2
@@ -206,11 +206,11 @@
     inside[...] = jnp.where((col >= 0) & (col < cols), 1.0, 0.0)
 
     def frame(f, _):
-        tile[0:UP, 0:wide, :] = above[at + f]
+        tile[0:UP, 0:wide, :] = above[out_at + f]
         for d in range(parts):
             source = lax.rem(member - d + parts, parts)
             tile[pl.ds(UP + source * sh, sh), 0:wide, :] = windows[d][at + f]
-        tile[UP + tr : UP + tr + DOWN, 0:wide, :] = below[at + f]
+        tile[UP + tr : UP + tr + DOWN, 0:wide, :] = below[out_at + f]
 
         step = 6
         flat = step * pitch
@@ -458,15 +458,17 @@
                     out_specs=[framed(window)] * members,
                 ),
                 out_shape=[window] * members,
-                compiler_params=limit(6),
+                compiler_params=limit(60),
             )(jnp.stack([column_of((member + d) % members) for d in range(members)]).astype(jnp.int32), source)
             windows = [windows[0]] + [
                 send(windows[d], [(g * members + m, g * members + (m + d) % members) for g in range(groups) for m in range(members)])
                 for d in range(1, members)
             ]
             last, head = pick(windows, (member + 1) % members, member, 1)
-            above = across(last, 1, 0)
-            below = across(head, -1, 0)
+            batch = step // 2 if step % 2 == 0 else step
+            rims = []
+            for b0 in range(0, step, batch):
+                rims.append((across(last[b0 : b0 + batch], 1, 0), across(head[b0 : b0 + batch], -1, 0)))
             shifts = []
             for h in range(HALVES):
                 shift = []
@@ -476,10 +478,10 @@
                     shift.append((s, r * n_cols + HALVES * tile_of[r % 2][m] + (k + h) % HALVES))
                 shifts.append(shift)
             vmem = pl.BlockSpec(memory_space=pltpu.VMEM)
-            batch = step
             for b0 in range(0, step, batch):
                 blocks = jax.ShapeDtypeStruct((batch, pairs2, 2, w, block), BF)
-                runs = [(f, 1) for f in range(batch)]
+                above, below = rims[b0 // batch]
+                runs = [(0, batch)] if b0 == 0 else [(f, 1) for f in range(batch)]
                 tiles = []
                 for f1, many in runs:
                     tiles = pl.pallas_call(

time: 129 us -> 137 us (1.062)
  the two profiles are of different devices: /device:TPU:0 before, /device:TPU:26 now
where the time goes in v6:
time: 137 us; the launch traced here: 136 us
  starting transfers between devices  45.4 us (33%)
  waiting for transfers between devices  45 us (33%)
  Pallas kernels  40.8 us (30%)
  local copies, waits for them, and re-layouts  3.66 us (3%)
    ppermute x19, starting transfers between devices, send(): return lax.ppermute(x, AXES, pairs)  45.4 us
    ppermute x19, waiting for transfers between devices, send(): return lax.ppermute(x, AXES, pairs)  45 us
    pallas_call x3, Pallas kernels, local(): pl.pallas_call(functools.partial(conv_kernel, parts=members, sh=sh, tr=tr...  23.3 us
    pallas_call x1, Pallas kernels, local(): pl.pallas_call(functools.partial(window_kernel, tw=tw), grid_spec=pltpu.P...  4.9 us
    pallas_call x1, Pallas kernels, local(): pl.pallas_call(lambda *refs: camera_unpack_kernel(*refs, groups=groups, s...  4.83 us
    pallas_call x2, Pallas kernels, local(): pl.pallas_call(lambda *refs: encode_kernel(*refs, parts=HALVES, half_rows...  4.52 us
    unnamed x32, local copies, waits for them, and re-layouts  3.62 us
  transfers between devices with their start and end apart: 19, of which 5 were waited for; matrix products, arithmetic and copies ran while one was open for 0% of the time, Pallas kernels for 25%

profile of v6, /device:TPU:26, one launch (start us, length us, event | category | flops | bytes accessed | tf_op | source)
XLA Modules:
  0.0 136.1 jit_solution(15968088017014551738)
XLA Ops:
  0.6 4.9 %shard_map.100 = (bf16[4,6,56,256]{3,2,1,0:T(8,128)(2,1)}, bf16[4,6,56,256]{3,2,1,0:T(8,128)(2,1)}, bf16[4,6,56,256]{3,2,1,0:T(8,128)(2,1)}, bf16[4,6,56,256]{3,2,1,0:T(8,128)(2,1)}) custom-call(s32[4]{0:T(128)} %pad_add_fusion.1.pos, bf16[4,6,192,256]{3,2,1,0:T(8,128)(2,1)} %x.1), custom_call_target="tpu_custom_call" | custom-call | tf_op jit(solution)/shard_map/pallas_call | solution.py:452
  5.5 1.5 %collective-permute-start = (bf16[4,6,56,256]{3,2,1,0:T(8,128)(2,1)}, bf16[4,6,56,256]{3,2,1,0:T(8,128)(2,1)S(1)}, u32[]{:S(2)}, u32[]{:S(2)}) collective-permute-start(bf16[4,6,56,256]{3,2,1,0:T(8,128)(2,1)} %get-tuple-element.28), channel_id=1, source_target_pairs={{0,2},{2,4},{4,6},{6,0},{8,10},{10,12},{12,14},{14,8},{16,18},{18,... | collective-permute-start | bytes 2064392 | tf_op jit(solution)/shard_map/ppermute | solution.py:369
  7.5 1.4 %collective-permute-start.2 = (bf16[4,6,56,256]{3,2,1,0:T(8,128)(2,1)}, bf16[4,6,56,256]{3,2,1,0:T(8,128)(2,1)S(1)}, u32[]{:S(2)}, u32[]{:S(2)}) collective-permute-start(bf16[4,6,56,256]{3,2,1,0:T(8,128)(2,1)} %get-tuple-element.30), channel_id=1, source_target_pairs={{0,6},{2,0},{4,2},{6,4},{8,14},{10,8},{12,10},{14,12},{16,22},{18,... | collective-permute-start | bytes 2064392 | tf_op jit(solution)/shard_map/ppermute | solution.py:369
  8.9 2.1 %camera_pack.1 = (bf16[12,80,128]{2,1,0:T(8,128)(2,1)}, bf16[12,80,128]{2,1,0:T(8,128)(2,1)}, bf16[12,80,128]{2,1,0:T(8,128)(2,1)S(1)}, bf16[12,80,128]{2,1,0:T(...) custom-call(s32[1]{0:T(128)} %bitcast.10.refs_0_, ...), custom_call_target="tpu_custom_call" | custom-call | tf_op jit(solution)/shard_map/camera_pack/pallas_call | solution.py:405
  13.5 2.3 %collective-permute-start.5 = (bf16[12,80,128]{2,1,0:T(8,128)(2,1)}, bf16[12,80,128]{2,1,0:T(8,128)(2,1)S(1)}, u32[]{:S(2)}, u32[]{:S(2)}) collective-permute-start(bf16[12,80,128]{2,1,0:T(8,128)(2,1)} %get-tuple-element.33), channel_id=1, source_target_pairs={{0,0},{2,8},{4,18},{6,26},{8,6},{10,14},{12,20},{14,28},{16,2},{18... | collective-permute-start | bytes 737288 | tf_op jit(solution)/shard_map/ppermute | solution.py:369
  16.0 13.2 %collective-permute-done.refs_1_.refs_5_ = bf16[4,6,56,256]{3,2,1,0:T(8,128)(2,1)S(1)} collective-permute-done((bf16[4,6,56,256]{3,2,1,0:T(8,128)(2,1)}, bf16[4,6,56,256]{3,2,1,0:T(8,128)(2,1)S(1)}, u32[]{:S(2)}, u32[]{:S(2)}) %collective-permute-start) | collective-permute-done | bytes 688160 | tf_op jit(solution)/shard_map/ppermute | solution.py:369
  30.5 13.3 %collective-permute-done.2.refs_3_.refs_7_ = bf16[4,6,56,256]{3,2,1,0:T(8,128)(2,1)S(1)} collective-permute-done((bf16[4,6,56,256]{3,2,1,0:T(8,128)(2,1)}, bf16[4,6,56,256]{3,2,1,0:T(8,128)(2,1)S(1)}, u32[]{:S(2)}, u32[]{:S(2)}) %collective-permute-start.2) | collective-permute-done | bytes 688160 | tf_op jit(solution)/shard_map/ppermute | solution.py:369
  47.0 4.8 %collective-permute-start.7 = (bf16[12,80,128]{2,1,0:T(8,128)(2,1)S(1)}, bf16[12,80,128]{2,1,0:T(8,128)(2,1)S(1)}, u32[]{:S(2)}, u32[]{:S(2)}) collective-permute-start(bf16[12,80,128]{2,1,0:T(8,128)(2,1)S(1)} %get-tuple-element.35), channel_id=1, source_target_pairs={{0,18},{2,26},{4,0},{6,8},{8,20},{10,28},{12,6},{14,14},{16,16},{1... | collective-permute-start | bytes 737288 | tf_op jit(solution)/shard_map/ppermute | solution.py:369
  51.8 4.8 %collective-permute-start.8 = (bf16[12,80,128]{2,1,0:T(8,128)(2,1)S(1)}, bf16[12,80,128]{2,1,0:T(8,128)(2,1)S(1)}, u32[]{:S(2)}, u32[]{:S(2)}) collective-permute-start(bf16[12,80,128]{2,1,0:T(8,128)(2,1)S(1)} %get-tuple-element.36), channel_id=1, source_target_pairs={{0,26},{2,0},{4,8},{6,18},{8,28},{10,6},{12,14},{14,20},{16,24},{1... | collective-permute-start | bytes 737288 | tf_op jit(solution)/shard_map/ppermute | solution.py:369
  57.9 7.6 %collective-permute-done.12.refs_8_ = bf16[3,80,128]{2,1,0:T(8,128)(2,1)S(1)} collective-permute-done((bf16[3,80,128]{2,1,0:T(8,128)(2,1)S(1)}, bf16[3,80,128]{2,1,0:T(8,128)(2,1)S(1)}, u32[]{:S(2)}, u32[]{:S(2)}) %collective-permute-start.12) | collective-permute-done | bytes 61472 | tf_op jit(solution)/shard_map/ppermute | solution.py:369
  66.8 5.5 %collective-permute-start.16 = (bf16[2,2,56,256]{3,2,1,0:T(8,128)(2,1)S(1)}, bf16[2,2,56,256]{3,2,1,0:T(8,128)(2,1)S(1)}, u32[]{:S(2)}, u32[]{:S(2)}) collective-permute-start(bf16[2,2,56,256]{3,2,1,0:T(8,128)(2,1)S(1)} %get-tuple-element.51), channel_id=1, source_target_pairs={{8,0},{14,6},{10,2},{12,4},{18,8},{20,14},{16,10},{22,12},{26,18},... | collective-permute-start | bytes 344072 | tf_op jit(solution)/shard_map/ppermute | solution.py:369
  72.8 4.8 %camera_unpack.1 = bf16[128,64,256]{2,1,0:T(8,128)(2,1)S(1)} custom-call(s32[1]{0:T(128)} %bitcast.1.refs_0_, bf16[12,80,128]{2,1,0:T(8,128)(2,1)S(1)} %collective-permute-done.5.refs_1_, bf16[12,80,128]{2,1,0:T(8,128)(2,1)S(1)} %collective-permute-done.6.refs_2_, bf16[12,80,128]{2,1,0:T(8,128)(2,1)S(1)} %collective-permute-done.7.refs_3_, ...), custom_call_target="tpu_custom_call" | custom-call | tf_op jit(solution)/shard_map/camera_unpack/pallas_call | solution.py:422
  78.9 5.5 %collective-permute-start.4 = (bf16[2,2,56,256]{3,2,1,0:T(8,128)(2,1)S(1)}, bf16[2,2,56,256]{3,2,1,0:T(8,128)(2,1)S(1)}, u32[]{:S(2)}, u32[]{:S(2)}) collective-permute-start(bf16[2,2,56,256]{3,2,1,0:T(8,128)(2,1)S(1)} %get-tuple-element.52), channel_id=1, source_target_pairs={{8,0},{14,6},{10,2},{12,4},{18,8},{20,14},{16,10},{22,12},{26,18},... | collective-permute-start | bytes 344072 | tf_op jit(solution)/shard_map/ppermute | solution.py:369
  84.4 11.3 %shard_map.104 = (bf16[2,13,2,24,128]{4,3,2,1,0:T(8,128)(2,1)S(1)}, bf16[2,13,2,24,128]{4,3,2,1,0:T(8,128)(2,1)S(1)}) custom-call(s32[4]{0:T(128)S(1)} %pad_add_fusion.pos, bf16[4,6,56,256]{3,2,1,0:T(8,128)(2,1)S(1)} %copy-done.1, bf16[4,6,56,256]{3,2,1,0:T(8,128)(2,1)S(1)} %collective-permute-done.refs_1_.refs_5_, ...), custom_call_target="tpu_custom_call" | custom-call | flops 8254390272 | bytes 2000000 | tf_op jit(solution)/shard_map/pallas_call | solution.py:487
  95.7 7.0 %collective-permute-start.17 = (bf16[2,13,2,24,128]{4,3,2,1,0:T(8,128)(2,1)S(1)}, bf16[2,13,2,24,128]{4,3,2,1,0:T(8,128)(2,1)S(1)}, u32[]{:S(2)}, u32[]{:S(2)}) collective-permute-start(bf16[2,13,2,24,128]{4,3,2,1,0:T(8,128)(2,1)S(1)} %get-tuple-element.47), channel_id=1, source_target_pairs={{0,0},{2,8},{4,12},{6,4},{8,2},{10,10},{12,14},{14,6},{16,24},{18,... | collective-permute-start | bytes 958472 | tf_op jit(solution)/shard_map/ppermute | solution.py:369
  102.7 1.9 %collective-permute-start.18 = (bf16[2,13,2,24,128]{4,3,2,1,0:T(8,128)(2,1)S(1)}, bf16[2,13,2,24,128]{4,3,2,1,0:T(8,128)(2,1)S(1)}, u32[]{:S(2)}, u32[]{:S(2)}) collective-permute-start(bf16[2,13,2,24,128]{4,3,2,1,0:T(8,128)(2,1)S(1)} %get-tuple-element.48), channel_id=1, source_target_pairs={{0,2},{2,10},{4,14},{6,6},{8,0},{10,8},{12,12},{14,4},{16,26},{18,... | collective-permute-start | bytes 958472 | tf_op jit(solution)/shard_map/ppermute | solution.py:369
  104.7 6.1 %shard_map.102 = (bf16[2,13,2,24,128]{4,3,2,1,0:T(8,128)(2,1)S(1)}, bf16[2,13,2,24,128]{4,3,2,1,0:T(8,128)(2,1)S(1)}) custom-call(s32[4]{0:T(128)S(1)} %pad_add_fusion.pos, bf16[4,6,56,256]{3,2,1,0:T(8,128)(2,1)S(1)} %copy-done.1, bf16[4,6,56,256]{3,2,1,0:T(8,128)(2,1)S(1)} %collective-permute-done.refs_1_.refs_5_, ...), custom_call_target="tpu_custom_call" | custom-call | flops 4127195136 | bytes 2000000 | tf_op jit(solution)/shard_map/pallas_call | solution.py:487
  110.8 5.9 %shard_map.103 = (bf16[2,13,2,24,128]{4,3,2,1,0:T(8,128)(2,1)S(1)}, bf16[2,13,2,24,128]{4,3,2,1,0:T(8,128)(2,1)S(1)}) custom-call(s32[4]{0:T(128)S(1)} %pad_add_fusion.pos, bf16[4,6,56,256]{3,2,1,0:T(8,128)(2,1)S(1)} %copy-done.1, bf16[4,6,56,256]{3,2,1,0:T(8,128)(2,1)S(1)} %collective-permute-done.refs_1_.refs_5_, ...), custom_call_target="tpu_custom_call", output_to_operand_aliasing={{0}: (12, {}), {1}: (13, {})} | custom-call | flops 4127195136 | bytes 2000000 | tf_op jit(solution)/shard_map/pallas_call | solution.py:487
  116.7 1.9 %collective-permute-start.13 = (bf16[2,13,2,24,128]{4,3,2,1,0:T(8,128)(2,1)S(1)}, bf16[2,13,2,24,128]{4,3,2,1,0:T(8,128)(2,1)S(1)}, u32[]{:S(2)}, u32[]{:S(2)}) collective-permute-start(bf16[2,13,2,24,128]{4,3,2,1,0:T(8,128)(2,1)S(1)} %get-tuple-element.45), channel_id=1, source_target_pairs={{0,0},{2,8},{4,12},{6,4},{8,2},{10,10},{12,14},{14,6},{16,24},{18,... | collective-permute-start | bytes 958472 | tf_op jit(solution)/shard_map/ppermute | solution.py:369
  118.7 1.9 %collective-permute-start.14 = (bf16[2,13,2,24,128]{4,3,2,1,0:T(8,128)(2,1)S(1)}, bf16[2,13,2,24,128]{4,3,2,1,0:T(8,128)(2,1)S(1)}, u32[]{:S(2)}, u32[]{:S(2)}) collective-permute-start(bf16[2,13,2,24,128]{4,3,2,1,0:T(8,128)(2,1)S(1)} %get-tuple-element.46), channel_id=1, source_target_pairs={{0,2},{2,10},{4,14},{6,6},{8,0},{10,8},{12,12},{14,4},{16,26},{18,... | collective-permute-start | bytes 958472 | tf_op jit(solution)/shard_map/ppermute | solution.py:369
  120.7 2.3 %shard_map.105.refs_7_ = bf16[4,24,2,24,256]{4,3,2,1,0:T(8,128)(2,1)} custom-call(s32[1]{0:T(128)} %bitcast.refs_0_, bf16[2,13,2,24,128]{4,3,2,1,0:T(8,128)(2,1)S(1)} %collective-permute-done.17.refs_1_, bf16[2,13,2,24,128]{4,3,2,1,0:T(8,128)(2,1)S(1)} %collective-permute-done.18.refs_2_, bf16[1152,256]{1,0:T(8,128)(2,1)S(1)} %bitcast.24, ...), custom_call_target="tpu_custom_call" | custom-call | flops 452984832 | bytes 2000000 | tf_op jit(solution)/shard_map/pallas_call | solution.py:501
  123.0 7.6 %collective-permute-done.13.refs_1_ = bf16[2,13,2,24,128]{4,3,2,1,0:T(8,128)(2,1)S(1)} collective-permute-done((bf16[2,13,2,24,128]{4,3,2,1,0:T(8,128)(2,1)S(1)}, bf16[2,13,2,24,128]{4,3,2,1,0:T(8,128)(2,1)S(1)}, u32[]{:S(2)}, u32[]{:S(2)}) %collective-permute-start.13) | collective-permute-done | bytes 319520 | tf_op jit(solution)/shard_map/ppermute | solution.py:369
  130.5 3.4 %collective-permute-done.14.refs_2_ = bf16[2,13,2,24,128]{4,3,2,1,0:T(8,128)(2,1)S(1)} collective-permute-done((bf16[2,13,2,24,128]{4,3,2,1,0:T(8,128)(2,1)S(1)}, bf16[2,13,2,24,128]{4,3,2,1,0:T(8,128)(2,1)S(1)}, u32[]{:S(2)}, u32[]{:S(2)}) %collective-permute-start.14) | collective-permute-done | bytes 319520 | tf_op jit(solution)/shard_map/ppermute | solution.py:369
  133.9 2.2 %shard_map.106 = bf16[4,24,2,24,256]{4,3,2,1,0:T(8,128)(2,1)} custom-call(s32[1]{0:T(128)} %bitcast.refs_0_, bf16[2,13,2,24,128]{4,3,2,1,0:T(8,128)(2,1)S(1)} %collective-permute-done.13.refs_1_, bf16[2,13,2,24,128]{4,3,2,1,0:T(8,128)(2,1)S(1)} %collective-permute-done.14.refs_2_, bf16[1152,256]{1,0:T(8,128)(2,1)S(1)} %bitcast.25, ...), custom_call_target="tpu_custom_call", output_to_operand_aliasing={{}: (7, {})} | custom-call | flops 452984832 | bytes 2000000 | tf_op jit(solution)/shard_map/pallas_call | solution.py:501
  (62 shorter events, 12.6 us)
Async XLA Ops:
  5.5 23.6 %collective-permute-start = (bf16[4,6,56,256]{3,2,1,0:T(8,128)(2,1)}, bf16[4,6,56,256]{3,2,1,0:T(8,128)(2,1)S(1)}, u32[]{:S(2)}, u32[]{:S(2)}) collective-permute-start(bf16[4,6,56,256]{3,2,1,0:T(8,128)(2,1)} %get-tuple-element.28), channel_id=1, source_target_pairs={{0,2},{2,4},{4,6},{6,0},{8,10},{10,12},{12,14},{14,8},{16,18},{18,... | collective-permute-start | bytes 2064392 | tf_op jit(solution)/shard_map/ppermute | solution.py:369
  7.0 22.8 %collective-permute-start.1 = (bf16[4,6,56,256]{3,2,1,0:T(8,128)(2,1)}, bf16[4,6,56,256]{3,2,1,0:T(8,128)(2,1)S(1)}, u32[]{:S(2)}, u32[]{:S(2)}) collective-permute-start(bf16[4,6,56,256]{3,2,1,0:T(8,128)(2,1)} %get-tuple-element.29), channel_id=1, source_target_pairs={{0,4},{2,6},{4,0},{6,2},{8,12},{10,14},{12,8},{14,10},{16,20},{18,... | collective-permute-start | bytes 2064392 | tf_op jit(solution)/shard_map/ppermute | solution.py:369
  7.5 36.3 %collective-permute-start.2 = (bf16[4,6,56,256]{3,2,1,0:T(8,128)(2,1)}, bf16[4,6,56,256]{3,2,1,0:T(8,128)(2,1)S(1)}, u32[]{:S(2)}, u32[]{:S(2)}) collective-permute-start(bf16[4,6,56,256]{3,2,1,0:T(8,128)(2,1)} %get-tuple-element.30), channel_id=1, source_target_pairs={{0,6},{2,0},{4,2},{6,4},{8,14},{10,8},{12,10},{14,12},{16,22},{18,... | collective-permute-start | bytes 2064392 | tf_op jit(solution)/shard_map/ppermute | solution.py:369
  13.5 53.3 %collective-permute-start.5 = (bf16[12,80,128]{2,1,0:T(8,128)(2,1)}, bf16[12,80,128]{2,1,0:T(8,128)(2,1)S(1)}, u32[]{:S(2)}, u32[]{:S(2)}) collective-permute-start(bf16[12,80,128]{2,1,0:T(8,128)(2,1)} %get-tuple-element.33), channel_id=1, source_target_pairs={{0,0},{2,8},{4,18},{6,26},{8,6},{10,14},{12,20},{14,28},{16,2},{18... | collective-permute-start | bytes 737288 | tf_op jit(solution)/shard_map/ppermute | solution.py:369
  15.8 56.9 %collective-permute-start.6 = (bf16[12,80,128]{2,1,0:T(8,128)(2,1)}, bf16[12,80,128]{2,1,0:T(8,128)(2,1)S(1)}, u32[]{:S(2)}, u32[]{:S(2)}) collective-permute-start(bf16[12,80,128]{2,1,0:T(8,128)(2,1)} %get-tuple-element.34), channel_id=1, source_target_pairs={{0,8},{2,18},{4,26},{6,0},{8,14},{10,20},{12,28},{14,6},{16,10},{1... | collective-permute-start | bytes 737288 | tf_op jit(solution)/shard_map/ppermute | solution.py:369
  29.2 17.9 %collective-permute-start.9 = (bf16[3,80,128]{2,1,0:T(8,128)(2,1)}, bf16[3,80,128]{2,1,0:T(8,128)(2,1)S(1)}, u32[]{:S(2)}, u32[]{:S(2)}) collective-permute-start(bf16[3,80,128]{2,1,0:T(8,128)(2,1)} %copy-done.13), channel_id=1, source_target_pairs={{6,6},{14,2},{22,4},{8,8},{16,14},{24,10},{7,7},{15,3},{23,5},{9,9... | collective-permute-start | bytes 184328 | tf_op jit(solution)/shard_map/ppermute | solution.py:369
  29.8 22.0 %collective-permute-start.10 = (bf16[3,80,128]{2,1,0:T(8,128)(2,1)}, bf16[3,80,128]{2,1,0:T(8,128)(2,1)S(1)}, u32[]{:S(2)}, u32[]{:S(2)}) collective-permute-start(bf16[3,80,128]{2,1,0:T(8,128)(2,1)} %copy-done.12), channel_id=1, source_target_pairs={{6,14},{14,10},{22,12},{8,18},{16,20},{24,16},{7,15},{15,11},{23,1... | collective-permute-start | bytes 184328 | tf_op jit(solution)/shard_map/ppermute | solution.py:369
  43.8 12.8 %collective-permute-start.11 = (bf16[3,80,128]{2,1,0:T(8,128)(2,1)}, bf16[3,80,128]{2,1,0:T(8,128)(2,1)S(1)}, u32[]{:S(2)}, u32[]{:S(2)}) collective-permute-start(bf16[3,80,128]{2,1,0:T(8,128)(2,1)} %copy-done.11), channel_id=1, source_target_pairs={{6,20},{14,16},{22,22},{8,26},{16,28},{24,24},{7,21},{15,17},{23,2... | collective-permute-start | bytes 184328 | tf_op jit(solution)/shard_map/ppermute | solution.py:369
  46.2 26.1 %copy-start.3 = (bf16[3,3,336,256]{3,2,1,0:T(8,128)(2,1)S(1)}, bf16[3,3,336,256]{3,2,1,0:T(8,128)(2,1)}, u32[]{:S(2)}) copy-start(bf16[3,3,336,256]{3,2,1,0:T(8,128)(2,1)} %param.12) | copy-start | bytes 4644868
  46.2 26.1 %copy-start.5 = (bf16[3,3,256,128]{3,2,1,0:T(8,128)(2,1)S(1)}, bf16[3,3,256,128]{3,2,1,0:T(8,128)(2,1)}, u32[]{:S(2)}) copy-start(bf16[3,3,256,128]{3,2,1,0:T(8,128)(2,1)} %param.14) | copy-start | bytes 1769476
  47.0 25.7 %copy-start.15 = (f32[128]{0:T(128)S(1)}, f32[128]{0:T(128)}, u32[]{:S(2)}) copy-start(f32[128]{0:T(128)} %param.15) | copy-start | bytes 1540
  47.0 25.7 %collective-permute-start.7 = (bf16[12,80,128]{2,1,0:T(8,128)(2,1)S(1)}, bf16[12,80,128]{2,1,0:T(8,128)(2,1)S(1)}, u32[]{:S(2)}, u32[]{:S(2)}) collective-permute-start(bf16[12,80,128]{2,1,0:T(8,128)(2,1)S(1)} %get-tuple-element.35), channel_id=1, source_target_pairs={{0,18},{2,26},{4,0},{6,8},{8,20},{10,28},{12,6},{14,14},{16,16},{1... | collective-permute-start | bytes 737288 | tf_op jit(solution)/shard_map/ppermute | solution.py:369
  51.8 20.9 %collective-permute-start.8 = (bf16[12,80,128]{2,1,0:T(8,128)(2,1)S(1)}, bf16[12,80,128]{2,1,0:T(8,128)(2,1)S(1)}, u32[]{:S(2)}, u32[]{:S(2)}) collective-permute-start(bf16[12,80,128]{2,1,0:T(8,128)(2,1)S(1)} %get-tuple-element.36), channel_id=1, source_target_pairs={{0,26},{2,0},{4,8},{6,18},{8,28},{10,6},{12,14},{14,20},{16,24},{1... | collective-permute-start | bytes 737288 | tf_op jit(solution)/shard_map/ppermute | solution.py:369
  56.6 8.9 %collective-permute-start.12 = (bf16[3,80,128]{2,1,0:T(8,128)(2,1)S(1)}, bf16[3,80,128]{2,1,0:T(8,128)(2,1)S(1)}, u32[]{:S(2)}, u32[]{:S(2)}) collective-permute-start(bf16[3,80,128]{2,1,0:T(8,128)(2,1)S(1)} %copy-done.10), channel_id=1, source_target_pairs={{6,28},{14,24},{22,30},{8,0},{16,6},{24,2},{7,29},{15,25},{23,31},... | collective-permute-start | bytes 184328 | tf_op jit(solution)/shard_map/ppermute | solution.py:369
  65.5 18.9 %collective-permute-start.15 = (bf16[2,3,56,256]{3,2,1,0:T(8,128)(2,1)S(1)}, bf16[2,3,56,256]{3,2,1,0:T(8,128)(2,1)S(1)}, u32[]{:S(2)}, u32[]{:S(2)}) collective-permute-start(bf16[2,3,56,256]{3,2,1,0:T(8,128)(2,1)S(1)} %get-tuple-element.49), channel_id=1, source_target_pairs={{0,8},{6,14},{2,10},{4,12},{8,18},{14,20},{10,16},{12,22},{18,26},... | collective-permute-start | bytes 516104 | tf_op jit(solution)/shard_map/ppermute | solution.py:369
  66.8 17.6 %collective-permute-start.16 = (bf16[2,2,56,256]{3,2,1,0:T(8,128)(2,1)S(1)}, bf16[2,2,56,256]{3,2,1,0:T(8,128)(2,1)S(1)}, u32[]{:S(2)}, u32[]{:S(2)}) collective-permute-start(bf16[2,2,56,256]{3,2,1,0:T(8,128)(2,1)S(1)} %get-tuple-element.51), channel_id=1, source_target_pairs={{8,0},{14,6},{10,2},{12,4},{18,8},{20,14},{16,10},{22,12},{26,18},... | collective-permute-start | bytes 344072 | tf_op jit(solution)/shard_map/ppermute | solution.py:369
  72.7 11.7 %copy-start.1 = (bf16[4,6,56,256]{3,2,1,0:T(8,128)(2,1)S(1)}, bf16[4,6,56,256]{3,2,1,0:T(8,128)(2,1)}, u32[]{:S(2)}) copy-start(bf16[4,6,56,256]{3,2,1,0:T(8,128)(2,1)} %get-tuple-element.27.refs_0_.refs_4_) | copy-start | bytes 2064388
  72.7 11.7 %copy-start.14 = (f32[256]{0:T(256)S(1)}, f32[256]{0:T(256)}, u32[]{:S(2)}) copy-start(f32[256]{0:T(256)} %param.13) | copy-start | bytes 3076
  77.6 27.1 %collective-permute-start.3 = (bf16[2,3,56,256]{3,2,1,0:T(8,128)(2,1)S(1)}, bf16[2,3,56,256]{3,2,1,0:T(8,128)(2,1)S(1)}, u32[]{:S(2)}, u32[]{:S(2)}) collective-permute-start(bf16[2,3,56,256]{3,2,1,0:T(8,128)(2,1)S(1)} %get-tuple-element.50), channel_id=1, source_target_pairs={{0,8},{6,14},{2,10},{4,12},{8,18},{14,20},{10,16},{12,22},{18,26},... | collective-permute-start | bytes 516104 | tf_op jit(solution)/shard_map/ppermute | solution.py:369
  78.9 25.8 %collective-permute-start.4 = (bf16[2,2,56,256]{3,2,1,0:T(8,128)(2,1)S(1)}, bf16[2,2,56,256]{3,2,1,0:T(8,128)(2,1)S(1)}, u32[]{:S(2)}, u32[]{:S(2)}) collective-permute-start(bf16[2,2,56,256]{3,2,1,0:T(8,128)(2,1)S(1)} %get-tuple-element.52), channel_id=1, source_target_pairs={{8,0},{14,6},{10,2},{12,4},{18,8},{20,14},{16,10},{22,12},{26,18},... | collective-permute-start | bytes 344072 | tf_op jit(solution)/shard_map/ppermute | solution.py:369
  95.7 24.9 %collective-permute-start.17 = (bf16[2,13,2,24,128]{4,3,2,1,0:T(8,128)(2,1)S(1)}, bf16[2,13,2,24,128]{4,3,2,1,0:T(8,128)(2,1)S(1)}, u32[]{:S(2)}, u32[]{:S(2)}) collective-permute-start(bf16[2,13,2,24,128]{4,3,2,1,0:T(8,128)(2,1)S(1)} %get-tuple-element.47), channel_id=1, source_target_pairs={{0,0},{2,8},{4,12},{6,4},{8,2},{10,10},{12,14},{14,6},{16,24},{18,... | collective-permute-start | bytes 958472 | tf_op jit(solution)/shard_map/ppermute | solution.py:369
  102.7 17.9 %collective-permute-start.18 = (bf16[2,13,2,24,128]{4,3,2,1,0:T(8,128)(2,1)S(1)}, bf16[2,13,2,24,128]{4,3,2,1,0:T(8,128)(2,1)S(1)}, u32[]{:S(2)}, u32[]{:S(2)}) collective-permute-start(bf16[2,13,2,24,128]{4,3,2,1,0:T(8,128)(2,1)S(1)} %get-tuple-element.48), channel_id=1, source_target_pairs={{0,2},{2,10},{4,14},{6,6},{8,0},{10,8},{12,12},{14,4},{16,26},{18,... | collective-permute-start | bytes 958472 | tf_op jit(solution)/shard_map/ppermute | solution.py:369
  116.7 13.8 %collective-permute-start.13 = (bf16[2,13,2,24,128]{4,3,2,1,0:T(8,128)(2,1)S(1)}, bf16[2,13,2,24,128]{4,3,2,1,0:T(8,128)(2,1)S(1)}, u32[]{:S(2)}, u32[]{:S(2)}) collective-permute-start(bf16[2,13,2,24,128]{4,3,2,1,0:T(8,128)(2,1)S(1)} %get-tuple-element.45), channel_id=1, source_target_pairs={{0,0},{2,8},{4,12},{6,4},{8,2},{10,10},{12,14},{14,6},{16,24},{18,... | collective-permute-start | bytes 958472 | tf_op jit(solution)/shard_map/ppermute | solution.py:369
  118.7 15.2 %collective-permute-start.14 = (bf16[2,13,2,24,128]{4,3,2,1,0:T(8,128)(2,1)S(1)}, bf16[2,13,2,24,128]{4,3,2,1,0:T(8,128)(2,1)S(1)}, u32[]{:S(2)}, u32[]{:S(2)}) collective-permute-start(bf16[2,13,2,24,128]{4,3,2,1,0:T(8,128)(2,1)S(1)} %get-tuple-element.46), channel_id=1, source_target_pairs={{0,2},{2,10},{4,14},{6,6},{8,0},{10,8},{12,12},{14,4},{16,26},{18,... | collective-permute-start | bytes 958472 | tf_op jit(solution)/shard_map/ppermute | solution.py:369
  (11 other events, 62.3 us)

commit v7 on v6

--- a/solution.py
+++ b/solution.py
@@ -187,7 +187,7 @@
     ]
 
 
-def conv_kernel(pos, *refs, parts, sh, tr, pitch, rows, cols, at, cam_at, out_at, many):
+def conv_kernel(pos, *refs, parts, sh, tr, pitch, rows, cols, at, cam_at, rim_at, many):
     windows = refs[:parts]
     above, below, camera, w1, b1, w2, b2 = refs[parts : parts + 7]
     outs = refs[-5 - HALVES : -5]
@@ -206,11 +206,11 @@
     inside[...] = jnp.where((col >= 0) & (col < cols), 1.0, 0.0)
 
     def frame(f, _):
-        tile[0:UP, 0:wide, :] = above[out_at + f]
+        tile[0:UP, 0:wide, :] = above[rim_at + f]
         for d in range(parts):
             source = lax.rem(member - d + parts, parts)
             tile[pl.ds(UP + source * sh, sh), 0:wide, :] = windows[d][at + f]
-        tile[UP + tr : UP + tr + DOWN, 0:wide, :] = below[out_at + f]
+        tile[UP + tr : UP + tr + DOWN, 0:wide, :] = below[rim_at + f]
 
         step = 6
         flat = step * pitch
@@ -277,10 +277,10 @@
 
                 @pl.when(lax.rem(half_id + h, HALVES) == sub)
                 def _():
-                    outs[h][out_at + f, 0:pairs, 0] = even
-                    outs[h][out_at + f, 0:pairs, 1] = odd
-                    outs[h][out_at + f, pairs, 0] = edge
-                    outs[h][out_at + f, pairs, 1] = beside
+                    outs[h][f, 0:pairs, 0] = even
+                    outs[h][f, 0:pairs, 1] = odd
+                    outs[h][f, pairs, 0] = edge
+                    outs[h][f, pairs, 1] = beside
         return 0
 
     if many == 1:
@@ -458,7 +458,7 @@
                     out_specs=[framed(window)] * members,
                 ),
                 out_shape=[window] * members,
-                compiler_params=limit(60),
+                compiler_params=limit(6),
             )(jnp.stack([column_of((member + d) % members) for d in range(members)]).astype(jnp.int32), source)
             windows = [windows[0]] + [
                 send(windows[d], [(g * members + m, g * members + (m + d) % members) for g in range(groups) for m in range(members)])
@@ -478,22 +478,19 @@
                     shift.append((s, r * n_cols + HALVES * tile_of[r % 2][m] + (k + h) % HALVES))
                 shifts.append(shift)
             vmem = pl.BlockSpec(memory_space=pltpu.VMEM)
-            for b0 in range(0, step, batch):
-                blocks = jax.ShapeDtypeStruct((batch, pairs2, 2, w, block), BF)
+            batches = [(0, batch)] + [(f, 1) for f in range(batch, step)]
+            for b0, many in batches:
+                blocks = jax.ShapeDtypeStruct((many, pairs2, 2, w, block), BF)
                 above, below = rims[b0 // batch]
-                runs = [(0, batch)] if b0 == 0 else [(f, 1) for f in range(batch)]
-                tiles = []
-                for f1, many in runs:
-                    tiles = pl.pallas_call(
-                        functools.partial(conv_kernel, parts=members, sh=sh, tr=tr, pitch=pitch, rows=rows, cols=cols, at=b0 + f1, cam_at=f0 + b0 + f1, out_at=f1, many=many),
-                        in_specs=[pl.BlockSpec(memory_space=pltpu.SMEM)] + [vmem] * (members + 7 + len(tiles)),
-                        out_specs=[vmem] * HALVES,
-                        scratch_shapes=conv_scratch(tr, pitch, lidar_ch, joined, block, pairs2),
-                        out_shape=[blocks] * HALVES,
-                        input_output_aliases={members + 8 + h: h for h in range(HALVES)} if tiles else {},
-                        compiler_params=limit(20),
-                        cost_estimate=pl.CostEstimate(flops=flops * many, bytes_accessed=2 * 10**6, transcendentals=0),
-                    )(pos, *windows, above, below, cam, w1, b1, w2, b2, *tiles)
+                tiles = pl.pallas_call(
+                    functools.partial(conv_kernel, parts=members, sh=sh, tr=tr, pitch=pitch, rows=rows, cols=cols, at=b0, cam_at=f0 + b0, rim_at=b0 % batch, many=many),
+                    in_specs=[pl.BlockSpec(memory_space=pltpu.SMEM)] + [vmem] * (members + 7),
+                    out_specs=[vmem] * HALVES,
+                    scratch_shapes=conv_scratch(tr, pitch, lidar_ch, joined, block, pairs2),
+                    out_shape=[blocks] * HALVES,
+                    compiler_params=limit(20),
+                    cost_estimate=pl.CostEstimate(flops=flops * many, bytes_accessed=2 * 10**6, transcendentals=0),
+                )(pos, *windows, above, below, cam, w1, b1, w2, b2)
                 pieces = []
                 for h in range(HALVES):
                     pieces.append(send(tiles[h], shifts[h]))
@@ -502,7 +499,7 @@
                     lambda *refs: encode_kernel(*refs, parts=HALVES, half_rows=half_rows, w=w),
                     grid_spec=pltpu.PrefetchScalarGridSpec(
                         num_scalar_prefetch=1,
-                        grid=(batch,),
+                        grid=(many,),
                         in_specs=[framed(x) for x in pieces] + [whole(x) for x in (w3, b3, proj_weight, bp)] + [pl.BlockSpec(memory_space=pl.ANY)] * len(old),
                         out_specs=pl.BlockSpec((1, n, 2, w, 2 * block), lambda f, p, lo=f0 + b0: (f + lo, 0, 0, 0, 0)),
                         scratch_shapes=[
@@ -513,7 +510,7 @@
                     out_shape=jax.ShapeDtypeStruct((frames, n, 2, w, 2 * block), BF),
                     input_output_aliases={5 + HALVES: 0} if old else {},
                     compiler_params=limit(12),
-                    cost_estimate=pl.CostEstimate(flops=2 * batch * n * jd * w3.shape[0] * 256, bytes_accessed=batch * 10**6, transcendentals=0),
+                    cost_estimate=pl.CostEstimate(flops=2 * many * n * jd * w3.shape[0] * 256, bytes_accessed=many * 10**6, transcendentals=0),
                 )(cindex.reshape(1).astype(jnp.int32), *pieces, w3, b3, proj_weight, bp, *old)
         return encoded.reshape(frames, 2 * n, w, 2 * block)
 

time: 137 us -> 138 us (level)
  the two profiles are of different devices: /device:TPU:26 before, /device:TPU:8 now
where the time goes in v7:
time: 138 us
  starting transfers between devices  66.7 us (48%)
  Pallas kernels  39.4 us (29%)
  waiting for transfers between devices  26.6 us (19%)
  local copies, waits for them, and re-layouts  4.3 us (3%)
    ppermute x21, starting transfers between devices, send(): return lax.ppermute(x, AXES, pairs)  66.7 us
    ppermute x21, waiting for transfers between devices, send(): return lax.ppermute(x, AXES, pairs)  26.6 us
    pallas_call x3, Pallas kernels, local(): pl.pallas_call(functools.partial(conv_kernel, parts=members, sh=sh, tr=tr...  23.2 us
    pallas_call x3, Pallas kernels, local(): pl.pallas_call(lambda *refs: encode_kernel(*refs, parts=HALVES, half_rows...  5.38 us
    pallas_call x1, Pallas kernels, local(): pl.pallas_call(lambda *refs: camera_unpack_kernel(*refs, groups=groups, s...  4.82 us
    unnamed x30, local copies, waits for them, and re-layouts  4.26 us
  transfers between devices with their start and end apart: 21, of which 3 were waited for; matrix products, arithmetic and copies ran while one was open for 0% of the time, Pallas kernels for 25%

profile of v7, /device:TPU:8, one launch (start us, length us, event | category | flops | bytes accessed | tf_op | source)
XLA Modules:
  0.0 137.7 jit_solution(5781527431673385948)
XLA Ops:
  0.1 1.7 %copy-done.1 = bf16[4,6,192,256]{3,2,1,0:T(8,128)(2,1)S(1)} copy-done((bf16[4,6,192,256]{3,2,1,0:T(8,128)(2,1)S(1)}, bf16[4,6,192,256]{3,2,1,0:T(8,128)(2,1)}, u32[]{:S(2)}) %copy-start.1) | copy-done | bytes 2359320
  1.7 2.8 %shard_map.100 = (bf16[4,6,56,256]{3,2,1,0:T(8,128)(2,1)S(1)}, bf16[4,6,56,256]{3,2,1,0:T(8,128)(2,1)}, bf16[4,6,56,256]{3,2,1,0:T(8,128)(2,1)}, bf16[4,6,56,256]{3,2,1,0:T(8,128)(2,1)}) custom-call(s32[4]{0:T(128)S(1)} %pad_add_fusion.1.pos, bf16[4,6,192,256]{3,2,1,0:T(8,128)(2,1)S(1)} %copy-done.1), custom_call_target="tpu_custom_call" | custom-call | tf_op jit(solution)/shard_map/pallas_call | solution.py:452
  7.5 2.2 %camera_pack.1 = (bf16[12,80,128]{2,1,0:T(8,128)(2,1)}, bf16[12,80,128]{2,1,0:T(8,128)(2,1)}, bf16[12,80,128]{2,1,0:T(8,128)(2,1)S(1)}, bf16[12,80,128]{2,1,0:T(...) custom-call(s32[1]{0:T(128)} %bitcast.10.refs_0_, ...), custom_call_target="tpu_custom_call" | custom-call | tf_op jit(solution)/shard_map/camera_pack/pallas_call | solution.py:405
  12.2 4.8 %collective-permute-start.5 = (bf16[12,80,128]{2,1,0:T(8,128)(2,1)}, bf16[12,80,128]{2,1,0:T(8,128)(2,1)S(1)}, u32[]{:S(2)}, u32[]{:S(2)}) collective-permute-start(bf16[12,80,128]{2,1,0:T(8,128)(2,1)} %get-tuple-element.33), channel_id=1, source_target_pairs={{0,0},{2,8},{4,18},{6,26},{8,6},{10,14},{12,20},{14,28},{16,2},{18... | collective-permute-start | bytes 737288 | tf_op jit(solution)/shard_map/ppermute | solution.py:369
  17.0 2.5 %collective-permute-start.6 = (bf16[12,80,128]{2,1,0:T(8,128)(2,1)}, bf16[12,80,128]{2,1,0:T(8,128)(2,1)S(1)}, u32[]{:S(2)}, u32[]{:S(2)}) collective-permute-start(bf16[12,80,128]{2,1,0:T(8,128)(2,1)} %get-tuple-element.34), channel_id=1, source_target_pairs={{0,8},{2,18},{4,26},{6,0},{8,14},{10,20},{12,28},{14,6},{16,10},{1... | collective-permute-start | bytes 737288 | tf_op jit(solution)/shard_map/ppermute | solution.py:369
  19.6 21.5 %collective-permute-done.refs_1_.refs_5_ = bf16[4,6,56,256]{3,2,1,0:T(8,128)(2,1)S(1)} collective-permute-done((bf16[4,6,56,256]{3,2,1,0:T(8,128)(2,1)}, bf16[4,6,56,256]{3,2,1,0:T(8,128)(2,1)S(1)}, u32[]{:S(2)}, u32[]{:S(2)}) %collective-permute-start) | collective-permute-done | bytes 688160 | tf_op jit(solution)/shard_map/ppermute | solution.py:369
  44.6 4.0 %collective-permute-done.9.refs_5_ = bf16[3,80,128]{2,1,0:T(8,128)(2,1)S(1)} collective-permute-done((bf16[3,80,128]{2,1,0:T(8,128)(2,1)}, bf16[3,80,128]{2,1,0:T(8,128)(2,1)S(1)}, u32[]{:S(2)}, u32[]{:S(2)}) %collective-permute-start.9) | collective-permute-done | bytes 61472 | tf_op jit(solution)/shard_map/ppermute | solution.py:369
  48.6 1.9 %collective-permute-start.7 = (bf16[12,80,128]{2,1,0:T(8,128)(2,1)S(1)}, bf16[12,80,128]{2,1,0:T(8,128)(2,1)S(1)}, u32[]{:S(2)}, u32[]{:S(2)}) collective-permute-start(bf16[12,80,128]{2,1,0:T(8,128)(2,1)S(1)} %copy-done.9), channel_id=1, source_target_pairs={{0,18},{2,26},{4,0},{6,8},{8,20},{10,28},{12,6},{14,14},{16,16},{1... | collective-permute-start | bytes 737288 | tf_op jit(solution)/shard_map/ppermute | solution.py:369
  50.5 1.7 %collective-permute-start.8 = (bf16[12,80,128]{2,1,0:T(8,128)(2,1)S(1)}, bf16[12,80,128]{2,1,0:T(8,128)(2,1)S(1)}, u32[]{:S(2)}, u32[]{:S(2)}) collective-permute-start(bf16[12,80,128]{2,1,0:T(8,128)(2,1)S(1)} %get-tuple-element.36), channel_id=1, source_target_pairs={{0,26},{2,0},{4,8},{6,18},{8,28},{10,6},{12,14},{14,20},{16,24},{1... | collective-permute-start | bytes 737288 | tf_op jit(solution)/shard_map/ppermute | solution.py:369
  52.8 8.1 %collective-permute-start.3 = (bf16[2,3,56,256]{3,2,1,0:T(8,128)(2,1)S(1)}, bf16[2,3,56,256]{3,2,1,0:T(8,128)(2,1)S(1)}, u32[]{:S(2)}, u32[]{:S(2)}) collective-permute-start(bf16[2,3,56,256]{3,2,1,0:T(8,128)(2,1)S(1)} %get-tuple-element.50), channel_id=1, source_target_pairs={{0,8},{6,14},{2,10},{4,12},{8,18},{14,20},{10,16},{12,22},{18,26},... | collective-permute-start | bytes 516104 | tf_op jit(solution)/shard_map/ppermute | solution.py:369
  63.9 4.8 %camera_unpack.1 = bf16[128,64,256]{2,1,0:T(8,128)(2,1)S(1)} custom-call(s32[1]{0:T(128)} %bitcast.1.refs_0_, bf16[12,80,128]{2,1,0:T(8,128)(2,1)S(1)} %collective-permute-done.5.refs_1_, bf16[12,80,128]{2,1,0:T(8,128)(2,1)S(1)} %collective-permute-done.6.refs_2_, bf16[12,80,128]{2,1,0:T(8,128)(2,1)S(1)} %collective-permute-done.7.refs_3_, ...), custom_call_target="tpu_custom_call" | custom-call | tf_op jit(solution)/shard_map/camera_unpack/pallas_call | solution.py:422
  68.8 10.9 %collective-permute-start.17 = (bf16[2,3,56,256]{3,2,1,0:T(8,128)(2,1)S(1)}, bf16[2,3,56,256]{3,2,1,0:T(8,128)(2,1)S(1)}, u32[]{:S(2)}, u32[]{:S(2)}) collective-permute-start(bf16[2,3,56,256]{3,2,1,0:T(8,128)(2,1)S(1)} %get-tuple-element.49), channel_id=1, source_target_pairs={{0,8},{6,14},{2,10},{4,12},{8,18},{14,20},{10,16},{12,22},{18,26},... | collective-permute-start | bytes 516104 | tf_op jit(solution)/shard_map/ppermute | solution.py:369
  81.0 5.9 %shard_map.103 = (bf16[1,13,2,24,128]{4,3,2,1,0:T(8,128)(2,1)S(1)}, bf16[1,13,2,24,128]{4,3,2,1,0:T(8,128)(2,1)S(1)}) custom-call(s32[4]{0:T(128)S(1)} %pad_add_fusion.pos, bf16[4,6,56,256]{3,2,1,0:T(8,128)(2,1)S(1)} %get-tuple-element.27.refs_0_.refs_4_, bf16[4,6,56,256]{3,2,1,0:T(8,128)(2,1)S(1)} %collective-permute-done.refs_1_.refs_5_, ...), custom_call_target="tpu_custom_call" | custom-call | flops 4127195136 | bytes 2000000 | tf_op jit(solution)/shard_map/pallas_call | solution.py:485
  87.0 7.2 %collective-permute-start.15 = (bf16[1,13,2,24,128]{4,3,2,1,0:T(8,128)(2,1)S(1)}, bf16[1,13,2,24,128]{4,3,2,1,0:T(8,128)(2,1)S(1)}, u32[]{:S(2)}, u32[]{:S(2)}) collective-permute-start(bf16[1,13,2,24,128]{4,3,2,1,0:T(8,128)(2,1)S(1)} %get-tuple-element.45), channel_id=1, source_target_pairs={{0,0},{2,8},{4,12},{6,4},{8,2},{10,10},{12,14},{14,6},{16,24},{18,... | collective-permute-start | bytes 479240 | tf_op jit(solution)/shard_map/ppermute | solution.py:369
  94.2 1.9 %collective-permute-start.16 = (bf16[1,13,2,24,128]{4,3,2,1,0:T(8,128)(2,1)S(1)}, bf16[1,13,2,24,128]{4,3,2,1,0:T(8,128)(2,1)S(1)}, u32[]{:S(2)}, u32[]{:S(2)}) collective-permute-start(bf16[1,13,2,24,128]{4,3,2,1,0:T(8,128)(2,1)S(1)} %get-tuple-element.46), channel_id=1, source_target_pairs={{0,2},{2,10},{4,14},{6,6},{8,0},{10,8},{12,12},{14,4},{16,26},{18,... | collective-permute-start | bytes 479240 | tf_op jit(solution)/shard_map/ppermute | solution.py:369
  96.1 11.3 %shard_map.104 = (bf16[2,13,2,24,128]{4,3,2,1,0:T(8,128)(2,1)S(1)}, bf16[2,13,2,24,128]{4,3,2,1,0:T(8,128)(2,1)S(1)}) custom-call(s32[4]{0:T(128)S(1)} %pad_add_fusion.pos, bf16[4,6,56,256]{3,2,1,0:T(8,128)(2,1)S(1)} %get-tuple-element.27.refs_0_.refs_4_, bf16[4,6,56,256]{3,2,1,0:T(8,128)(2,1)S(1)} %collective-permute-done.refs_1_.refs_5_, ...), custom_call_target="tpu_custom_call" | custom-call | flops 8254390272 | bytes 2000000 | tf_op jit(solution)/shard_map/pallas_call | solution.py:485
  107.5 1.9 %collective-permute-start.19 = (bf16[2,13,2,24,128]{4,3,2,1,0:T(8,128)(2,1)S(1)}, bf16[2,13,2,24,128]{4,3,2,1,0:T(8,128)(2,1)S(1)}, u32[]{:S(2)}, u32[]{:S(2)}) collective-permute-start(bf16[2,13,2,24,128]{4,3,2,1,0:T(8,128)(2,1)S(1)} %get-tuple-element.47), channel_id=1, source_target_pairs={{0,0},{2,8},{4,12},{6,4},{8,2},{10,10},{12,14},{14,6},{16,24},{18,... | collective-permute-start | bytes 958472 | tf_op jit(solution)/shard_map/ppermute | solution.py:369
  109.4 6.0 %collective-permute-start.20 = (bf16[2,13,2,24,128]{4,3,2,1,0:T(8,128)(2,1)S(1)}, bf16[2,13,2,24,128]{4,3,2,1,0:T(8,128)(2,1)S(1)}, u32[]{:S(2)}, u32[]{:S(2)}) collective-permute-start(bf16[2,13,2,24,128]{4,3,2,1,0:T(8,128)(2,1)S(1)} %get-tuple-element.48), channel_id=1, source_target_pairs={{0,2},{2,10},{4,14},{6,6},{8,0},{10,8},{12,12},{14,4},{16,26},{18,... | collective-permute-start | bytes 958472 | tf_op jit(solution)/shard_map/ppermute | solution.py:369
  115.5 5.9 %shard_map.102 = (bf16[1,13,2,24,128]{4,3,2,1,0:T(8,128)(2,1)S(1)}, bf16[1,13,2,24,128]{4,3,2,1,0:T(8,128)(2,1)S(1)}) custom-call(s32[4]{0:T(128)S(1)} %pad_add_fusion.pos, bf16[4,6,56,256]{3,2,1,0:T(8,128)(2,1)S(1)} %get-tuple-element.27.refs_0_.refs_4_, bf16[4,6,56,256]{3,2,1,0:T(8,128)(2,1)S(1)} %collective-permute-done.refs_1_.refs_5_, ...), custom_call_target="tpu_custom_call" | custom-call | flops 4127195136 | bytes 2000000 | tf_op jit(solution)/shard_map/pallas_call | solution.py:485
  121.4 1.9 %collective-permute-start.13 = (bf16[1,13,2,24,128]{4,3,2,1,0:T(8,128)(2,1)S(1)}, bf16[1,13,2,24,128]{4,3,2,1,0:T(8,128)(2,1)S(1)}, u32[]{:S(2)}, u32[]{:S(2)}) collective-permute-start(bf16[1,13,2,24,128]{4,3,2,1,0:T(8,128)(2,1)S(1)} %get-tuple-element.43), channel_id=1, source_target_pairs={{0,0},{2,8},{4,12},{6,4},{8,2},{10,10},{12,14},{14,6},{16,24},{18,... | collective-permute-start | bytes 479240 | tf_op jit(solution)/shard_map/ppermute | solution.py:369
  123.3 8.9 %collective-permute-start.14 = (bf16[1,13,2,24,128]{4,3,2,1,0:T(8,128)(2,1)S(1)}, bf16[1,13,2,24,128]{4,3,2,1,0:T(8,128)(2,1)S(1)}, u32[]{:S(2)}, u32[]{:S(2)}) collective-permute-start(bf16[1,13,2,24,128]{4,3,2,1,0:T(8,128)(2,1)S(1)} %get-tuple-element.44), channel_id=1, source_target_pairs={{0,2},{2,10},{4,14},{6,6},{8,0},{10,8},{12,12},{14,4},{16,26},{18,... | collective-permute-start | bytes 479240 | tf_op jit(solution)/shard_map/ppermute | solution.py:369
  132.3 2.3 %shard_map.105.refs_7_ = bf16[4,24,2,24,256]{4,3,2,1,0:T(8,128)(2,1)} custom-call(s32[1]{0:T(128)} %bitcast.refs_0_, bf16[2,13,2,24,128]{4,3,2,1,0:T(8,128)(2,1)S(1)} %collective-permute-done.19.refs_1_, bf16[2,13,2,24,128]{4,3,2,1,0:T(8,128)(2,1)S(1)} %collective-permute-done.20.refs_2_, bf16[1152,256]{1,0:T(8,128)(2,1)S(1)} %bitcast.21, ...), custom_call_target="tpu_custom_call" | custom-call | flops 452984832 | bytes 2000000 | tf_op jit(solution)/shard_map/pallas_call | solution.py:498
  134.6 1.5 %shard_map.106.refs_7_ = bf16[4,24,2,24,256]{4,3,2,1,0:T(8,128)(2,1)} custom-call(s32[1]{0:T(128)} %bitcast.refs_0_, bf16[1,13,2,24,128]{4,3,2,1,0:T(8,128)(2,1)S(1)} %collective-permute-done.15.refs_1_, bf16[1,13,2,24,128]{4,3,2,1,0:T(8,128)(2,1)S(1)} %collective-permute-done.16.refs_2_, ...), custom_call_target="tpu_custom_call", output_to_operand_aliasing={{}: (7, {})} | custom-call | flops 226492416 | bytes 1000000 | tf_op jit(solution)/shard_map/pallas_call | solution.py:498
  136.2 1.5 %shard_map.107 = bf16[4,24,2,24,256]{4,3,2,1,0:T(8,128)(2,1)} custom-call(s32[1]{0:T(128)} %bitcast.refs_0_, bf16[1,13,2,24,128]{4,3,2,1,0:T(8,128)(2,1)S(1)} %collective-permute-done.13.refs_1_, bf16[1,13,2,24,128]{4,3,2,1,0:T(8,128)(2,1)S(1)} %collective-permute-done.14.refs_2_, bf16[1152,256]{1,0:T(8,128)(2,1)S(1)} %bitcast.23, ...), custom_call_target="tpu_custom_call", output_to_operand_aliasing={{}: (7, {})} | custom-call | flops 226492416 | bytes 1000000 | tf_op jit(solution)/shard_map/pallas_call | solution.py:498
  (65 shorter events, 14.0 us)
Async XLA Ops:
  4.5 36.6 %collective-permute-start = (bf16[4,6,56,256]{3,2,1,0:T(8,128)(2,1)}, bf16[4,6,56,256]{3,2,1,0:T(8,128)(2,1)S(1)}, u32[]{:S(2)}, u32[]{:S(2)}) collective-permute-start(bf16[4,6,56,256]{3,2,1,0:T(8,128)(2,1)} %get-tuple-element.28), channel_id=1, source_target_pairs={{0,2},{2,4},{4,6},{6,0},{8,10},{10,12},{12,14},{14,8},{16,18},{18,... | collective-permute-start | bytes 2064392 | tf_op jit(solution)/shard_map/ppermute | solution.py:369
  6.0 36.3 %collective-permute-start.1 = (bf16[4,6,56,256]{3,2,1,0:T(8,128)(2,1)}, bf16[4,6,56,256]{3,2,1,0:T(8,128)(2,1)S(1)}, u32[]{:S(2)}, u32[]{:S(2)}) collective-permute-start(bf16[4,6,56,256]{3,2,1,0:T(8,128)(2,1)} %get-tuple-element.29), channel_id=1, source_target_pairs={{0,4},{2,6},{4,0},{6,2},{8,12},{10,14},{12,8},{14,10},{16,20},{18,... | collective-permute-start | bytes 2064392 | tf_op jit(solution)/shard_map/ppermute | solution.py:369
  6.5 36.6 %collective-permute-start.2 = (bf16[4,6,56,256]{3,2,1,0:T(8,128)(2,1)}, bf16[4,6,56,256]{3,2,1,0:T(8,128)(2,1)S(1)}, u32[]{:S(2)}, u32[]{:S(2)}) collective-permute-start(bf16[4,6,56,256]{3,2,1,0:T(8,128)(2,1)} %get-tuple-element.30), channel_id=1, source_target_pairs={{0,6},{2,0},{4,2},{6,4},{8,14},{10,8},{12,10},{14,12},{16,22},{18,... | collective-permute-start | bytes 2064392 | tf_op jit(solution)/shard_map/ppermute | solution.py:369
  12.2 48.8 %collective-permute-start.5 = (bf16[12,80,128]{2,1,0:T(8,128)(2,1)}, bf16[12,80,128]{2,1,0:T(8,128)(2,1)S(1)}, u32[]{:S(2)}, u32[]{:S(2)}) collective-permute-start(bf16[12,80,128]{2,1,0:T(8,128)(2,1)} %get-tuple-element.33), channel_id=1, source_target_pairs={{0,0},{2,8},{4,18},{6,26},{8,6},{10,14},{12,20},{14,28},{16,2},{18... | collective-permute-start | bytes 737288 | tf_op jit(solution)/shard_map/ppermute | solution.py:369
  17.0 45.7 %collective-permute-start.6 = (bf16[12,80,128]{2,1,0:T(8,128)(2,1)}, bf16[12,80,128]{2,1,0:T(8,128)(2,1)S(1)}, u32[]{:S(2)}, u32[]{:S(2)}) collective-permute-start(bf16[12,80,128]{2,1,0:T(8,128)(2,1)} %get-tuple-element.34), channel_id=1, source_target_pairs={{0,8},{2,18},{4,26},{6,0},{8,14},{10,20},{12,28},{14,6},{16,10},{1... | collective-permute-start | bytes 737288 | tf_op jit(solution)/shard_map/ppermute | solution.py:369
  41.1 7.5 %collective-permute-start.9 = (bf16[3,80,128]{2,1,0:T(8,128)(2,1)}, bf16[3,80,128]{2,1,0:T(8,128)(2,1)S(1)}, u32[]{:S(2)}, u32[]{:S(2)}) collective-permute-start(bf16[3,80,128]{2,1,0:T(8,128)(2,1)} %copy-done.12), channel_id=1, source_target_pairs={{6,6},{14,2},{22,4},{8,8},{16,14},{24,10},{7,7},{15,3},{23,5},{9,9... | collective-permute-start | bytes 184328 | tf_op jit(solution)/shard_map/ppermute | solution.py:369
  42.4 8.1 %collective-permute-start.10 = (bf16[3,80,128]{2,1,0:T(8,128)(2,1)}, bf16[3,80,128]{2,1,0:T(8,128)(2,1)S(1)}, u32[]{:S(2)}, u32[]{:S(2)}) collective-permute-start(bf16[3,80,128]{2,1,0:T(8,128)(2,1)} %copy-done.11), channel_id=1, source_target_pairs={{6,14},{14,10},{22,12},{8,18},{16,20},{24,16},{7,15},{15,11},{23,1... | collective-permute-start | bytes 184328 | tf_op jit(solution)/shard_map/ppermute | solution.py:369
  43.0 9.1 %collective-permute-start.11 = (bf16[3,80,128]{2,1,0:T(8,128)(2,1)}, bf16[3,80,128]{2,1,0:T(8,128)(2,1)S(1)}, u32[]{:S(2)}, u32[]{:S(2)}) collective-permute-start(bf16[3,80,128]{2,1,0:T(8,128)(2,1)} %copy-done.10), channel_id=1, source_target_pairs={{6,20},{14,16},{22,22},{8,26},{16,28},{24,24},{7,21},{15,17},{23,2... | collective-permute-start | bytes 184328 | tf_op jit(solution)/shard_map/ppermute | solution.py:369
  48.6 14.2 %collective-permute-start.7 = (bf16[12,80,128]{2,1,0:T(8,128)(2,1)S(1)}, bf16[12,80,128]{2,1,0:T(8,128)(2,1)S(1)}, u32[]{:S(2)}, u32[]{:S(2)}) collective-permute-start(bf16[12,80,128]{2,1,0:T(8,128)(2,1)S(1)} %copy-done.9), channel_id=1, source_target_pairs={{0,18},{2,26},{4,0},{6,8},{8,20},{10,28},{12,6},{14,14},{16,16},{1... | collective-permute-start | bytes 737288 | tf_op jit(solution)/shard_map/ppermute | solution.py:369
  50.5 13.4 %collective-permute-start.8 = (bf16[12,80,128]{2,1,0:T(8,128)(2,1)S(1)}, bf16[12,80,128]{2,1,0:T(8,128)(2,1)S(1)}, u32[]{:S(2)}, u32[]{:S(2)}) collective-permute-start(bf16[12,80,128]{2,1,0:T(8,128)(2,1)S(1)} %get-tuple-element.36), channel_id=1, source_target_pairs={{0,26},{2,0},{4,8},{6,18},{8,28},{10,6},{12,14},{14,20},{16,24},{1... | collective-permute-start | bytes 737288 | tf_op jit(solution)/shard_map/ppermute | solution.py:369
  52.1 0.7 collective-permute-start.12
  52.8 28.2 %collective-permute-start.3 = (bf16[2,3,56,256]{3,2,1,0:T(8,128)(2,1)S(1)}, bf16[2,3,56,256]{3,2,1,0:T(8,128)(2,1)S(1)}, u32[]{:S(2)}, u32[]{:S(2)}) collective-permute-start(bf16[2,3,56,256]{3,2,1,0:T(8,128)(2,1)S(1)} %get-tuple-element.50), channel_id=1, source_target_pairs={{0,8},{6,14},{2,10},{4,12},{8,18},{14,20},{10,16},{12,22},{18,26},... | collective-permute-start | bytes 516104 | tf_op jit(solution)/shard_map/ppermute | solution.py:369
  61.0 20.0 %collective-permute-start.4 = (bf16[2,2,56,256]{3,2,1,0:T(8,128)(2,1)S(1)}, bf16[2,2,56,256]{3,2,1,0:T(8,128)(2,1)S(1)}, u32[]{:S(2)}, u32[]{:S(2)}) collective-permute-start(bf16[2,2,56,256]{3,2,1,0:T(8,128)(2,1)S(1)} %get-tuple-element.52), channel_id=1, source_target_pairs={{8,0},{14,6},{10,2},{12,4},{18,8},{20,14},{16,10},{22,12},{26,18},... | collective-permute-start | bytes 344072 | tf_op jit(solution)/shard_map/ppermute | solution.py:369
  68.8 27.4 %collective-permute-start.17 = (bf16[2,3,56,256]{3,2,1,0:T(8,128)(2,1)S(1)}, bf16[2,3,56,256]{3,2,1,0:T(8,128)(2,1)S(1)}, u32[]{:S(2)}, u32[]{:S(2)}) collective-permute-start(bf16[2,3,56,256]{3,2,1,0:T(8,128)(2,1)S(1)} %get-tuple-element.49), channel_id=1, source_target_pairs={{0,8},{6,14},{2,10},{4,12},{8,18},{14,20},{10,16},{12,22},{18,26},... | collective-permute-start | bytes 516104 | tf_op jit(solution)/shard_map/ppermute | solution.py:369
  79.7 16.4 %collective-permute-start.18 = (bf16[2,2,56,256]{3,2,1,0:T(8,128)(2,1)S(1)}, bf16[2,2,56,256]{3,2,1,0:T(8,128)(2,1)S(1)}, u32[]{:S(2)}, u32[]{:S(2)}) collective-permute-start(bf16[2,2,56,256]{3,2,1,0:T(8,128)(2,1)S(1)} %get-tuple-element.51), channel_id=1, source_target_pairs={{8,0},{14,6},{10,2},{12,4},{18,8},{20,14},{16,10},{22,12},{26,18},... | collective-permute-start | bytes 344072 | tf_op jit(solution)/shard_map/ppermute | solution.py:369
  87.0 47.7 %collective-permute-start.15 = (bf16[1,13,2,24,128]{4,3,2,1,0:T(8,128)(2,1)S(1)}, bf16[1,13,2,24,128]{4,3,2,1,0:T(8,128)(2,1)S(1)}, u32[]{:S(2)}, u32[]{:S(2)}) collective-permute-start(bf16[1,13,2,24,128]{4,3,2,1,0:T(8,128)(2,1)S(1)} %get-tuple-element.45), channel_id=1, source_target_pairs={{0,0},{2,8},{4,12},{6,4},{8,2},{10,10},{12,14},{14,6},{16,24},{18,... | collective-permute-start | bytes 479240 | tf_op jit(solution)/shard_map/ppermute | solution.py:369
  94.2 40.4 %collective-permute-start.16 = (bf16[1,13,2,24,128]{4,3,2,1,0:T(8,128)(2,1)S(1)}, bf16[1,13,2,24,128]{4,3,2,1,0:T(8,128)(2,1)S(1)}, u32[]{:S(2)}, u32[]{:S(2)}) collective-permute-start(bf16[1,13,2,24,128]{4,3,2,1,0:T(8,128)(2,1)S(1)} %get-tuple-element.46), channel_id=1, source_target_pairs={{0,2},{2,10},{4,14},{6,6},{8,0},{10,8},{12,12},{14,4},{16,26},{18,... | collective-permute-start | bytes 479240 | tf_op jit(solution)/shard_map/ppermute | solution.py:369
  107.5 15.9 %collective-permute-start.19 = (bf16[2,13,2,24,128]{4,3,2,1,0:T(8,128)(2,1)S(1)}, bf16[2,13,2,24,128]{4,3,2,1,0:T(8,128)(2,1)S(1)}, u32[]{:S(2)}, u32[]{:S(2)}) collective-permute-start(bf16[2,13,2,24,128]{4,3,2,1,0:T(8,128)(2,1)S(1)} %get-tuple-element.47), channel_id=1, source_target_pairs={{0,0},{2,8},{4,12},{6,4},{8,2},{10,10},{12,14},{14,6},{16,24},{18,... | collective-permute-start | bytes 958472 | tf_op jit(solution)/shard_map/ppermute | solution.py:369
  109.4 22.9 %copy-start = (bf16[3,3,128,256]{3,2,1,0:T(8,128)(2,1)S(1)}, bf16[3,3,128,256]{3,2,1,0:T(8,128)(2,1)}, u32[]{:S(2)}) copy-start(bf16[3,3,128,256]{3,2,1,0:T(8,128)(2,1)} %param.16) | copy-start | bytes 1769476
  109.4 22.9 %copy-start.5 = (bf16[256,128]{1,0:T(8,128)(2,1)S(1)}, bf16[256,128]{1,0:T(8,128)(2,1)}, u32[]{:S(2)}) copy-start(bf16[256,128]{1,0:T(8,128)(2,1)} %refs_5_.5) | copy-start | bytes 196612
  109.4 22.9 %copy-start.6 = (f32[256]{0:T(256)S(1)}, f32[256]{0:T(256)}, u32[]{:S(2)}) copy-start(f32[256]{0:T(256)} %param.17) | copy-start | bytes 3076
  109.4 22.9 %collective-permute-start.20 = (bf16[2,13,2,24,128]{4,3,2,1,0:T(8,128)(2,1)S(1)}, bf16[2,13,2,24,128]{4,3,2,1,0:T(8,128)(2,1)S(1)}, u32[]{:S(2)}, u32[]{:S(2)}) collective-permute-start(bf16[2,13,2,24,128]{4,3,2,1,0:T(8,128)(2,1)S(1)} %get-tuple-element.48), channel_id=1, source_target_pairs={{0,2},{2,10},{4,14},{6,6},{8,0},{10,8},{12,12},{14,4},{16,26},{18,... | collective-permute-start | bytes 958472 | tf_op jit(solution)/shard_map/ppermute | solution.py:369
  121.4 14.8 %collective-permute-start.13 = (bf16[1,13,2,24,128]{4,3,2,1,0:T(8,128)(2,1)S(1)}, bf16[1,13,2,24,128]{4,3,2,1,0:T(8,128)(2,1)S(1)}, u32[]{:S(2)}, u32[]{:S(2)}) collective-permute-start(bf16[1,13,2,24,128]{4,3,2,1,0:T(8,128)(2,1)S(1)} %get-tuple-element.43), channel_id=1, source_target_pairs={{0,0},{2,8},{4,12},{6,4},{8,2},{10,10},{12,14},{14,6},{16,24},{18,... | collective-permute-start | bytes 479240 | tf_op jit(solution)/shard_map/ppermute | solution.py:369
  123.3 12.9 %collective-permute-start.14 = (bf16[1,13,2,24,128]{4,3,2,1,0:T(8,128)(2,1)S(1)}, bf16[1,13,2,24,128]{4,3,2,1,0:T(8,128)(2,1)S(1)}, u32[]{:S(2)}, u32[]{:S(2)}) collective-permute-start(bf16[1,13,2,24,128]{4,3,2,1,0:T(8,128)(2,1)S(1)} %get-tuple-element.44), channel_id=1, source_target_pairs={{0,2},{2,10},{4,14},{6,6},{8,0},{10,8},{12,12},{14,4},{16,26},{18,... | collective-permute-start | bytes 479240 | tf_op jit(solution)/shard_map/ppermute | solution.py:369
  (12 other events, 111.5 us)

commit v8 on v7

--- a/solution.py
+++ b/solution.py
@@ -9,7 +9,7 @@
 
 
 AXES = ("rows", "cols")
-CHUNKS = 1
+CHUNKS = 2
 HALVES = 2
 SIDE = 4
 UP, DOWN = 3, 2
@@ -465,10 +465,7 @@
                 for d in range(1, members)
             ]
             last, head = pick(windows, (member + 1) % members, member, 1)
-            batch = step // 2 if step % 2 == 0 else step
-            rims = []
-            for b0 in range(0, step, batch):
-                rims.append((across(last[b0 : b0 + batch], 1, 0), across(head[b0 : b0 + batch], -1, 0)))
+            above, below = across(last, 1, 0), across(head, -1, 0)
             shifts = []
             for h in range(HALVES):
                 shift = []
@@ -478,12 +475,10 @@
                     shift.append((s, r * n_cols + HALVES * tile_of[r % 2][m] + (k + h) % HALVES))
                 shifts.append(shift)
             vmem = pl.BlockSpec(memory_space=pltpu.VMEM)
-            batches = [(0, batch)] + [(f, 1) for f in range(batch, step)]
-            for b0, many in batches:
+            for b0, many in [(0, step)] if f0 == 0 else [(f, 1) for f in range(step)]:
                 blocks = jax.ShapeDtypeStruct((many, pairs2, 2, w, block), BF)
-                above, below = rims[b0 // batch]
                 tiles = pl.pallas_call(
-                    functools.partial(conv_kernel, parts=members, sh=sh, tr=tr, pitch=pitch, rows=rows, cols=cols, at=b0, cam_at=f0 + b0, rim_at=b0 % batch, many=many),
+                    functools.partial(conv_kernel, parts=members, sh=sh, tr=tr, pitch=pitch, rows=rows, cols=cols, at=b0, cam_at=f0 + b0, rim_at=b0, many=many),
                     in_specs=[pl.BlockSpec(memory_space=pltpu.SMEM)] + [vmem] * (members + 7),
                     out_specs=[vmem] * HALVES,
                     scratch_shapes=conv_scratch(tr, pitch, lidar_ch, joined, block, pairs2),

time: 138 us -> 134 us (0.971)
  the two profiles are of different devices: /device:TPU:8 before, /device:TPU:2 now
where the time goes in v8:
time: 134 us; the launch traced here: 133 us
  starting transfers between devices  64 us (48%)
  Pallas kernels  42.9 us (32%)
  waiting for transfers between devices  19.6 us (15%)
  local copies, waits for them, and re-layouts  5.47 us (4%)
    ppermute x24, starting transfers between devices, send(): return lax.ppermute(x, AXES, pairs)  64 us
    pallas_call x3, Pallas kernels, local(): pl.pallas_call(functools.partial(conv_kernel, parts=members, sh=sh, tr=tr...  23.8 us
    ppermute x24, waiting for transfers between devices, send(): return lax.ppermute(x, AXES, pairs)  19.6 us
    pallas_call x1, Pallas kernels, local(): pl.pallas_call(lambda *refs: camera_unpack_kernel(*refs, groups=groups, s...  5.89 us
    unnamed x40, local copies, waits for them, and re-layouts  5.47 us
    pallas_call x3, Pallas kernels, local(): pl.pallas_call(lambda *refs: encode_kernel(*refs, parts=HALVES, half_rows...  5.38 us
    pallas_call x2, Pallas kernels, local(): pl.pallas_call(functools.partial(window_kernel, tw=tw), grid_spec=pltpu.P...  2.79 us
  transfers between devices with their start and end apart: 24, of which 7 were waited for; matrix products, arithmetic and copies ran while one was open for 0% of the time, Pallas kernels for 30%

profile of v8, /device:TPU:2, one launch (start us, length us, event | category | flops | bytes accessed | tf_op | source)
XLA Modules:
  0.0 132.7 jit_solution(4928996183619562674)
XLA Ops:
  1.2 2.2 %camera_pack.1 = (bf16[12,80,128]{2,1,0:T(8,128)(2,1)S(1)}, bf16[12,80,128]{2,1,0:T(8,128)(2,1)S(1)}, bf16[12,80,128]{2,1,0:T(8,128)(2,1)}, bf16[12,80,128]{2,1,...) custom-call(s32[1]{0:T(128)} %bitcast.9.refs_0_, ...), custom_call_target="tpu_custom_call" | custom-call | tf_op jit(solution)/shard_map/camera_pack/pallas_call | solution.py:405
  3.4 6.4 %collective-permute-start.9 = (bf16[3,80,128]{2,1,0:T(8,128)(2,1)S(1)}, bf16[3,80,128]{2,1,0:T(8,128)(2,1)S(1)}, u32[]{:S(2)}, u32[]{:S(2)}) collective-permute-start(bf16[3,80,128]{2,1,0:T(8,128)(2,1)S(1)} %get-tuple-element.45), channel_id=1, source_target_pairs={{6,6},{14,2},{22,4},{8,8},{16,14},{24,10},{7,7},{15,3},{23,5},{9,9... | collective-permute-start | bytes 184328 | tf_op jit(solution)/shard_map/ppermute | solution.py:369
  9.8 1.9 %collective-permute-start.5 = (bf16[12,80,128]{2,1,0:T(8,128)(2,1)S(1)}, bf16[12,80,128]{2,1,0:T(8,128)(2,1)S(1)}, u32[]{:S(2)}, u32[]{:S(2)}) collective-permute-start(bf16[12,80,128]{2,1,0:T(8,128)(2,1)S(1)} %get-tuple-element.34), channel_id=1, source_target_pairs={{0,0},{2,8},{4,18},{6,26},{8,6},{10,14},{12,20},{14,28},{16,2},{18... | collective-permute-start | bytes 737288 | tf_op jit(solution)/shard_map/ppermute | solution.py:369
  12.5 3.2 %collective-permute-start.10 = (bf16[3,80,128]{2,1,0:T(8,128)(2,1)S(1)}, bf16[3,80,128]{2,1,0:T(8,128)(2,1)S(1)}, u32[]{:S(2)}, u32[]{:S(2)}) collective-permute-start(bf16[3,80,128]{2,1,0:T(8,128)(2,1)S(1)} %get-tuple-element.46), channel_id=1, source_target_pairs={{6,14},{14,10},{22,12},{8,18},{16,20},{24,16},{7,15},{15,11},{23,1... | collective-permute-start | bytes 184328 | tf_op jit(solution)/shard_map/ppermute | solution.py:369
  15.7 1.9 %collective-permute-start.11 = (bf16[3,80,128]{2,1,0:T(8,128)(2,1)S(1)}, bf16[3,80,128]{2,1,0:T(8,128)(2,1)S(1)}, u32[]{:S(2)}, u32[]{:S(2)}) collective-permute-start(bf16[3,80,128]{2,1,0:T(8,128)(2,1)S(1)} %get-tuple-element.47), channel_id=1, source_target_pairs={{6,20},{14,16},{22,22},{8,26},{16,28},{24,24},{7,21},{15,17},{23,2... | collective-permute-start | bytes 184328 | tf_op jit(solution)/shard_map/ppermute | solution.py:369
  17.8 3.6 %collective-permute-start.12 = (bf16[3,80,128]{2,1,0:T(8,128)(2,1)S(1)}, bf16[3,80,128]{2,1,0:T(8,128)(2,1)S(1)}, u32[]{:S(2)}, u32[]{:S(2)}) collective-permute-start(bf16[3,80,128]{2,1,0:T(8,128)(2,1)S(1)} %get-tuple-element.48), channel_id=1, source_target_pairs={{6,28},{14,24},{22,30},{8,0},{16,6},{24,2},{7,29},{15,25},{23,31},... | collective-permute-start | bytes 184328 | tf_op jit(solution)/shard_map/ppermute | solution.py:369
  29.0 3.5 %collective-permute-start.7 = (bf16[12,80,128]{2,1,0:T(8,128)(2,1)}, bf16[12,80,128]{2,1,0:T(8,128)(2,1)}, u32[]{:S(2)}, u32[]{:S(2)}) collective-permute-start(bf16[12,80,128]{2,1,0:T(8,128)(2,1)} %get-tuple-element.43), channel_id=1, source_target_pairs={{0,18},{2,26},{4,0},{6,8},{8,20},{10,28},{12,6},{14,14},{16,16},{1... | collective-permute-start | bytes 737288 | tf_op jit(solution)/shard_map/ppermute | solution.py:369
  38.5 6.2 %collective-permute-done.2.refs_3_.refs_7_ = bf16[2,6,56,256]{3,2,1,0:T(8,128)(2,1)S(1)} collective-permute-done((bf16[2,6,56,256]{3,2,1,0:T(8,128)(2,1)S(1)}, bf16[2,6,56,256]{3,2,1,0:T(8,128)(2,1)S(1)}, u32[]{:S(2)}, u32[]{:S(2)}) %collective-permute-start.2) | collective-permute-done | bytes 344096 | tf_op jit(solution)/shard_map/ppermute | solution.py:369
  44.7 3.4 %collective-permute-start.19 = (bf16[2,6,56,256]{3,2,1,0:T(8,128)(2,1)}, bf16[2,6,56,256]{3,2,1,0:T(8,128)(2,1)}, u32[]{:S(2)}, u32[]{:S(2)}) collective-permute-start(bf16[2,6,56,256]{3,2,1,0:T(8,128)(2,1)} %get-tuple-element.58), channel_id=1, source_target_pairs={{0,6},{2,0},{4,2},{6,4},{8,14},{10,8},{12,10},{14,12},{16,22},{18,... | collective-permute-start | bytes 1032200 | tf_op jit(solution)/shard_map/ppermute | solution.py:369
  48.9 2.8 %collective-permute-start.3 = (bf16[2,3,56,256]{3,2,1,0:T(8,128)(2,1)S(1)}, bf16[2,3,56,256]{3,2,1,0:T(8,128)(2,1)S(1)}, u32[]{:S(2)}, u32[]{:S(2)}) collective-permute-start(bf16[2,3,56,256]{3,2,1,0:T(8,128)(2,1)S(1)} %get-tuple-element.40), channel_id=1, source_target_pairs={{0,8},{6,14},{2,10},{4,12},{8,18},{14,20},{10,16},{12,22},{18,26},... | collective-permute-start | bytes 516104 | tf_op jit(solution)/shard_map/ppermute | solution.py:369
  51.7 5.7 %collective-permute-start.4 = (bf16[2,2,56,256]{3,2,1,0:T(8,128)(2,1)S(1)}, bf16[2,2,56,256]{3,2,1,0:T(8,128)(2,1)S(1)}, u32[]{:S(2)}, u32[]{:S(2)}) collective-permute-start(bf16[2,2,56,256]{3,2,1,0:T(8,128)(2,1)S(1)} %get-tuple-element.41), channel_id=1, source_target_pairs={{8,0},{14,6},{10,2},{12,4},{18,8},{20,14},{16,10},{22,12},{26,18},... | collective-permute-start | bytes 344072 | tf_op jit(solution)/shard_map/ppermute | solution.py:369
  58.0 5.9 %camera_unpack.1 = bf16[128,64,256]{2,1,0:T(8,128)(2,1)S(1)} custom-call(s32[1]{0:T(128)} %bitcast.1.refs_0_, bf16[12,80,128]{2,1,0:T(8,128)(2,1)S(1)} %collective-permute-done.5.refs_1_, bf16[12,80,128]{2,1,0:T(8,128)(2,1)S(1)} %copy-done.7, bf16[12,80,128]{2,1,0:T(8,128)(2,1)} %collective-permute-done.7.refs_3_, ...), custom_call_target="tpu_custom_call" | custom-call | tf_op jit(solution)/shard_map/camera_unpack/pallas_call | solution.py:422
  67.5 1.9 %collective-permute-start.20 = (bf16[2,3,56,256]{3,2,1,0:T(8,128)(2,1)S(1)}, bf16[2,3,56,256]{3,2,1,0:T(8,128)(2,1)S(1)}, u32[]{:S(2)}, u32[]{:S(2)}) collective-permute-start(bf16[2,3,56,256]{3,2,1,0:T(8,128)(2,1)S(1)} %get-tuple-element.59), channel_id=1, source_target_pairs={{0,8},{6,14},{2,10},{4,12},{8,18},{14,20},{10,16},{12,22},{18,26},... | collective-permute-start | bytes 516104 | tf_op jit(solution)/shard_map/ppermute | solution.py:369
  69.4 7.7 %collective-permute-start.21 = (bf16[2,2,56,256]{3,2,1,0:T(8,128)(2,1)S(1)}, bf16[2,2,56,256]{3,2,1,0:T(8,128)(2,1)S(1)}, u32[]{:S(2)}, u32[]{:S(2)}) collective-permute-start(bf16[2,2,56,256]{3,2,1,0:T(8,128)(2,1)S(1)} %get-tuple-element.60), channel_id=1, source_target_pairs={{8,0},{14,6},{10,2},{12,4},{18,8},{20,14},{16,10},{22,12},{26,18},... | collective-permute-start | bytes 344072 | tf_op jit(solution)/shard_map/ppermute | solution.py:369
  77.2 5.9 %shard_map.103 = (bf16[1,13,2,24,128]{4,3,2,1,0:T(8,128)(2,1)S(1)}, bf16[1,13,2,24,128]{4,3,2,1,0:T(8,128)(2,1)S(1)}) custom-call(s32[4]{0:T(128)S(1)} %pad_add_fusion.pos, bf16[2,6,56,256]{3,2,1,0:T(8,128)(2,1)S(1)} %get-tuple-element.36.refs_0_.refs_4_, bf16[2,6,56,256]{3,2,1,0:T(8,128)(2,1)S(1)} %collective-permute-done.refs_1_.refs_5_, ...), custom_call_target="tpu_custom_call" | custom-call | flops 4127195136 | bytes 2000000 | tf_op jit(solution)/shard_map/pallas_call | solution.py:480
  83.1 1.9 %collective-permute-start.15 = (bf16[1,13,2,24,128]{4,3,2,1,0:T(8,128)(2,1)S(1)}, bf16[1,13,2,24,128]{4,3,2,1,0:T(8,128)(2,1)S(1)}, u32[]{:S(2)}, u32[]{:S(2)}) collective-permute-start(bf16[1,13,2,24,128]{4,3,2,1,0:T(8,128)(2,1)S(1)} %get-tuple-element.53), channel_id=1, source_target_pairs={{0,0},{2,8},{4,12},{6,4},{8,2},{10,10},{12,14},{14,6},{16,24},{18,... | collective-permute-start | bytes 479240 | tf_op jit(solution)/shard_map/ppermute | solution.py:369
  85.0 6.4 %collective-permute-start.16 = (bf16[1,13,2,24,128]{4,3,2,1,0:T(8,128)(2,1)S(1)}, bf16[1,13,2,24,128]{4,3,2,1,0:T(8,128)(2,1)S(1)}, u32[]{:S(2)}, u32[]{:S(2)}) collective-permute-start(bf16[1,13,2,24,128]{4,3,2,1,0:T(8,128)(2,1)S(1)} %get-tuple-element.54), channel_id=1, source_target_pairs={{0,2},{2,10},{4,14},{6,6},{8,0},{10,8},{12,12},{14,4},{16,26},{18,... | collective-permute-start | bytes 479240 | tf_op jit(solution)/shard_map/ppermute | solution.py:369
  91.5 11.9 %shard_map.106 = (bf16[2,13,2,24,128]{4,3,2,1,0:T(8,128)(2,1)S(1)}, bf16[2,13,2,24,128]{4,3,2,1,0:T(8,128)(2,1)S(1)}) custom-call(s32[4]{0:T(128)S(1)} %pad_add_fusion.pos, bf16[2,6,56,256]{3,2,1,0:T(8,128)(2,1)S(1)} %get-tuple-element.55.refs_0_.refs_4_, bf16[2,6,56,256]{3,2,1,0:T(8,128)(2,1)} %collective-permute-done.17.refs_1_.refs_5_, ...), custom_call_target="tpu_custom_call" | custom-call | flops 8254390272 | bytes 2000000 | tf_op jit(solution)/shard_map/pallas_call | solution.py:480
  103.4 1.9 %collective-permute-start.22 = (bf16[2,13,2,24,128]{4,3,2,1,0:T(8,128)(2,1)S(1)}, bf16[2,13,2,24,128]{4,3,2,1,0:T(8,128)(2,1)S(1)}, u32[]{:S(2)}, u32[]{:S(2)}) collective-permute-start(bf16[2,13,2,24,128]{4,3,2,1,0:T(8,128)(2,1)S(1)} %get-tuple-element.61), channel_id=1, source_target_pairs={{0,0},{2,8},{4,12},{6,4},{8,2},{10,10},{12,14},{14,6},{16,24},{18,... | collective-permute-start | bytes 958472 | tf_op jit(solution)/shard_map/ppermute | solution.py:369
  105.4 2.2 %collective-permute-start.23 = (bf16[2,13,2,24,128]{4,3,2,1,0:T(8,128)(2,1)S(1)}, bf16[2,13,2,24,128]{4,3,2,1,0:T(8,128)(2,1)S(1)}, u32[]{:S(2)}, u32[]{:S(2)}) collective-permute-start(bf16[2,13,2,24,128]{4,3,2,1,0:T(8,128)(2,1)S(1)} %get-tuple-element.62), channel_id=1, source_target_pairs={{0,2},{2,10},{4,14},{6,6},{8,0},{10,8},{12,12},{14,4},{16,26},{18,... | collective-permute-start | bytes 958472 | tf_op jit(solution)/shard_map/ppermute | solution.py:369
  107.7 5.9 %shard_map.102 = (bf16[1,13,2,24,128]{4,3,2,1,0:T(8,128)(2,1)S(1)}, bf16[1,13,2,24,128]{4,3,2,1,0:T(8,128)(2,1)S(1)}) custom-call(s32[4]{0:T(128)S(1)} %pad_add_fusion.pos, bf16[2,6,56,256]{3,2,1,0:T(8,128)(2,1)S(1)} %get-tuple-element.36.refs_0_.refs_4_, bf16[2,6,56,256]{3,2,1,0:T(8,128)(2,1)S(1)} %collective-permute-done.refs_1_.refs_5_, ...), custom_call_target="tpu_custom_call" | custom-call | flops 4127195136 | bytes 2000000 | tf_op jit(solution)/shard_map/pallas_call | solution.py:480
  115.5 6.7 %collective-permute-done.22.refs_1_ = bf16[2,13,2,24,128]{4,3,2,1,0:T(8,128)(2,1)S(1)} collective-permute-done((bf16[2,13,2,24,128]{4,3,2,1,0:T(8,128)(2,1)S(1)}, bf16[2,13,2,24,128]{4,3,2,1,0:T(8,128)(2,1)S(1)}, u32[]{:S(2)}, u32[]{:S(2)}) %collective-permute-start.22) | collective-permute-done | bytes 319520 | tf_op jit(solution)/shard_map/ppermute | solution.py:369
  124.2 2.3 %shard_map.107.refs_7_ = bf16[4,24,2,24,256]{4,3,2,1,0:T(8,128)(2,1)} custom-call(s32[1]{0:T(128)} %bitcast.refs_0_, bf16[2,13,2,24,128]{4,3,2,1,0:T(8,128)(2,1)S(1)} %collective-permute-done.22.refs_1_, bf16[2,13,2,24,128]{4,3,2,1,0:T(8,128)(2,1)S(1)} %collective-permute-done.23.refs_2_, bf16[1152,256]{1,0:T(8,128)(2,1)S(1)} %bitcast.21, ...), custom_call_target="tpu_custom_call" | custom-call | flops 452984832 | bytes 2000000 | tf_op jit(solution)/shard_map/pallas_call | solution.py:493
  128.1 3.1 %collective-permute-done.14.refs_2_ = bf16[1,13,2,24,128]{4,3,2,1,0:T(8,128)(2,1)S(1)} collective-permute-done((bf16[1,13,2,24,128]{4,3,2,1,0:T(8,128)(2,1)S(1)}, bf16[1,13,2,24,128]{4,3,2,1,0:T(8,128)(2,1)S(1)}, u32[]{:S(2)}, u32[]{:S(2)}) %collective-permute-start.14) | collective-permute-done | bytes 159776 | tf_op jit(solution)/shard_map/ppermute | solution.py:369
  (81 shorter events, 27.3 us)
Async XLA Ops:
  3.4 14.4 %collective-permute-start.9 = (bf16[3,80,128]{2,1,0:T(8,128)(2,1)S(1)}, bf16[3,80,128]{2,1,0:T(8,128)(2,1)S(1)}, u32[]{:S(2)}, u32[]{:S(2)}) collective-permute-start(bf16[3,80,128]{2,1,0:T(8,128)(2,1)S(1)} %get-tuple-element.45), channel_id=1, source_target_pairs={{6,6},{14,2},{22,4},{8,8},{16,14},{24,10},{7,7},{15,3},{23,5},{9,9... | collective-permute-start | bytes 184328 | tf_op jit(solution)/shard_map/ppermute | solution.py:369
  9.8 19.2 %collective-permute-start.5 = (bf16[12,80,128]{2,1,0:T(8,128)(2,1)S(1)}, bf16[12,80,128]{2,1,0:T(8,128)(2,1)S(1)}, u32[]{:S(2)}, u32[]{:S(2)}) collective-permute-start(bf16[12,80,128]{2,1,0:T(8,128)(2,1)S(1)} %get-tuple-element.34), channel_id=1, source_target_pairs={{0,0},{2,8},{4,18},{6,26},{8,6},{10,14},{12,20},{14,28},{16,2},{18... | collective-permute-start | bytes 737288 | tf_op jit(solution)/shard_map/ppermute | solution.py:369
  11.7 20.8 %collective-permute-start.6 = (bf16[12,80,128]{2,1,0:T(8,128)(2,1)S(1)}, bf16[12,80,128]{2,1,0:T(8,128)(2,1)S(1)}, u32[]{:S(2)}, u32[]{:S(2)}) collective-permute-start(bf16[12,80,128]{2,1,0:T(8,128)(2,1)S(1)} %get-tuple-element.42), channel_id=1, source_target_pairs={{0,8},{2,18},{4,26},{6,0},{8,14},{10,20},{12,28},{14,6},{16,10},{1... | collective-permute-start | bytes 737288 | tf_op jit(solution)/shard_map/ppermute | solution.py:369
  12.5 11.7 %collective-permute-start.10 = (bf16[3,80,128]{2,1,0:T(8,128)(2,1)S(1)}, bf16[3,80,128]{2,1,0:T(8,128)(2,1)S(1)}, u32[]{:S(2)}, u32[]{:S(2)}) collective-permute-start(bf16[3,80,128]{2,1,0:T(8,128)(2,1)S(1)} %get-tuple-element.46), channel_id=1, source_target_pairs={{6,14},{14,10},{22,12},{8,18},{16,20},{24,16},{7,15},{15,11},{23,1... | collective-permute-start | bytes 184328 | tf_op jit(solution)/shard_map/ppermute | solution.py:369
  15.7 10.0 %collective-permute-start.11 = (bf16[3,80,128]{2,1,0:T(8,128)(2,1)S(1)}, bf16[3,80,128]{2,1,0:T(8,128)(2,1)S(1)}, u32[]{:S(2)}, u32[]{:S(2)}) collective-permute-start(bf16[3,80,128]{2,1,0:T(8,128)(2,1)S(1)} %get-tuple-element.47), channel_id=1, source_target_pairs={{6,20},{14,16},{22,22},{8,26},{16,28},{24,24},{7,21},{15,17},{23,2... | collective-permute-start | bytes 184328 | tf_op jit(solution)/shard_map/ppermute | solution.py:369
  17.8 9.2 %collective-permute-start.12 = (bf16[3,80,128]{2,1,0:T(8,128)(2,1)S(1)}, bf16[3,80,128]{2,1,0:T(8,128)(2,1)S(1)}, u32[]{:S(2)}, u32[]{:S(2)}) collective-permute-start(bf16[3,80,128]{2,1,0:T(8,128)(2,1)S(1)} %get-tuple-element.48), channel_id=1, source_target_pairs={{6,28},{14,24},{22,30},{8,0},{16,6},{24,2},{7,29},{15,25},{23,31},... | collective-permute-start | bytes 184328 | tf_op jit(solution)/shard_map/ppermute | solution.py:369
  24.8 11.9 %collective-permute-start = (bf16[2,6,56,256]{3,2,1,0:T(8,128)(2,1)S(1)}, bf16[2,6,56,256]{3,2,1,0:T(8,128)(2,1)S(1)}, u32[]{:S(2)}, u32[]{:S(2)}) collective-permute-start(bf16[2,6,56,256]{3,2,1,0:T(8,128)(2,1)S(1)} %get-tuple-element.37), channel_id=1, source_target_pairs={{0,2},{2,4},{4,6},{6,0},{8,10},{10,12},{12,14},{14,8},{16,18},{18,... | collective-permute-start | bytes 1032200 | tf_op jit(solution)/shard_map/ppermute | solution.py:369
  26.3 10.9 %collective-permute-start.1 = (bf16[2,6,56,256]{3,2,1,0:T(8,128)(2,1)S(1)}, bf16[2,6,56,256]{3,2,1,0:T(8,128)(2,1)S(1)}, u32[]{:S(2)}, u32[]{:S(2)}) collective-permute-start(bf16[2,6,56,256]{3,2,1,0:T(8,128)(2,1)S(1)} %get-tuple-element.38), channel_id=1, source_target_pairs={{0,4},{2,6},{4,0},{6,2},{8,12},{10,14},{12,8},{14,10},{16,20},{18,... | collective-permute-start | bytes 1032200 | tf_op jit(solution)/shard_map/ppermute | solution.py:369
  27.6 17.0 %collective-permute-start.2 = (bf16[2,6,56,256]{3,2,1,0:T(8,128)(2,1)S(1)}, bf16[2,6,56,256]{3,2,1,0:T(8,128)(2,1)S(1)}, u32[]{:S(2)}, u32[]{:S(2)}) collective-permute-start(bf16[2,6,56,256]{3,2,1,0:T(8,128)(2,1)S(1)} %get-tuple-element.39), channel_id=1, source_target_pairs={{0,6},{2,0},{4,2},{6,4},{8,14},{10,8},{12,10},{14,12},{16,22},{18,... | collective-permute-start | bytes 1032200 | tf_op jit(solution)/shard_map/ppermute | solution.py:369
  29.0 19.9 %collective-permute-start.7 = (bf16[12,80,128]{2,1,0:T(8,128)(2,1)}, bf16[12,80,128]{2,1,0:T(8,128)(2,1)}, u32[]{:S(2)}, u32[]{:S(2)}) collective-permute-start(bf16[12,80,128]{2,1,0:T(8,128)(2,1)} %get-tuple-element.43), channel_id=1, source_target_pairs={{0,18},{2,26},{4,0},{6,8},{8,20},{10,28},{12,6},{14,14},{16,16},{1... | collective-permute-start | bytes 737288 | tf_op jit(solution)/shard_map/ppermute | solution.py:369
  33.2 18.5 %collective-permute-start.8 = (bf16[12,80,128]{2,1,0:T(8,128)(2,1)}, bf16[12,80,128]{2,1,0:T(8,128)(2,1)}, u32[]{:S(2)}, u32[]{:S(2)}) collective-permute-start(bf16[12,80,128]{2,1,0:T(8,128)(2,1)} %get-tuple-element.44), channel_id=1, source_target_pairs={{0,26},{2,0},{4,8},{6,18},{8,28},{10,6},{12,14},{14,20},{16,24},{1... | collective-permute-start | bytes 737288 | tf_op jit(solution)/shard_map/ppermute | solution.py:369
  36.7 27.2 %collective-permute-start.17 = (bf16[2,6,56,256]{3,2,1,0:T(8,128)(2,1)}, bf16[2,6,56,256]{3,2,1,0:T(8,128)(2,1)}, u32[]{:S(2)}, u32[]{:S(2)}) collective-permute-start(bf16[2,6,56,256]{3,2,1,0:T(8,128)(2,1)} %get-tuple-element.56), channel_id=1, source_target_pairs={{0,2},{2,4},{4,6},{6,0},{8,10},{10,12},{12,14},{14,8},{16,18},{18,... | collective-permute-start | bytes 1032200 | tf_op jit(solution)/shard_map/ppermute | solution.py:369
  37.2 26.7 %collective-permute-start.18 = (bf16[2,6,56,256]{3,2,1,0:T(8,128)(2,1)}, bf16[2,6,56,256]{3,2,1,0:T(8,128)(2,1)}, u32[]{:S(2)}, u32[]{:S(2)}) collective-permute-start(bf16[2,6,56,256]{3,2,1,0:T(8,128)(2,1)} %get-tuple-element.57), channel_id=1, source_target_pairs={{0,4},{2,6},{4,0},{6,2},{8,12},{10,14},{12,8},{14,10},{16,20},{18,... | collective-permute-start | bytes 1032200 | tf_op jit(solution)/shard_map/ppermute | solution.py:369
  44.7 20.9 %collective-permute-start.19 = (bf16[2,6,56,256]{3,2,1,0:T(8,128)(2,1)}, bf16[2,6,56,256]{3,2,1,0:T(8,128)(2,1)}, u32[]{:S(2)}, u32[]{:S(2)}) collective-permute-start(bf16[2,6,56,256]{3,2,1,0:T(8,128)(2,1)} %get-tuple-element.58), channel_id=1, source_target_pairs={{0,6},{2,0},{4,2},{6,4},{8,14},{10,8},{12,10},{14,12},{16,22},{18,... | collective-permute-start | bytes 1032200 | tf_op jit(solution)/shard_map/ppermute | solution.py:369
  48.9 28.3 %collective-permute-start.3 = (bf16[2,3,56,256]{3,2,1,0:T(8,128)(2,1)S(1)}, bf16[2,3,56,256]{3,2,1,0:T(8,128)(2,1)S(1)}, u32[]{:S(2)}, u32[]{:S(2)}) collective-permute-start(bf16[2,3,56,256]{3,2,1,0:T(8,128)(2,1)S(1)} %get-tuple-element.40), channel_id=1, source_target_pairs={{0,8},{6,14},{2,10},{4,12},{8,18},{14,20},{10,16},{12,22},{18,26},... | collective-permute-start | bytes 516104 | tf_op jit(solution)/shard_map/ppermute | solution.py:369
  51.7 25.4 %collective-permute-start.4 = (bf16[2,2,56,256]{3,2,1,0:T(8,128)(2,1)S(1)}, bf16[2,2,56,256]{3,2,1,0:T(8,128)(2,1)S(1)}, u32[]{:S(2)}, u32[]{:S(2)}) collective-permute-start(bf16[2,2,56,256]{3,2,1,0:T(8,128)(2,1)S(1)} %get-tuple-element.41), channel_id=1, source_target_pairs={{8,0},{14,6},{10,2},{12,4},{18,8},{20,14},{16,10},{22,12},{26,18},... | collective-permute-start | bytes 344072 | tf_op jit(solution)/shard_map/ppermute | solution.py:369
  67.5 24.0 %collective-permute-start.20 = (bf16[2,3,56,256]{3,2,1,0:T(8,128)(2,1)S(1)}, bf16[2,3,56,256]{3,2,1,0:T(8,128)(2,1)S(1)}, u32[]{:S(2)}, u32[]{:S(2)}) collective-permute-start(bf16[2,3,56,256]{3,2,1,0:T(8,128)(2,1)S(1)} %get-tuple-element.59), channel_id=1, source_target_pairs={{0,8},{6,14},{2,10},{4,12},{8,18},{14,20},{10,16},{12,22},{18,26},... | collective-permute-start | bytes 516104 | tf_op jit(solution)/shard_map/ppermute | solution.py:369
  69.4 22.0 %collective-permute-start.21 = (bf16[2,2,56,256]{3,2,1,0:T(8,128)(2,1)S(1)}, bf16[2,2,56,256]{3,2,1,0:T(8,128)(2,1)S(1)}, u32[]{:S(2)}, u32[]{:S(2)}) collective-permute-start(bf16[2,2,56,256]{3,2,1,0:T(8,128)(2,1)S(1)} %get-tuple-element.60), channel_id=1, source_target_pairs={{8,0},{14,6},{10,2},{12,4},{18,8},{20,14},{16,10},{22,12},{26,18},... | collective-permute-start | bytes 344072 | tf_op jit(solution)/shard_map/ppermute | solution.py:369
  83.1 43.4 %collective-permute-start.15 = (bf16[1,13,2,24,128]{4,3,2,1,0:T(8,128)(2,1)S(1)}, bf16[1,13,2,24,128]{4,3,2,1,0:T(8,128)(2,1)S(1)}, u32[]{:S(2)}, u32[]{:S(2)}) collective-permute-start(bf16[1,13,2,24,128]{4,3,2,1,0:T(8,128)(2,1)S(1)} %get-tuple-element.53), channel_id=1, source_target_pairs={{0,0},{2,8},{4,12},{6,4},{8,2},{10,10},{12,14},{14,6},{16,24},{18,... | collective-permute-start | bytes 479240 | tf_op jit(solution)/shard_map/ppermute | solution.py:369
  85.0 41.5 %collective-permute-start.16 = (bf16[1,13,2,24,128]{4,3,2,1,0:T(8,128)(2,1)S(1)}, bf16[1,13,2,24,128]{4,3,2,1,0:T(8,128)(2,1)S(1)}, u32[]{:S(2)}, u32[]{:S(2)}) collective-permute-start(bf16[1,13,2,24,128]{4,3,2,1,0:T(8,128)(2,1)S(1)} %get-tuple-element.54), channel_id=1, source_target_pairs={{0,2},{2,10},{4,14},{6,6},{8,0},{10,8},{12,12},{14,4},{16,26},{18,... | collective-permute-start | bytes 479240 | tf_op jit(solution)/shard_map/ppermute | solution.py:369
  103.4 18.8 %collective-permute-start.22 = (bf16[2,13,2,24,128]{4,3,2,1,0:T(8,128)(2,1)S(1)}, bf16[2,13,2,24,128]{4,3,2,1,0:T(8,128)(2,1)S(1)}, u32[]{:S(2)}, u32[]{:S(2)}) collective-permute-start(bf16[2,13,2,24,128]{4,3,2,1,0:T(8,128)(2,1)S(1)} %get-tuple-element.61), channel_id=1, source_target_pairs={{0,0},{2,8},{4,12},{6,4},{8,2},{10,10},{12,14},{14,6},{16,24},{18,... | collective-permute-start | bytes 958472 | tf_op jit(solution)/shard_map/ppermute | solution.py:369
  105.4 18.8 %collective-permute-start.23 = (bf16[2,13,2,24,128]{4,3,2,1,0:T(8,128)(2,1)S(1)}, bf16[2,13,2,24,128]{4,3,2,1,0:T(8,128)(2,1)S(1)}, u32[]{:S(2)}, u32[]{:S(2)}) collective-permute-start(bf16[2,13,2,24,128]{4,3,2,1,0:T(8,128)(2,1)S(1)} %get-tuple-element.62), channel_id=1, source_target_pairs={{0,2},{2,10},{4,14},{6,6},{8,0},{10,8},{12,12},{14,4},{16,26},{18,... | collective-permute-start | bytes 958472 | tf_op jit(solution)/shard_map/ppermute | solution.py:369
  113.6 14.5 %collective-permute-start.13 = (bf16[1,13,2,24,128]{4,3,2,1,0:T(8,128)(2,1)S(1)}, bf16[1,13,2,24,128]{4,3,2,1,0:T(8,128)(2,1)S(1)}, u32[]{:S(2)}, u32[]{:S(2)}) collective-permute-start(bf16[1,13,2,24,128]{4,3,2,1,0:T(8,128)(2,1)S(1)} %get-tuple-element.51), channel_id=1, source_target_pairs={{0,0},{2,8},{4,12},{6,4},{8,2},{10,10},{12,14},{14,6},{16,24},{18,... | collective-permute-start | bytes 479240 | tf_op jit(solution)/shard_map/ppermute | solution.py:369
  122.2 9.0 %collective-permute-start.14 = (bf16[1,13,2,24,128]{4,3,2,1,0:T(8,128)(2,1)S(1)}, bf16[1,13,2,24,128]{4,3,2,1,0:T(8,128)(2,1)S(1)}, u32[]{:S(2)}, u32[]{:S(2)}) collective-permute-start(bf16[1,13,2,24,128]{4,3,2,1,0:T(8,128)(2,1)S(1)} %get-tuple-element.52), channel_id=1, source_target_pairs={{0,2},{2,10},{4,14},{6,6},{8,0},{10,8},{12,12},{14,4},{16,26},{18,... | collective-permute-start | bytes 479240 | tf_op jit(solution)/shard_map/ppermute | solution.py:369
  (20 other events, 201.8 us)
